TPU v7x, 32 devices: a whole 2x2x4 slice. The times are simulated.
32 devices in a mesh: gz: 32 (over z, y, x, core).
Axes of the slice: x: 2, y: 2, z: 4, core: 2. Of those that a mesh axis runs over, the one named last changes fastest.
Arguments:
- coefficient: float32 [64, 512, 512], P('gz'), may hold values from 0.2 to 1.3
- initial_field: float32 [64, 512, 512], P('gz'), may hold values from -6 to 6
- observed: float32 [64, 512, 512], P('gz'), may hold values from -6 to 6
- misfit_weight: float32 [64, 512, 512], P('gz'), may hold values from 0.5 to 6, as said below
Outputs:
- coeff_gradient: float32 [64, 512, 512], P('gz')
- adjoint_field: float32 [64, 512, 512], P('gz')
- misfit: float32 [], replicated
Inputs may be any that keep to these rules, and one draw needn't show every extreme that they name: `misfit_weight`: positive cell weights.
All inputs are finite; a program needn't handle non-finite values.
Results may differ from a plain program's by a relative error of at most 0.00002.
Values sent between devices are 32-bit elements; how exact they have to be, the bound alone decides.
No kernel may reach another device: no remote copies, remote signals or barrier semaphores. Data moves between devices by JAX's collectives and lax.ppermute only.
A program may use at most 128 MiB of HBM per device.

v0:
```python
import jax
import jax.numpy as jnp
from jax import lax
from jax.experimental import pallas as pl
from jax.experimental.pallas import tpu as pltpu
from jax.sharding import PartitionSpec as P


ITERS = 4
time_step = 0.125

GROUP = 8
PARTS = 4
HALO = 8
ROUNDS = ((0, 0), (0, 1), (1, 0), (1, 1))


VM = pl.BlockSpec(memory_space=pltpu.VMEM)
SM = pl.BlockSpec(memory_space=pltpu.SMEM)
PARAMS = pltpu.CompilerParams(vmem_limit_bytes=60 * 1024 * 1024)
F32 = jnp.float32


def call(kernel, outs, n_in, scratch=(), out_specs=None):
    return pl.pallas_call(
        kernel,
        out_shape=outs,
        in_specs=[SM] + [VM] * n_in,
        out_specs=out_specs if out_specs is not None else [VM] * len(outs),
        scratch_shapes=scratch,
        compiler_params=PARAMS,
    )


def bits(me):
    return (me >> 2) & 1, (me >> 1) & 1, me & 1


def part(y, x):
    return 2 * y + x


def send_pairs(count, r1, r0):
    pairs = []
    for i in range(count):
        y, x, c = bits(i)
        pairs.append((i, (i & ~7) + 4 * (c ^ r1) + 2 * (x ^ r0) + y))
    return pairs


def row_loop(rows, body, step=16):
    def one(t, carry):
        body(pl.ds(pl.multiple_of(t * step, 8), step))
        return carry

    lax.fori_loop(0, rows // step, one, 0)


def pack_kernel(me_ref, a_ref, b_ref, *out_refs):
    _, x, c = bits(me_ref[0])
    height = a_ref.shape[1]
    rows = height // PARTS
    planes = a_ref.shape[0]
    for (r1, r0), out in zip(ROUNDS, out_refs):
        q = part(c ^ r1, x ^ r0)
        start = pl.multiple_of(q * rows, 8)
        above = pl.multiple_of(jnp.maximum(start - HALO, 0), 8)
        below = pl.multiple_of(jnp.minimum(start + rows, height - HALO), 8)
        for k, src in enumerate((a_ref, b_ref)):
            for i in range(planes):
                top = src[i, pl.ds(above, HALO), :]
                out[k, i, :HALO, :] = jnp.where(q > 0, top, 0.0)
                low = src[i, pl.ds(below, HALO), :]
                out[k, i, HALO + rows :, :] = jnp.where(q < PARTS - 1, low, 0.0)

                def one(t, carry, src=src, out=out, k=k, i=i, start=start):
                    at = pl.multiple_of(t * 16, 8)
                    out[k, i, pl.ds(at + HALO, 16), :] = src[i, pl.ds(pl.multiple_of(start + at, 8), 16), :]
                    return carry

                lax.fori_loop(0, rows // 16, one, 0, unroll=True)


def slot(me, r, planes, i):
    y, x, c = bits(me)
    r1, r0 = r
    from_c = y ^ r1
    block = x ^ r0 ^ c
    ahead = planes * from_c + i
    return block, jnp.where(c == 0, ahead, 2 * planes - 1 - ahead)


def place_kernel(me_ref, m0, m1, m2, m3, a_ref, b_ref):
    me = me_ref[0]
    planes, rows = m0.shape[1], m0.shape[2]
    for r, m in zip(ROUNDS, (m0, m1, m2, m3)):
        for i in range(planes):
            block, at = slot(me, r, planes, i)
            for flag, dst in ((1, a_ref), (0, b_ref)):

                @pl.when(block == flag)
                def _(dst=dst, m=m, i=i, at=at):
                    for k in range(2):
                        row_loop(rows, lambda s, k=k: dst.__setitem__((k, at, s), m[k, i, s]))


def edges(shape):
    col = lax.broadcasted_iota(jnp.int32, shape, 1)
    return col == 0, col == shape[1] - 1


def lap_rows(ref, s, r0, n, first, last):
    lo = HALO + r0
    mid = ref[s, lo : lo + n, :]
    width = mid.shape[1]
    beside = ref[s + 1, lo : lo + n, :] + ref[s - 1, lo : lo + n, :]
    beside = beside + (ref[s, lo + 1 : lo + n + 1, :] + ref[s, lo - 1 : lo + n - 1, :])
    right = jnp.where(last, 0.0, pltpu.roll(mid, width - 1, 1))
    left = jnp.where(first, 0.0, pltpu.roll(mid, 1, 1))
    return beside + (right + left) - 6.0 * mid, mid


def clear_rims(ref, rows):
    width = ref.shape[2]

    def one(s, carry):
        ref[s, :HALO, :] = jnp.zeros((HALO, width), F32)
        ref[s, HALO + rows :, :] = jnp.zeros((HALO, width), F32)
        return carry

    lax.fori_loop(0, ref.shape[0], one, 0)


def sequence(a_ref, b_ref, ra_ref, rb_ref, half):
    out = []
    for s in range(half):
        out.append((rb_ref, half - 1 - s, s))
        out.append((b_ref, s, half + s))
        out.append((a_ref, s, 2 * half + s))
        out.append((ra_ref, half - 1 - s, 3 * half + s))
    return out


CHUNK = 16


def forward_kernel(me_ref, a_ref, b_ref, ra_ref, rb_ref, u_out, c_out, slopes, u0, u1):
    half, rows = a_ref.shape[1], a_ref.shape[2]
    clear_rims(u0, rows)
    clear_rims(u1, rows)
    for src, at, s in sequence(a_ref, b_ref, ra_ref, rb_ref, half):

        def fill(t, carry, src=src, at=at, s=s):
            r = pl.multiple_of(t * 16, 8)
            u0[s, pl.ds(r + HALO, 16), :] = src[0, at, pl.ds(r, 16), :]
            c_out[s, pl.ds(r, 16), :] = time_step * src[1, at, pl.ds(r, 16), :]
            return carry

        lax.fori_loop(0, rows // 16, fill, 0)
    first, last = edges((CHUNK, a_ref.shape[3]))
    own = range(half, 3 * half)
    for k in range(ITERS):
        old, new = (u0, u1) if k % 2 == 0 else (u1, u0)
        wide = ITERS - 1 - k

        def plane(s, carry, k=k, old=old, new=new):
            keep = jnp.clip(s - half, 0, 2 * half - 1)
            for r0 in range(0, rows, CHUNK):
                slope, mid = lap_rows(old, s, r0, CHUNK, first, last)
                moved = mid + c_out[s, r0 : r0 + CHUNK, :] * slope
                if k == ITERS - 1:
                    u_out[s - half, r0 : r0 + CHUNK, :] = moved
                    slopes[k, s - half, r0 : r0 + CHUNK, :] = slope
                else:
                    new[s, HALO + r0 : HALO + r0 + CHUNK, :] = moved
                    slopes[k, keep, r0 : r0 + CHUNK, :] = slope
            return carry

        for lo, hi in ((own[0] - wide, own[0]), (own[-1] + 1, own[-1] + 1 + wide), (own[0], own[-1] + 1)):
            if hi > lo:
                lax.fori_loop(lo, hi, plane, 0)


def resid_kernel(me_ref, m0, m1, m2, m3, u_ref, a_ref, b_ref, total_ref, acc_ref):
    me = me_ref[0]
    planes, rows, width = m0.shape[1], m0.shape[2], m0.shape[3]
    acc_ref[...] = jnp.zeros((HALO, width), F32)
    for r, m in zip(ROUNDS, (m0, m1, m2, m3)):
        for i in range(planes):
            block, at = slot(me, r, planes, i)
            for flag, dst in ((1, a_ref), (0, b_ref)):

                @pl.when(block == flag)
                def _(m=m, i=i, at=at, dst=dst, flag=flag):
                    acc = acc_ref[...]
                    for lo in range(0, rows, HALO):
                        s = slice(lo, lo + HALO)
                        resid = u_ref[2 * planes * flag + at, s, :] - m[0, i, s, :]
                        weighted = m[1, i, s, :] * resid
                        dst[at, s, :] = weighted
                        if 0 < lo < rows - HALO:
                            acc = acc + weighted * resid
                    acc_ref[...] = acc

    total_ref[0, 0] = jnp.sum(acc_ref[...])


def backward_kernel(me_ref, part_ref, a_ref, b_ref, ra_ref, rb_ref, c_ref, slopes, o0, o1, o2, o3, lam, mv0, mv1, grad):
    me = me_ref[0]
    half, rows = a_ref.shape[0], a_ref.shape[1]
    inner = rows - 2 * HALO
    clear_rims(mv0, rows)
    clear_rims(mv1, rows)
    for src, at, s in sequence(a_ref, b_ref, ra_ref, rb_ref, half):

        def fill(t, carry, src=src, at=at, s=s):
            r = pl.multiple_of(t * 16, 8)
            v = src[at, pl.ds(r, 16), :]
            lam[s, pl.ds(r, 16), :] = v
            mv0[s, pl.ds(r + HALO, 16), :] = c_ref[s, pl.ds(r, 16), :] * v
            return carry

        lax.fori_loop(0, rows // 16, fill, 0)
    first, last = edges((CHUNK, a_ref.shape[2]))
    first8, last8 = edges((HALO, a_ref.shape[2]))
    own = range(half, 3 * half)
    for k in reversed(range(ITERS)):
        old, new = (mv0, mv1) if (ITERS - 1 - k) % 2 == 0 else (mv1, mv0)
        wide = k

        def halo_plane(s, carry, old=old, new=new):
            for r0 in range(0, rows, CHUNK):
                change, _ = lap_rows(old, s, r0, CHUNK, first, last)
                after = lam[s, r0 : r0 + CHUNK, :] + change
                lam[s, r0 : r0 + CHUNK, :] = after
                new[s, HALO + r0 : HALO + r0 + CHUNK, :] = c_ref[s, r0 : r0 + CHUNK, :] * after
            return carry

        def own_plane(s, carry, k=k, old=old, new=new):
            for r0 in range(HALO, rows - HALO, CHUNK):
                change, _ = lap_rows(old, s, r0, CHUNK, first, last)
                before = lam[s, r0 : r0 + CHUNK, :]
                g = before * slopes[k, s - half, r0 : r0 + CHUNK, :]
                at = slice(r0 - HALO, r0 - HALO + CHUNK)
                grad[s - half, at, :] = g if k == ITERS - 1 else grad[s - half, at, :] + g
                after = before + change
                lam[s, r0 : r0 + CHUNK, :] = after
                if k:
                    new[s, HALO + r0 : HALO + r0 + CHUNK, :] = c_ref[s, r0 : r0 + CHUNK, :] * after
            if k:
                for r0 in (0, rows - HALO):
                    change, _ = lap_rows(old, s, r0, HALO, first8, last8)
                    after = lam[s, r0 : r0 + HALO, :] + change
                    lam[s, r0 : r0 + HALO, :] = after
                    new[s, HALO + r0 : 2 * HALO + r0, :] = c_ref[s, r0 : r0 + HALO, :] * after
            return carry

        if wide:
            lax.fori_loop(own[0] - wide, own[0], halo_plane, 0)
            lax.fori_loop(own[-1] + 1, own[-1] + 1 + wide, halo_plane, 0)
        lax.fori_loop(own[0], own[-1] + 1, own_plane, 0)
    planes = half // 2
    for r, out in zip(ROUNDS, (o0, o1, o2, o3)):
        for i in range(planes):
            block, at = slot(me, r, planes, i)
            pos = half * block + at

            def one(t, carry, out=out, i=i, pos=pos):
                s = pl.multiple_of(t * 16, 8)
                out[0, i, pl.ds(s, 16), :] = grad[pos, pl.ds(s, 16), :]
                out[1, i, pl.ds(s, 16), :] = lam[half + pos, pl.ds(s + HALO, 16), :]
                return carry

            lax.fori_loop(0, inner // 16, one, 0)


def home_kernel(me_ref, scale_ref, m0, m1, m2, m3, g_ref, a_ref):
    _, x, c = bits(me_ref[0])
    planes, rows = m0.shape[1], m0.shape[2]
    for (r1, r0), m in zip(ROUNDS, (m0, m1, m2, m3)):
        start = part(c ^ r1, x ^ r0) * rows
        for k, out in enumerate((g_ref, a_ref)):
            scale = scale_ref[k]
            for i in range(planes):

                def one(t, carry, m=m, k=k, i=i, out=out, start=start, scale=scale):
                    s = pl.multiple_of(t * 16, 8)
                    out[i, pl.ds(pl.multiple_of(start + s, 8), 16), :] = m[k, i, pl.ds(s, 16), :] * scale
                    return carry

                lax.fori_loop(0, rows // 16, one, 0)


def shape(*dims):
    return jax.ShapeDtypeStruct(dims, F32)


def exchange_sum(value, axis, count, steps):
    for step in steps:
        value = value + lax.ppermute(value, axis, [(i, i ^ step) for i in range(count)])
    return value


def on_device(coefficient, initial_field, observed, misfit_weight):
    axis = "gz"
    count = lax.axis_size(axis)
    planes, height, width = coefficient.shape
    if count % GROUP or height % (16 * PARTS) or 2 * planes < ITERS or ITERS * 2 > HALO:
        raise ValueError("unsupported sizes")
    rows = height // PARTS
    tall = rows + 2 * HALO
    half = 2 * planes
    me = lax.axis_index(axis).astype(jnp.int32).reshape(1)

    partner = [(i, i ^ 1) for i in range(count)]
    beyond = []
    for i in range(count - GROUP + 1):
        if i % 2:
            if i + GROUP - 1 < count:
                beyond += [(i, i + GROUP - 1), (i + GROUP - 1, i)]

    def regroup(a, b):
        msgs = call(pack_kernel, [shape(2, planes, tall, width)] * 4, 2)(me, a, b)
        got = []
        for m, r in zip(msgs, ROUNDS):
            got.append(lax.ppermute(m, axis, send_pairs(count, *r)))
        return got

    first = regroup(initial_field, coefficient)
    second = regroup(observed, misfit_weight)

    pair = [shape(2, half, tall, width)] * 2
    blk_a, blk_b = call(place_kernel, pair, 4)(me, *first)
    far_a = lax.ppermute(blk_a, axis, partner)
    far_b = lax.ppermute(blk_b, axis, beyond)
    final, coef, slopes = call(
        forward_kernel,
        [shape(2 * half, tall, width), shape(4 * half, tall, width), shape(ITERS, 2 * half, tall, width)],
        4,
        [pltpu.VMEM((4 * half, tall + 2 * HALO, width), F32)] * 2,
    )(me, blk_a, blk_b, far_a, far_b)

    lam_a, lam_b, part_total = call(
        resid_kernel,
        [shape(half, tall, width)] * 2 + [shape(1, 1)],
        5,
        [pltpu.VMEM((HALO, width), F32)],
        out_specs=[VM, VM, SM],
    )(me, *second, final)
    far_la = lax.ppermute(lam_a, axis, partner)
    far_lb = lax.ppermute(lam_b, axis, beyond)
    near = [2, 4]
    far = [1] + [1 << k for k in range(3, count.bit_length() - 1)]
    part_total = exchange_sum(part_total, axis, count, near)
    outs = pl.pallas_call(
        backward_kernel,
        name="backward",
        out_shape=[shape(2, planes, rows, width)] * 4,
        in_specs=[SM, SM] + [VM] * 6,
        out_specs=[VM] * 4,
        compiler_params=PARAMS,
        scratch_shapes=[pltpu.VMEM((4 * half, tall, width), F32)]
        + [pltpu.VMEM((4 * half, tall + 2 * HALO, width), F32)] * 2
        + [pltpu.VMEM((2 * half, rows, width), F32)],
    )(me, part_total, lam_a, lam_b, far_la, far_lb, coef, slopes)
    back = [
        lax.ppermute(m, axis, [(j, i) for i, j in send_pairs(count, *r)]) for m, r in zip(outs, ROUNDS)
    ]

    if count & (count - 1):
        total = lax.psum(part_total, axis) / 4
    else:
        total = exchange_sum(part_total, axis, count, far)
    cells = count * planes * height * width
    misfit = jnp.sqrt(total[0, 0] / cells + 1e-06)
    inverse = 1.0 / misfit
    scale = jnp.stack([time_step * inverse, inverse])
    gradient, adjoint = pl.pallas_call(
        home_kernel,
        name="home",
        out_shape=[shape(planes, height, width)] * 2,
        in_specs=[SM, SM] + [VM] * 4,
        out_specs=[VM] * 2,
        compiler_params=PARAMS,
    )(me, scale, *back)
    return gradient, adjoint, misfit


def solution(mesh):
    placed = P("gz", None, None)
    return jax.shard_map(
        on_device,
        mesh=mesh,
        in_specs=(placed,) * 4,
        out_specs=(placed, placed, P()),
        check_vma=False,
    )
```

profile of v0, /device:TPU:0, one launch (start us, length us, event | category | flops | bytes accessed | tf_op | source)
XLA Modules:
  0.0 235.4 jit_solution(3819375443893526526)
XLA Ops:
  0.6 4.7 %shard_map.68 = (f32[2,2,144,512]{3,2,1,0:T(8,128)}, f32[2,2,144,512]{3,2,1,0:T(8,128)}, f32[2,2,144,512]{3,2,1,0:T(8,128)}, f32[2,2,144,512]{3,2,1,0:T(8,128)}) custom-call(s32[1]{0:T(128)} %bitcast.me_ref, f32[2,512,512]{2,1,0:T(8,128)} %a_ref.3, f32[2,512,512]{2,1,0:T(8,128)} %b_ref.3), custom_call_target="tpu_custom_call" | custom-call | tf_op jit(solution)/shard_map/pallas_call | solution.py:323
  5.3 1.9 collective-permute-start.4
  7.3 3.0 %collective-permute-start.5 = (f32[2,2,144,512]{3,2,1,0:T(8,128)}, f32[2,2,144,512]{3,2,1,0:T(8,128)S(1)}, u32[]{:S(2)}, u32[]{:S(2)}) collective-permute-start(f32[2,2,144,512]{3,2,1,0:T(8,128)} %get-tuple-element.30), channel_id=1, source_target_pairs={{0,2},{1,6},{2,0},{3,4},{4,3},{5,7},{6,1},{7,5},{8,10},{9,14},{10,... | collective-permute-start | bytes 3538952 | tf_op jit(solution)/shard_map/ppermute | solution.py:326
  10.2 2.8 %collective-permute-start.6 = (f32[2,2,144,512]{3,2,1,0:T(8,128)}, f32[2,2,144,512]{3,2,1,0:T(8,128)S(1)}, u32[]{:S(2)}, u32[]{:S(2)}) collective-permute-start(f32[2,2,144,512]{3,2,1,0:T(8,128)} %get-tuple-element.31), channel_id=1, source_target_pairs={{0,4},{1,0},{2,6},{3,2},{4,5},{5,1},{6,7},{7,3},{8,12},{9,8},{10,1... | collective-permute-start | bytes 3538952 | tf_op jit(solution)/shard_map/ppermute | solution.py:326
  13.0 23.5 %collective-permute-done.5.m1 = f32[2,2,144,512]{3,2,1,0:T(8,128)S(1)} collective-permute-done((f32[2,2,144,512]{3,2,1,0:T(8,128)}, f32[2,2,144,512]{3,2,1,0:T(8,128)S(1)}, u32[]{:S(2)}, u32[]{:S(2)}) %collective-permute-start.5) | collective-permute-done | bytes 1179680 | tf_op jit(solution)/shard_map/ppermute | solution.py:326
  36.5 25.1 %collective-permute-done.6.m2 = f32[2,2,144,512]{3,2,1,0:T(8,128)S(1)} collective-permute-done((f32[2,2,144,512]{3,2,1,0:T(8,128)}, f32[2,2,144,512]{3,2,1,0:T(8,128)S(1)}, u32[]{:S(2)}, u32[]{:S(2)}) %collective-permute-start.6) | collective-permute-done | bytes 1179680 | tf_op jit(solution)/shard_map/ppermute | solution.py:326
  62.7 5.4 %shard_map.69 = (f32[2,4,144,512]{3,2,1,0:T(8,128)}, f32[2,4,144,512]{3,2,1,0:T(8,128)}) custom-call(s32[1]{0:T(128)} %bitcast.me_ref, f32[2,2,144,512]{3,2,1,0:T(8,128)} %copy-done.4, f32[2,2,144,512]{3,2,1,0:T(8,128)} %copy-done.5, f32[2,2,144,512]{3,2,1,0:T(8,128)} %copy-done.6, f32[2,2,144,512]{3,2,1,0:T(8,128)} %collective-permute-done.7.m3), custom_call_target="tpu_custom_call" | custom-call | tf_op jit(solution)/shard_map/pallas_call | solution.py:333
  69.2 2.1 collective-permute-start.9
  71.3 4.7 %shard_map.67 = (f32[2,2,144,512]{3,2,1,0:T(8,128)}, f32[2,2,144,512]{3,2,1,0:T(8,128)}, f32[2,2,144,512]{3,2,1,0:T(8,128)}, f32[2,2,144,512]{3,2,1,0:T(8,128)}) custom-call(s32[1]{0:T(128)} %bitcast.me_ref, f32[2,512,512]{2,1,0:T(8,128)} %a_ref.2, f32[2,512,512]{2,1,0:T(8,128)} %b_ref.2), custom_call_target="tpu_custom_call" | custom-call | tf_op jit(solution)/shard_map/pallas_call | solution.py:323
  76.0 1.9 collective-permute-start
  79.4 2.6 %collective-permute-start.2 = (f32[2,2,144,512]{3,2,1,0:T(8,128)}, f32[2,2,144,512]{3,2,1,0:T(8,128)}, u32[]{:S(2)}, u32[]{:S(2)}) collective-permute-start(f32[2,2,144,512]{3,2,1,0:T(8,128)} %get-tuple-element.27), channel_id=1, source_target_pairs={{0,4},{1,0},{2,6},{3,2},{4,5},{5,1},{6,7},{7,3},{8,12},{9,8},{10,1... | collective-permute-start | bytes 3538952 | tf_op jit(solution)/shard_map/ppermute | solution.py:326
  83.5 20.9 %shard_map.70 = (f32[8,144,512]{2,1,0:T(8,128)}, f32[16,144,512]{2,1,0:T(8,128)}, f32[4,8,144,512]{3,2,1,0:T(8,128)}) custom-call(s32[1]{0:T(128)} %bitcast.me_ref, f32[2,4,144,512]{3,2,1,0:T(8,128)} %get-tuple-element.33.a_ref, f32[2,4,144,512]{3,2,1,0:T(8,128)} %get-tuple-element.34.b_ref, f32[2,4,144,512]{3,2,1,0:T(8,128)} %copy-done, ...), custom_call_target="tpu_custom_call" | custom-call | tf_op jit(solution)/shard_map/pallas_call | solution.py:336
  105.1 25.6 %collective-permute-done.2.m2 = f32[2,2,144,512]{3,2,1,0:T(8,128)} collective-permute-done((f32[2,2,144,512]{3,2,1,0:T(8,128)}, f32[2,2,144,512]{3,2,1,0:T(8,128)}, u32[]{:S(2)}, u32[]{:S(2)}) %collective-permute-start.2) | collective-permute-done | bytes 1179680 | tf_op jit(solution)/shard_map/ppermute | solution.py:326
  132.4 5.1 %shard_map.71 = (f32[4,144,512]{2,1,0:T(8,128)}, f32[4,144,512]{2,1,0:T(8,128)}, f32[1,1]{1,0:T(1,128)}) custom-call(s32[1]{0:T(128)} %bitcast.me_ref, f32[2,2,144,512]{3,2,1,0:T(8,128)} %copy-done.3, f32[2,2,144,512]{3,2,1,0:T(8,128)} %collective-permute-done.1.m1, f32[2,2,144,512]{3,2,1,0:T(8,128)} %collective-permute-done.2.m2, ...), custom_call_target="tpu_custom_call" | custom-call | tf_op jit(solution)/shard_map/pallas_call | solution.py:343
  140.7 2.3 collective-permute-done.10
  144.3 2.0 collective-permute-start.11
  150.0 20.8 %backward.1 = (f32[2,2,128,512]{3,2,1,0:T(8,128)}, f32[2,2,128,512]{3,2,1,0:T(8,128)}, f32[2,2,128,512]{3,2,1,0:T(8,128)}, f32[2,2,128,512]{3,2,1,0:T(8,128)}) custom-call(s32[1]{0:T(128)} %bitcast.me_ref, f32[1,1]{1,0:T(1,128)} %add.20.part_ref, f32[4,144,512]{2,1,0:T(8,128)} %get-tuple-element.37.a_ref, f32[4,144,512]{2,1,0:T(8,128)} %get-tuple-element.38.b_ref, ...), custom_call_target="tpu_custom_call" | custom-call | tf_op jit(solution)/shard_map/backward/pallas_call | solution.py:355
  170.8 1.9 collective-permute-start.17
  174.1 8.5 %collective-permute-start.19 = (f32[2,2,128,512]{3,2,1,0:T(8,128)}, f32[2,2,128,512]{3,2,1,0:T(8,128)S(1)}, u32[]{:S(2)}, u32[]{:S(2)}) collective-permute-start(f32[2,2,128,512]{3,2,1,0:T(8,128)} %get-tuple-element.43), channel_id=1, source_target_pairs={{4,0},{0,1},{6,2},{2,3},{5,4},{1,5},{7,6},{3,7},{12,8},{8,9},{14,1... | collective-permute-start | bytes 3145736 | tf_op jit(solution)/shard_map/ppermute | solution.py:367
  182.8 2.5 %collective-permute-start.12 = (f32[1,1]{1,0:T(1,128)}, f32[1,1]{1,0:T(1,128)}, u32[]{:S(2)}, u32[]{:S(2)}) collective-permute-start(f32[1,1]{1,0:T(1,128)} %add.20.part_ref), channel_id=1, source_target_pairs={{0,1},{1,0},{2,3},{3,2},{4,5},{5,4},{6,7},{7,6},{8,9},{9,8},{10,11... | collective-permute-start | bytes 20 | tf_op jit(solution)/shard_map/ppermute | solution.py:300
  185.8 3.0 %collective-permute-start.13 = (f32[1,1]{1,0:T(1,128)}, f32[1,1]{1,0:T(1,128)}, u32[]{:S(2)}, u32[]{:S(2)}) collective-permute-start(f32[1,1]{1,0:T(1,128)} %add.21), channel_id=1, source_target_pairs={{0,8},{1,9},{2,10},{3,11},{4,12},{5,13},{6,14},{7,15},{8,0},{9,1},... | collective-permute-start | bytes 20 | tf_op jit(solution)/shard_map/ppermute | solution.py:300
  190.1 4.0 %collective-permute-start.14 = (f32[1,1]{1,0:T(1,128)}, f32[1,1]{1,0:T(1,128)}, u32[]{:S(2)}, u32[]{:S(2)}) collective-permute-start(f32[1,1]{1,0:T(1,128)} %add.22), channel_id=1, source_target_pairs={{0,16},{1,17},{2,18},{3,19},{4,20},{5,21},{6,22},{7,23},{8,24},{9,... | collective-permute-start | bytes 20 | tf_op jit(solution)/shard_map/ppermute | solution.py:300
  195.9 32.3 %collective-permute-done.19.m2 = f32[2,2,128,512]{3,2,1,0:T(8,128)S(1)} collective-permute-done((f32[2,2,128,512]{3,2,1,0:T(8,128)}, f32[2,2,128,512]{3,2,1,0:T(8,128)S(1)}, u32[]{:S(2)}, u32[]{:S(2)}) %collective-permute-start.19) | collective-permute-done | bytes 1048608 | tf_op jit(solution)/shard_map/ppermute | solution.py:367
  229.2 5.1 %home.1 = (f32[2,512,512]{2,1,0:T(8,128)}, f32[2,512,512]{2,1,0:T(8,128)}) custom-call(s32[1]{0:T(128)} %bitcast.me_ref, f32[2]{0:T(128)} %pad_maximum_fusion.scale_ref, f32[2,2,128,512]{3,2,1,0:T(8,128)} %copy-done.7, f32[2,2,128,512]{3,2,1,0:T(8,128)} %copy-done.8, f32[2,2,128,512]{3,2,1,0:T(8,128)} %copy-done.9, f32[2,2,128,512]{3,2,1,0:T(8,128)} %collective-permute-done.20.m3), custom_call_target="tpu_custom_call" | custom-call | tf_op jit(solution)/shard_map/home/pallas_call | solution.py:378
  (46 shorter events, 18.3 us)
Async XLA Ops:
  5.3 7.6 %collective-permute-start.4 = (f32[2,2,144,512]{3,2,1,0:T(8,128)}, f32[2,2,144,512]{3,2,1,0:T(8,128)S(1)}, u32[]{:S(2)}, u32[]{:S(2)}) collective-permute-start(f32[2,2,144,512]{3,2,1,0:T(8,128)} %get-tuple-element.29), channel_id=1, source_target_pairs={{0,0},{1,4},{2,2},{3,6},{4,1},{5,5},{6,3},{7,7},{8,8},{9,12},{10,1... | collective-permute-start | bytes 3538952 | tf_op jit(solution)/shard_map/ppermute | solution.py:326
  7.3 29.2 %collective-permute-start.5 = (f32[2,2,144,512]{3,2,1,0:T(8,128)}, f32[2,2,144,512]{3,2,1,0:T(8,128)S(1)}, u32[]{:S(2)}, u32[]{:S(2)}) collective-permute-start(f32[2,2,144,512]{3,2,1,0:T(8,128)} %get-tuple-element.30), channel_id=1, source_target_pairs={{0,2},{1,6},{2,0},{3,4},{4,3},{5,7},{6,1},{7,5},{8,10},{9,14},{10,... | collective-permute-start | bytes 3538952 | tf_op jit(solution)/shard_map/ppermute | solution.py:326
  10.2 51.4 %collective-permute-start.6 = (f32[2,2,144,512]{3,2,1,0:T(8,128)}, f32[2,2,144,512]{3,2,1,0:T(8,128)S(1)}, u32[]{:S(2)}, u32[]{:S(2)}) collective-permute-start(f32[2,2,144,512]{3,2,1,0:T(8,128)} %get-tuple-element.31), channel_id=1, source_target_pairs={{0,4},{1,0},{2,6},{3,2},{4,5},{5,1},{6,7},{7,3},{8,12},{9,8},{10,1... | collective-permute-start | bytes 3538952 | tf_op jit(solution)/shard_map/ppermute | solution.py:326
  13.0 49.7 %collective-permute-start.7 = (f32[2,2,144,512]{3,2,1,0:T(8,128)}, f32[2,2,144,512]{3,2,1,0:T(8,128)}, u32[]{:S(2)}, u32[]{:S(2)}) collective-permute-start(f32[2,2,144,512]{3,2,1,0:T(8,128)} %get-tuple-element.32), channel_id=1, source_target_pairs={{0,6},{1,2},{2,4},{3,0},{4,7},{5,3},{6,5},{7,1},{8,14},{9,10},{10,... | collective-permute-start | bytes 3538952 | tf_op jit(solution)/shard_map/ppermute | solution.py:326
  13.0 49.7 %copy-start.4 = (f32[2,2,144,512]{3,2,1,0:T(8,128)}, f32[2,2,144,512]{3,2,1,0:T(8,128)S(1)}, u32[]{:S(2)}) copy-start(f32[2,2,144,512]{3,2,1,0:T(8,128)S(1)} %collective-permute-done.4.m0) | copy-start | bytes 3538948
  68.1 13.9 %collective-permute-start.8 = (f32[2,4,144,512]{3,2,1,0:T(8,128)}, f32[2,4,144,512]{3,2,1,0:T(8,128)S(1)}, u32[]{:S(2)}, u32[]{:S(2)}) collective-permute-start(f32[2,4,144,512]{3,2,1,0:T(8,128)} %get-tuple-element.33.a_ref), channel_id=1, source_target_pairs={{0,1},{1,0},{2,3},{3,2},{4,5},{5,4},{6,7},{7,6},{8,9},{9,8},{10,11... | collective-permute-start | bytes 7077896 | tf_op jit(solution)/shard_map/ppermute | solution.py:334
  69.2 12.9 %collective-permute-start.9 = (f32[2,4,144,512]{3,2,1,0:T(8,128)}, f32[2,4,144,512]{3,2,1,0:T(8,128)}, u32[]{:S(2)}, u32[]{:S(2)}) collective-permute-start(f32[2,4,144,512]{3,2,1,0:T(8,128)} %get-tuple-element.34.b_ref), channel_id=1, source_target_pairs={{1,8},{8,1},{3,10},{10,3},{5,12},{12,5},{7,14},{14,7},{9,16},{16,9... | collective-permute-start | bytes 7077896 | tf_op jit(solution)/shard_map/ppermute | solution.py:335
  76.0 28.4 %collective-permute-start = (f32[2,2,144,512]{3,2,1,0:T(8,128)}, f32[2,2,144,512]{3,2,1,0:T(8,128)S(1)}, u32[]{:S(2)}, u32[]{:S(2)}) collective-permute-start(f32[2,2,144,512]{3,2,1,0:T(8,128)} %get-tuple-element.25), channel_id=1, source_target_pairs={{0,0},{1,4},{2,2},{3,6},{4,1},{5,5},{6,3},{7,7},{8,8},{9,12},{10,1... | collective-permute-start | bytes 3538952 | tf_op jit(solution)/shard_map/ppermute | solution.py:326
  77.9 27.1 %collective-permute-start.1 = (f32[2,2,144,512]{3,2,1,0:T(8,128)}, f32[2,2,144,512]{3,2,1,0:T(8,128)}, u32[]{:S(2)}, u32[]{:S(2)}) collective-permute-start(f32[2,2,144,512]{3,2,1,0:T(8,128)} %get-tuple-element.26), channel_id=1, source_target_pairs={{0,2},{1,6},{2,0},{3,4},{4,3},{5,7},{6,1},{7,5},{8,10},{9,14},{10,... | collective-permute-start | bytes 3538952 | tf_op jit(solution)/shard_map/ppermute | solution.py:326
  79.4 51.3 %collective-permute-start.2 = (f32[2,2,144,512]{3,2,1,0:T(8,128)}, f32[2,2,144,512]{3,2,1,0:T(8,128)}, u32[]{:S(2)}, u32[]{:S(2)}) collective-permute-start(f32[2,2,144,512]{3,2,1,0:T(8,128)} %get-tuple-element.27), channel_id=1, source_target_pairs={{0,4},{1,0},{2,6},{3,2},{4,5},{5,1},{6,7},{7,3},{8,12},{9,8},{10,1... | collective-permute-start | bytes 3538952 | tf_op jit(solution)/shard_map/ppermute | solution.py:326
  82.1 50.4 %collective-permute-start.3 = (f32[2,2,144,512]{3,2,1,0:T(8,128)}, f32[2,2,144,512]{3,2,1,0:T(8,128)}, u32[]{:S(2)}, u32[]{:S(2)}) collective-permute-start(f32[2,2,144,512]{3,2,1,0:T(8,128)} %get-tuple-element.28), channel_id=1, source_target_pairs={{0,6},{1,2},{2,4},{3,0},{4,7},{5,3},{6,5},{7,1},{8,14},{9,10},{10,... | collective-permute-start | bytes 3538952 | tf_op jit(solution)/shard_map/ppermute | solution.py:326
  137.5 11.0 %collective-permute-start.15 = (f32[4,144,512]{2,1,0:T(8,128)}, f32[4,144,512]{2,1,0:T(8,128)S(1)}, u32[]{:S(2)}, u32[]{:S(2)}) collective-permute-start(f32[4,144,512]{2,1,0:T(8,128)} %get-tuple-element.37.a_ref), channel_id=1, source_target_pairs={{0,1},{1,0},{2,3},{3,2},{4,5},{5,4},{6,7},{7,6},{8,9},{9,8},{10,11... | collective-permute-start | bytes 3538952 | tf_op jit(solution)/shard_map/ppermute | solution.py:350
  138.5 10.1 %collective-permute-start.16 = (f32[4,144,512]{2,1,0:T(8,128)}, f32[4,144,512]{2,1,0:T(8,128)S(1)}, u32[]{:S(2)}, u32[]{:S(2)}) collective-permute-start(f32[4,144,512]{2,1,0:T(8,128)} %get-tuple-element.38.b_ref), channel_id=1, source_target_pairs={{1,8},{8,1},{3,10},{10,3},{5,12},{12,5},{7,14},{14,7},{9,16},{16,9... | collective-permute-start | bytes 3538952 | tf_op jit(solution)/shard_map/ppermute | solution.py:351
  139.2 3.9 %collective-permute-start.10 = (f32[1,1]{1,0:T(1,128)}, f32[1,1]{1,0:T(1,128)}, u32[]{:S(2)}, u32[]{:S(2)}) collective-permute-start(f32[1,1]{1,0:T(1,128)} %get-tuple-element.36), channel_id=1, source_target_pairs={{0,2},{1,3},{2,0},{3,1},{4,6},{5,7},{6,4},{7,5},{8,10},{9,11},{10,... | collective-permute-start | bytes 20 | tf_op jit(solution)/shard_map/ppermute | solution.py:300
  144.3 3.7 %collective-permute-start.11 = (f32[1,1]{1,0:T(1,128)}, f32[1,1]{1,0:T(1,128)}, u32[]{:S(2)}, u32[]{:S(2)}) collective-permute-start(f32[1,1]{1,0:T(1,128)} %add.19), channel_id=1, source_target_pairs={{0,4},{1,5},{2,6},{3,7},{4,0},{5,1},{6,2},{7,3},{8,12},{9,13},{10,... | collective-permute-start | bytes 20 | tf_op jit(solution)/shard_map/ppermute | solution.py:300
  170.8 25.2 %collective-permute-start.17 = (f32[2,2,128,512]{3,2,1,0:T(8,128)}, f32[2,2,128,512]{3,2,1,0:T(8,128)S(1)}, u32[]{:S(2)}, u32[]{:S(2)}) collective-permute-start(f32[2,2,128,512]{3,2,1,0:T(8,128)} %get-tuple-element.41), channel_id=1, source_target_pairs={{0,0},{4,1},{2,2},{6,3},{1,4},{5,5},{3,6},{7,7},{8,8},{12,9},{10,1... | collective-permute-start | bytes 3145736 | tf_op jit(solution)/shard_map/ppermute | solution.py:367
  172.6 23.3 %collective-permute-start.18 = (f32[2,2,128,512]{3,2,1,0:T(8,128)}, f32[2,2,128,512]{3,2,1,0:T(8,128)S(1)}, u32[]{:S(2)}, u32[]{:S(2)}) collective-permute-start(f32[2,2,128,512]{3,2,1,0:T(8,128)} %get-tuple-element.42), channel_id=1, source_target_pairs={{2,0},{6,1},{0,2},{4,3},{3,4},{7,5},{1,6},{5,7},{10,8},{14,9},{8,1... | collective-permute-start | bytes 3145736 | tf_op jit(solution)/shard_map/ppermute | solution.py:367
  174.1 54.1 %collective-permute-start.19 = (f32[2,2,128,512]{3,2,1,0:T(8,128)}, f32[2,2,128,512]{3,2,1,0:T(8,128)S(1)}, u32[]{:S(2)}, u32[]{:S(2)}) collective-permute-start(f32[2,2,128,512]{3,2,1,0:T(8,128)} %get-tuple-element.43), channel_id=1, source_target_pairs={{4,0},{0,1},{6,2},{2,3},{5,4},{1,5},{7,6},{3,7},{12,8},{8,9},{14,1... | collective-permute-start | bytes 3145736 | tf_op jit(solution)/shard_map/ppermute | solution.py:367
  182.6 45.6 %collective-permute-start.20 = (f32[2,2,128,512]{3,2,1,0:T(8,128)}, f32[2,2,128,512]{3,2,1,0:T(8,128)}, u32[]{:S(2)}, u32[]{:S(2)}) collective-permute-start(f32[2,2,128,512]{3,2,1,0:T(8,128)} %get-tuple-element.44), channel_id=1, source_target_pairs={{6,0},{2,1},{4,2},{0,3},{7,4},{3,5},{5,6},{1,7},{14,8},{10,9},{12,... | collective-permute-start | bytes 3145736 | tf_op jit(solution)/shard_map/ppermute | solution.py:367
  182.8 2.5 %collective-permute-start.12 = (f32[1,1]{1,0:T(1,128)}, f32[1,1]{1,0:T(1,128)}, u32[]{:S(2)}, u32[]{:S(2)}) collective-permute-start(f32[1,1]{1,0:T(1,128)} %add.20.part_ref), channel_id=1, source_target_pairs={{0,1},{1,0},{2,3},{3,2},{4,5},{5,4},{6,7},{7,6},{8,9},{9,8},{10,11... | collective-permute-start | bytes 20 | tf_op jit(solution)/shard_map/ppermute | solution.py:300
  185.8 3.7 %collective-permute-start.13 = (f32[1,1]{1,0:T(1,128)}, f32[1,1]{1,0:T(1,128)}, u32[]{:S(2)}, u32[]{:S(2)}) collective-permute-start(f32[1,1]{1,0:T(1,128)} %add.21), channel_id=1, source_target_pairs={{0,8},{1,9},{2,10},{3,11},{4,12},{5,13},{6,14},{7,15},{8,0},{9,1},... | collective-permute-start | bytes 20 | tf_op jit(solution)/shard_map/ppermute | solution.py:300
  190.1 4.6 %collective-permute-start.14 = (f32[1,1]{1,0:T(1,128)}, f32[1,1]{1,0:T(1,128)}, u32[]{:S(2)}, u32[]{:S(2)}) collective-permute-start(f32[1,1]{1,0:T(1,128)} %add.22), channel_id=1, source_target_pairs={{0,16},{1,17},{2,18},{3,19},{4,20},{5,21},{6,22},{7,23},{8,24},{9,... | collective-permute-start | bytes 20 | tf_op jit(solution)/shard_map/ppermute | solution.py:300
  195.9 32.3 %copy-start.7 = (f32[2,2,128,512]{3,2,1,0:T(8,128)}, f32[2,2,128,512]{3,2,1,0:T(8,128)S(1)}, u32[]{:S(2)}) copy-start(f32[2,2,128,512]{3,2,1,0:T(8,128)S(1)} %collective-permute-done.17.m0) | copy-start | bytes 3145732
  195.9 32.3 %copy-start.8 = (f32[2,2,128,512]{3,2,1,0:T(8,128)}, f32[2,2,128,512]{3,2,1,0:T(8,128)S(1)}, u32[]{:S(2)}) copy-start(f32[2,2,128,512]{3,2,1,0:T(8,128)S(1)} %collective-permute-done.18.m1) | copy-start | bytes 3145732
  (7 other events, 60.2 us)
where the time goes:
time: 236 us; the launch traced here: 235 us
  waiting for transfers between devices  115 us (49%)
  Pallas kernels  66.7 us (28%)
  starting transfers between devices  43.7 us (19%)
  between operations  5.38 us (2%)
  local copies, waits for them, and re-layouts  3.74 us (2%)
    ppermute x8, waiting for transfers between devices, regroup(): got.append(lax.ppermute(m, axis, send_pairs(count, *r)))  77.7 us
    ppermute x4, waiting for transfers between devices, on_device(): lax.ppermute(m, axis, [(j, i) for i, j in send_pairs(count, *r)])  32.3 us
    pallas_call x1, Pallas kernels, on_device(): call(forward_kernel, [shape(2 * half, tall, width), shape(4 * half, tall,...  20.9 us
    pallas_call x1, Pallas kernels, on_device(): pl.pallas_call(backward_kernel, name='backward', out_shape=[shape(2, plan...  20.8 us
    ppermute x8, starting transfers between devices, regroup(): got.append(lax.ppermute(m, axis, send_pairs(count, *r)))  13.8 us
    ppermute x5, starting transfers between devices, exchange_sum(): lax.ppermute(value, axis, [(i, i ^ step) for i in range(count)])  13.1 us
    ppermute x4, starting transfers between devices, on_device(): lax.ppermute(m, axis, [(j, i) for i, j in send_pairs(count, *r)])  12 us
    pallas_call x2, Pallas kernels, regroup(): msgs = call(pack_kernel, [shape(2, planes, tall, width)] * 4, 2)(me, a, b)  9.41 us
  transfers between devices with their start and end apart: 21, of which 11 were waited for; matrix products, arithmetic and copies ran while one was open for 0% of the time, Pallas kernels for 11%

commit v1 on v0

v1 whole, which is shorter than its diff:
```python
import jax
import jax.numpy as jnp
from jax import lax
from jax.experimental import pallas as pl
from jax.experimental.pallas import tpu as pltpu
from jax.sharding import PartitionSpec as P


ITERS = 4
time_step = 0.125

GROUP = 8
PARTS = 4
HALO = 8
ROUNDS = ((0, 0), (0, 1), (1, 0), (1, 1))


VM = pl.BlockSpec(memory_space=pltpu.VMEM)
SM = pl.BlockSpec(memory_space=pltpu.SMEM)
PARAMS = pltpu.CompilerParams(vmem_limit_bytes=32 * 1024 * 1024)
F32 = jnp.float32


def call(kernel, outs, scalars, arrays, scratch=(), total=False, **options):
    return pl.pallas_call(
        kernel,
        out_shape=outs,
        in_specs=[SM] * len(scalars) + [VM] * len(arrays),
        out_specs=[VM] * (len(outs) - total) + [SM] * total,
        scratch_shapes=scratch,
        compiler_params=PARAMS,
        **options,
    )(*scalars, *arrays)


def inside(*arrays):
    return [pltpu.with_memory_space_constraint(a, pltpu.VMEM) for a in arrays]


def outside(*arrays):
    return [pltpu.with_memory_space_constraint(a, pltpu.HBM) for a in arrays]


def bits(me):
    return (me >> 2) & 1, (me >> 1) & 1, me & 1


def part(y, x):
    return 2 * y + x


def send_pairs(count, r1, r0):
    pairs = []
    for i in range(count):
        y, x, c = bits(i)
        pairs.append((i, (i & ~7) + 4 * (c ^ r1) + 2 * (x ^ r0) + y))
    return pairs


def row_loop(rows, body, step=16):
    def one(t, carry):
        body(pl.ds(pl.multiple_of(t * step, 8), step))
        return carry

    lax.fori_loop(0, rows // step, one, 0)


def pack_kernel(me_ref, a_ref, b_ref, *out_refs):
    _, x, c = bits(me_ref[0])
    height = a_ref.shape[1]
    rows = height // PARTS
    planes = a_ref.shape[0]
    for (r1, r0), out in zip(ROUNDS, out_refs):
        q = part(c ^ r1, x ^ r0)
        start = pl.multiple_of(q * rows, 8)
        above = pl.multiple_of(jnp.maximum(start - HALO, 0), 8)
        below = pl.multiple_of(jnp.minimum(start + rows, height - HALO), 8)
        for k, src in enumerate((a_ref, b_ref)):
            for i in range(planes):
                top = src[i, pl.ds(above, HALO), :]
                out[k, i, :HALO, :] = jnp.where(q > 0, top, 0.0)
                low = src[i, pl.ds(below, HALO), :]
                out[k, i, HALO + rows :, :] = jnp.where(q < PARTS - 1, low, 0.0)

                def one(t, carry, src=src, out=out, k=k, i=i, start=start):
                    at = pl.multiple_of(t * 16, 8)
                    out[k, i, pl.ds(at + HALO, 16), :] = src[i, pl.ds(pl.multiple_of(start + at, 8), 16), :]
                    return carry

                lax.fori_loop(0, rows // 16, one, 0, unroll=True)


def slot(me, r, planes, i):
    y, x, c = bits(me)
    r1, r0 = r
    from_c = y ^ r1
    block = x ^ r0 ^ c
    ahead = planes * from_c + i
    return block, jnp.where(c == 0, ahead, 2 * planes - 1 - ahead)


def place_kernel(me_ref, m0, m1, m2, m3, a_ref, b_ref):
    me = me_ref[0]
    planes, rows = m0.shape[1], m0.shape[2]
    for r, m in zip(ROUNDS, (m0, m1, m2, m3)):
        for i in range(planes):
            block, at = slot(me, r, planes, i)
            for flag, dst in ((1, a_ref), (0, b_ref)):

                @pl.when(block == flag)
                def _(dst=dst, m=m, i=i, at=at):
                    for k in range(2):
                        row_loop(rows, lambda s, k=k: dst.__setitem__((k, at, s), m[k, i, s]))


def edges(shape):
    col = lax.broadcasted_iota(jnp.int32, shape, 1)
    return col == 0, col == shape[1] - 1


def lap_rows(ref, s, r0, n, first, last):
    lo = HALO + r0
    mid = ref[s, lo : lo + n, :]
    width = mid.shape[1]
    beside = ref[s + 1, lo : lo + n, :] + ref[s - 1, lo : lo + n, :]
    beside = beside + (ref[s, lo + 1 : lo + n + 1, :] + ref[s, lo - 1 : lo + n - 1, :])
    right = jnp.where(last, 0.0, pltpu.roll(mid, width - 1, 1))
    left = jnp.where(first, 0.0, pltpu.roll(mid, 1, 1))
    return beside + (right + left) - 6.0 * mid, mid


def clear_rims(ref, rows):
    width = ref.shape[2]

    def one(s, carry):
        ref[s, :HALO, :] = jnp.zeros((HALO, width), F32)
        ref[s, HALO + rows :, :] = jnp.zeros((HALO, width), F32)
        return carry

    lax.fori_loop(0, ref.shape[0], one, 0)


CHUNK = 16


def copy_rows(rows, move):
    def one(t, carry):
        r = pl.multiple_of(t * CHUNK, 8)
        move(pl.ds(r, CHUNK), pl.ds(r + HALO, CHUNK))
        return carry

    lax.fori_loop(0, rows // CHUNK, one, 0)


def spans(lo, hi, body):
    if hi > lo:
        lax.fori_loop(lo, hi, body, 0)


def forward_main(me_ref, a_ref, b_ref, ra_ref, u_out, c_out, slopes, saved, u0, u1):
    half, rows = a_ref.shape[1], a_ref.shape[2]
    clear_rims(u0, rows)
    clear_rims(u1, rows)
    for i in range(half):
        for src, at, t in ((b_ref, i, i), (a_ref, i, half + i), (ra_ref, half - 1 - i, 2 * half + i)):

            def fill(r, rh, src=src, at=at, t=t):
                u0[t, rh, :] = src[0, at, r, :]
                c_out[t, r, :] = time_step * src[1, at, r, :]

            copy_rows(rows, fill)
    first, last = edges((CHUNK, a_ref.shape[3]))
    for k in range(ITERS):
        old, new = (u0, u1) if k % 2 == 0 else (u1, u0)

        def plane(t, carry, own, k=k, old=old, new=new):
            for r0 in range(0, rows, CHUNK):
                slope, mid = lap_rows(old, t, r0, CHUNK, first, last)
                moved = mid + c_out[t, r0 : r0 + CHUNK, :] * slope
                if own:
                    slopes[k, t, r0 : r0 + CHUNK, :] = slope
                if k == ITERS - 1:
                    u_out[t, r0 : r0 + CHUNK, :] = moved
                else:
                    new[t, HALO + r0 : HALO + r0 + CHUNK, :] = moved
            return carry

        spans(1 + k, 2 * half, lambda t, c: plane(t, c, True))
        spans(2 * half, 2 * half + ITERS - 1 - k, lambda t, c: plane(t, c, False))
        if k < ITERS - 1:
            for i in range(2):

                def keep(r, rh, k=k, i=i, new=new):
                    saved[k, i, r, :] = new[k + 1 + i, rh, :]

                copy_rows(rows, keep)


def forward_wedge(me_ref, b_ref, rb_ref, c_ref, saved, u_in, slopes_in, u_out, slopes, w0, w1, cw):
    half, rows = b_ref.shape[1], b_ref.shape[2]
    clear_rims(w0, rows)
    clear_rims(w1, rows)
    for i in range(half):

        def fill(r, rh, i=i):
            w0[i, rh, :] = rb_ref[0, half - 1 - i, r, :]
            cw[i, r, :] = time_step * rb_ref[1, half - 1 - i, r, :]

        copy_rows(rows, fill)
    for i in range(2):
        copy_rows(rows, lambda r, rh, i=i: w0.__setitem__((half + i, rh), b_ref[0, i, r, :]))
    first, last = edges((CHUNK, b_ref.shape[3]))
    for k in range(ITERS):
        old, new = (w0, w1) if k % 2 == 0 else (w1, w0)
        if k:
            for i in range(2):
                copy_rows(rows, lambda r, rh, i=i: old.__setitem__((half + k + i, rh), saved[k - 1, i, r, :]))

        def plane(s, carry, own, k=k, old=old, new=new):
            for r0 in range(0, rows, CHUNK):
                slope, mid = lap_rows(old, s, r0, CHUNK, first, last)
                at = slice(r0, r0 + CHUNK)
                coef = c_ref[s - half, at, :] if own else cw[s, at, :]
                moved = mid + coef * slope
                if own:
                    slopes[k, s - half, at, :] = slope
                if k == ITERS - 1:
                    u_out[s - half, at, :] = moved
                else:
                    new[s, HALO + r0 : HALO + r0 + CHUNK, :] = moved
            return carry

        spans(half - ITERS + 1 + k, half, lambda s, c: plane(s, c, False))
        spans(half, half + k + 1, lambda s, c: plane(s, c, True))


def resid_kernel(me_ref, m0, m1, m2, m3, u_ref, a_ref, b_ref, total_ref, acc_ref):
    me = me_ref[0]
    planes, rows, width = m0.shape[1], m0.shape[2], m0.shape[3]
    acc_ref[...] = jnp.zeros((HALO, width), F32)
    for r, m in zip(ROUNDS, (m0, m1, m2, m3)):
        for i in range(planes):
            block, at = slot(me, r, planes, i)
            for flag, dst in ((1, a_ref), (0, b_ref)):

                @pl.when(block == flag)
                def _(m=m, i=i, at=at, dst=dst, flag=flag):
                    acc = acc_ref[...]
                    for lo in range(0, rows, HALO):
                        s = slice(lo, lo + HALO)
                        resid = u_ref[2 * planes * flag + at, s, :] - m[0, i, s, :]
                        weighted = m[1, i, s, :] * resid
                        dst[at, s, :] = weighted
                        if 0 < lo < rows - HALO:
                            acc = acc + weighted * resid
                    acc_ref[...] = acc

    total_ref[0, 0] = jnp.sum(acc_ref[...])


def pack_block(me, g_first, l_first, grad, lam, outs):
    y, _, c = bits(me)
    planes, rows = outs[0].shape[1], outs[0].shape[2]
    for r1, out in enumerate(outs):
        for i in range(planes):
            ahead = planes * (y ^ r1) + i
            at = jnp.where(c == 0, ahead, 2 * planes - 1 - ahead)

            def one(t, carry, out=out, i=i, at=at):
                r = pl.multiple_of(t * CHUNK, 8)
                out[0, i, pl.ds(r, CHUNK), :] = grad[g_first + at, pl.ds(r, CHUNK), :]
                out[1, i, pl.ds(r, CHUNK), :] = lam[l_first + at, pl.ds(r + HALO, CHUNK), :]
                return carry

            lax.fori_loop(0, rows // CHUNK, one, 0, unroll=True)


def backward_main(me_ref, part_ref, a_ref, b_ref, ra_ref, c_ref, slopes, o0, o1, lam_out, grad_out, saved, lam, mv0, mv1, grad):
    half, rows = a_ref.shape[0], a_ref.shape[1]
    clear_rims(mv0, rows)
    clear_rims(mv1, rows)
    for i in range(half):
        for src, at, t in ((b_ref, i, i), (a_ref, i, half + i), (ra_ref, half - 1 - i, 2 * half + i)):

            def fill(r, rh, src=src, at=at, t=t):
                v = src[at, r, :]
                lam[t, r, :] = v
                mv0[t, rh, :] = c_ref[t, r, :] * v

            copy_rows(rows, fill)
    first, last = edges((CHUNK, a_ref.shape[2]))
    first8, last8 = edges((HALO, a_ref.shape[2]))

    for j in range(ITERS):
        k = ITERS - 1 - j
        old, new = (mv0, mv1) if j % 2 == 0 else (mv1, mv0)

        def gain(t, r0, j=j, k=k):
            g = lam[t, r0 : r0 + CHUNK, :] * slopes[k, t, r0 : r0 + CHUNK, :]
            at = slice(r0 - HALO, r0 - HALO + CHUNK)
            grad[t, at, :] = grad[t, at, :] + g if j else g

        def gain_plane(t, carry, gain=gain):
            for r0 in range(HALO, rows - HALO, CHUNK):
                gain(t, r0)
            return carry

        def step(t, r0, n, f, l, j=j, old=old, new=new):
            change, _ = lap_rows(old, t, r0, n, f, l)
            after = lam[t, r0 : r0 + n, :] + change
            lam[t, r0 : r0 + n, :] = after
            if j < ITERS - 1:
                new[t, HALO + r0 : HALO + r0 + n, :] = c_ref[t, r0 : r0 + n, :] * after

        def own_plane(t, carry, gain=gain, step=step, j=j):
            for r0 in range(HALO, rows - HALO, CHUNK):
                gain(t, r0)
                step(t, r0, CHUNK, first, last)
            if j < ITERS - 1:
                step(t, 0, HALO, first8, last8)
                step(t, rows - HALO, HALO, first8, last8)
            return carry

        def halo_plane(t, carry, step=step):
            for r0 in range(0, rows, CHUNK):
                step(t, r0, CHUNK, first, last)
            return carry

        gain_plane(j, 0)
        spans(1 + j, 2 * half, own_plane)
        spans(2 * half, 2 * half + ITERS - 1 - j, halo_plane)
        if j < ITERS - 1:
            for i in range(2):

                def keep(r, rh, j=j, i=i, new=new):
                    saved[j, i, r, :] = new[j + 1 + i, rh, :]

                copy_rows(rows, keep)
    pack_block(me_ref[0], half, half, grad, lam, (o0, o1))
    for i in range(half):
        copy_rows(rows, lambda r, rh, i=i: lam_out.__setitem__((i, r), lam[i, r, :]))

        def one(t, carry, i=i):
            r = pl.multiple_of(t * CHUNK, 8)
            grad_out[i, pl.ds(r, CHUNK), :] = grad[i, pl.ds(r, CHUNK), :]
            return carry

        lax.fori_loop(0, (rows - 2 * HALO) // CHUNK, one, 0)


def backward_wedge(me_ref, b_ref, rb_ref, far_ref, c_ref, slopes, saved, lam_in, grad_in, o0, o1, lam, cw, mv0, mv1, grad):
    half, rows = b_ref.shape[0], b_ref.shape[1]
    clear_rims(mv0, rows)
    clear_rims(mv1, rows)
    for i in range(half):

        def fill(r, rh, i=i):
            v = rb_ref[half - 1 - i, r, :]
            coef = time_step * far_ref[1, half - 1 - i, r, :]
            lam[i, r, :] = v
            cw[i, r, :] = coef
            mv0[i, rh, :] = coef * v
            lam[half + i, r, :] = lam_in[i, r, :]

        copy_rows(rows, fill)
        if i < 2:
            copy_rows(rows, lambda r, rh, i=i: mv0.__setitem__((half + i, rh), c_ref[i, r, :] * b_ref[i, r, :]))

        def one(t, carry, i=i):
            r = pl.multiple_of(t * CHUNK, 8)
            grad[i, pl.ds(r, CHUNK), :] = grad_in[i, pl.ds(r, CHUNK), :]
            return carry

        lax.fori_loop(0, (rows - 2 * HALO) // CHUNK, one, 0)
    first, last = edges((CHUNK, b_ref.shape[2]))
    for j in range(ITERS):
        k = ITERS - 1 - j
        old, new = (mv0, mv1) if j % 2 == 0 else (mv1, mv0)
        if j:
            for i in range(2):
                copy_rows(rows, lambda r, rh, i=i: old.__setitem__((half + j + i, rh), saved[j - 1, i, r, :]))

        def plane(s, carry, own, j=j, k=k, old=old, new=new):
            if own:
                for r0 in range(HALO, rows - HALO, CHUNK):

                    @pl.when(s < half + j)
                    def _(r0=r0):
                        at = slice(r0 - HALO, r0 - HALO + CHUNK)
                        g = lam[s, r0 : r0 + CHUNK, :] * slopes[k, s - half, r0 : r0 + CHUNK, :]
                        grad[s - half, at, :] = grad[s - half, at, :] + g

            for r0 in range(0, rows, CHUNK):
                change, _ = lap_rows(old, s, r0, CHUNK, first, last)
                at = slice(r0, r0 + CHUNK)
                after = lam[s, at, :] + change
                lam[s, at, :] = after
                if j < ITERS - 1:
                    coef = c_ref[s - half, at, :] if own else cw[s, at, :]
                    new[s, HALO + r0 : HALO + r0 + CHUNK, :] = coef * after
            return carry

        spans(half - ITERS + 1 + j, half, lambda s, c: plane(s, c, False))
        spans(half, half + j + 1, lambda s, c: plane(s, c, True))
    pack_block(me_ref[0], 0, half, grad, lam, (o0, o1))


def home_kernel(me_ref, scale_ref, *refs):
    msgs, (g_ref, a_ref) = refs[:-2], refs[-2:]
    y, x, c = bits(me_ref[0])
    planes, rows = msgs[0].shape[1], msgs[0].shape[2]
    for flag in (0, 1):

        @pl.when(x ^ y == flag)
        def _(flag=flag):
            for (r1, r0), m in zip(ROUNDS, msgs[4 * flag : 4 * flag + 4]):
                start = part(c ^ r1, x ^ r0) * rows
                for k, out in enumerate((g_ref, a_ref)):
                    scale = scale_ref[k]
                    for i in range(planes):

                        def one(t, carry, m=m, k=k, i=i, out=out, start=start, scale=scale):
                            s = pl.multiple_of(t * CHUNK, 8)
                            out[i, pl.ds(pl.multiple_of(start + s, 8), CHUNK), :] = m[k, i, pl.ds(s, CHUNK), :] * scale
                            return carry

                        lax.fori_loop(0, rows // CHUNK, one, 0, unroll=True)


def shape(*dims):
    return pltpu.VMEM(dims, F32)


def exchange_sum(value, axis, count, steps):
    for step in steps:
        value = value + lax.ppermute(value, axis, [(i, i ^ step) for i in range(count)])
    return value


def on_device(coefficient, initial_field, observed, misfit_weight):
    axis = "gz"
    count = lax.axis_size(axis)
    planes, height, width = coefficient.shape
    if count % GROUP or height % (16 * PARTS) or 2 * planes < ITERS or ITERS * 2 > HALO:
        raise ValueError("unsupported sizes")
    rows = height // PARTS
    tall = rows + 2 * HALO
    half = 2 * planes
    me = lax.axis_index(axis).astype(jnp.int32).reshape(1)

    partner = [(i, i ^ 1) for i in range(count)]
    beyond = []
    for i in range(count - GROUP + 1):
        if i % 2:
            if i + GROUP - 1 < count:
                beyond += [(i, i + GROUP - 1), (i + GROUP - 1, i)]

    def regroup(a, b):
        msgs = call(pack_kernel, [shape(2, planes, tall, width)] * 4, [me], [a, b])
        got = []
        for m, r in zip(msgs, ROUNDS):
            got.append(lax.ppermute(m, axis, send_pairs(count, *r)))
        return outside(*got)

    first = regroup(initial_field, coefficient)
    second = regroup(observed, misfit_weight)

    plane_set = (tall, width)
    padded = (tall + 2 * HALO, width)
    saved_shape = shape(ITERS - 1, 2, *plane_set)
    blk_a, blk_b = call(place_kernel, [shape(2, half, *plane_set)] * 2, [me], first)
    far_b = lax.ppermute(blk_b, axis, beyond)
    far_a = lax.ppermute(blk_a, axis, partner)
    (far_a,), (far_b,) = outside(far_a), outside(far_b)
    final, coef, slopes, saved = call(
        forward_main,
        [shape(2 * half, *plane_set), shape(3 * half, *plane_set), shape(ITERS, 2 * half, *plane_set), saved_shape],
        [me],
        inside(blk_a, blk_b) + [far_a],
        [pltpu.VMEM((3 * half, *padded), F32)] * 2,
    )
    final, slopes = call(
        forward_wedge,
        [shape(2 * half, *plane_set), shape(ITERS, 2 * half, *plane_set)],
        [me],
        inside(blk_b) + [far_b] + inside(coef, saved, final, slopes),
        [pltpu.VMEM((half + ITERS + 2, *padded), F32)] * 2 + [pltpu.VMEM((half, *plane_set), F32)],
        input_output_aliases={5: 0, 6: 1},
    )

    lam_a, lam_b, part_total = call(
        resid_kernel,
        [shape(half, *plane_set)] * 2 + [jax.ShapeDtypeStruct((1, 1), F32)],
        [me],
        second + inside(final),
        [pltpu.VMEM((HALO, width), F32)],
        total=True,
    )
    far_lb = lax.ppermute(lam_b, axis, beyond)
    far_la = lax.ppermute(lam_a, axis, partner)
    (far_la,), (far_lb,) = outside(far_la), outside(far_lb)
    near = [2, 4]
    far = [1] + [1 << k for k in range(3, count.bit_length() - 1)]
    part_total = exchange_sum(part_total, axis, count, near)
    msg = [shape(2, planes, rows, width)] * 2
    *outs_a, lam_left, grad_left, saved = call(
        backward_main,
        msg + [shape(half, *plane_set), shape(half, rows, width), saved_shape],
        [me, part_total],
        inside(lam_a, lam_b) + [far_la] + inside(coef, slopes),
        [pltpu.VMEM((3 * half, *plane_set), F32)]
        + [pltpu.VMEM((3 * half, *padded), F32)] * 2
        + [pltpu.VMEM((2 * half, rows, width), F32)],
    )

    def send_home(outs, block):
        got = {}
        for r1, r0 in sorted(ROUNDS, key=lambda r: (-r[1], r[0])):
            pairs = [(j, i) for i, j in send_pairs(count, r1, r0) if (i >> 1 ^ i >> 2) & 1 == block]
            got[r1, r0] = lax.ppermute(outs[r1], axis, pairs)
        return outside(*[got[r] for r in ROUNDS])

    back_a = send_home(outs_a, 1)
    outs_b = call(
        backward_wedge,
        msg,
        [me],
        inside(lam_b) + [far_lb, far_b] + inside(coef, slopes, saved, lam_left, grad_left),
        [pltpu.VMEM((2 * half, *plane_set), F32), pltpu.VMEM((half, *plane_set), F32)]
        + [pltpu.VMEM((half + ITERS + 2, *padded), F32)] * 2
        + [pltpu.VMEM((half, rows, width), F32)],
    )
    back_b = send_home(outs_b, 0)

    if count & (count - 1):
        total = lax.psum(part_total, axis) / 4
    else:
        total = exchange_sum(part_total, axis, count, far)
    cells = count * planes * height * width
    misfit = jnp.sqrt(total[0, 0] / cells + 1e-06)
    inverse = 1.0 / misfit
    scale = jnp.stack([time_step * inverse, inverse])
    gradient, adjoint = call(
        home_kernel, [jax.ShapeDtypeStruct((planes, height, width), F32)] * 2, [me, scale], back_b + back_a
    )
    return gradient, adjoint, misfit


def solution(mesh):
    placed = P("gz", None, None)
    return jax.shard_map(
        on_device,
        mesh=mesh,
        in_specs=(placed,) * 4,
        out_specs=(placed, placed, P()),
        check_vma=False,
    )
```

time: 236 us -> 246 us (1.042)
  the two profiles are of different devices: /device:TPU:0 before, /device:TPU:18 now
where the time goes in v1:
time: 246 us
  waiting for transfers between devices  119 us (48%)
  starting transfers between devices  63 us (26%)
  Pallas kernels  48.7 us (20%)
  local copies, waits for them, and re-layouts  9.69 us (4%)
  between operations  5.82 us (2%)
    ppermute x8, waiting for transfers between devices, regroup(): got.append(lax.ppermute(m, axis, send_pairs(count, *r)))  69.5 us
    pallas_call x9, Pallas kernels, call(): pl.pallas_call(kernel, out_shape=outs, in_specs=[SM] * len(scalars) + [VM...  48.7 us
    ppermute x8, waiting for transfers between devices, send_home(): got[r1, r0] = lax.ppermute(outs[r1], axis, pairs)  33.8 us
    ppermute x8, starting transfers between devices, send_home(): got[r1, r0] = lax.ppermute(outs[r1], axis, pairs)  33.7 us
    ppermute x8, starting transfers between devices, regroup(): got.append(lax.ppermute(m, axis, send_pairs(count, *r)))  12.9 us
    ppermute x1, waiting for transfers between devices, on_device(): far_b = lax.ppermute(blk_b, axis, beyond)  9.9 us
    unnamed x36, local copies, waits for them, and re-layouts  9.69 us
    ppermute x5, starting transfers between devices, exchange_sum(): lax.ppermute(value, axis, [(i, i ^ step) for i in range(count)])  9.57 us
  transfers between devices with their start and end apart: 25, of which 9 were waited for; matrix products, arithmetic and copies ran while one was open for 0% of the time, Pallas kernels for 11%

profile of v1, /device:TPU:18, one launch (start us, length us, event | category | flops | bytes accessed | tf_op | source)
XLA Modules:
  0.0 245.9 jit_solution(313332281051695741)
XLA Ops:
  5.5 3.9 %collective-permute-start.6 = (f32[2,2,144,512]{3,2,1,0:T(8,128)S(1)}, f32[2,2,144,512]{3,2,1,0:T(8,128)S(1)}, u32[]{:S(2)}, u32[]{:S(2)}) collective-permute-start(f32[2,2,144,512]{3,2,1,0:T(8,128)S(1)} %get-tuple-element.37), channel_id=1, source_target_pairs={{0,4},{1,0},{2,6},{3,2},{4,5},{5,1},{6,7},{7,3},{8,12},{9,8},{10,1... | collective-permute-start | bytes 3538952 | tf_op jit(solution)/shard_map/ppermute | solution.py:462
  10.3 21.9 %collective-permute-done.5.m1 = f32[2,2,144,512]{3,2,1,0:T(8,128)S(1)} collective-permute-done((f32[2,2,144,512]{3,2,1,0:T(8,128)S(1)}, f32[2,2,144,512]{3,2,1,0:T(8,128)S(1)}, u32[]{:S(2)}, u32[]{:S(2)}) %collective-permute-start.5) | collective-permute-done | bytes 1179680 | tf_op jit(solution)/shard_map/ppermute | solution.py:462
  32.2 26.4 %collective-permute-done.6.m2 = f32[2,2,144,512]{3,2,1,0:T(8,128)S(1)} collective-permute-done((f32[2,2,144,512]{3,2,1,0:T(8,128)S(1)}, f32[2,2,144,512]{3,2,1,0:T(8,128)S(1)}, u32[]{:S(2)}, u32[]{:S(2)}) %collective-permute-start.6) | collective-permute-done | bytes 1179680 | tf_op jit(solution)/shard_map/ppermute | solution.py:462
  60.7 3.5 %shard_map.69 = (f32[2,4,144,512]{3,2,1,0:T(8,128)S(1)}, f32[2,4,144,512]{3,2,1,0:T(8,128)S(1)}) custom-call(s32[1]{0:T(128)} %bitcast.me_ref, f32[2,2,144,512]{3,2,1,0:T(8,128)} %copy-done.11, f32[2,2,144,512]{3,2,1,0:T(8,128)} %copy-done.12, f32[2,2,144,512]{3,2,1,0:T(8,128)} %copy-done.13, f32[2,2,144,512]{3,2,1,0:T(8,128)} %copy-done.14), custom_call_target="tpu_custom_call" | custom-call | tf_op jit(solution)/shard_map/pallas_call | solution.py:25
  65.1 2.0 collective-permute-start.8
  68.8 4.5 %collective-permute-start.2 = (f32[2,2,144,512]{3,2,1,0:T(8,128)S(1)}, f32[2,2,144,512]{3,2,1,0:T(8,128)S(1)}, u32[]{:S(2)}, u32[]{:S(2)}) collective-permute-start(f32[2,2,144,512]{3,2,1,0:T(8,128)S(1)} %get-tuple-element.33), channel_id=1, source_target_pairs={{0,4},{1,0},{2,6},{3,2},{4,5},{5,1},{6,7},{7,3},{8,12},{9,8},{10,1... | collective-permute-start | bytes 3538952 | tf_op jit(solution)/shard_map/ppermute | solution.py:462
  75.6 9.8 %shard_map.70 = (f32[8,144,512]{2,1,0:T(8,128)S(1)}, f32[12,144,512]{2,1,0:T(8,128)S(1)}, f32[4,8,144,512]{3,2,1,0:T(8,128)S(1)}, f32[3,2,144,512]{3,2,1,0:T(8,128)S(1)}) custom-call(s32[1]{0:T(128)} %bitcast.me_ref, f32[2,4,144,512]{3,2,1,0:T(8,128)S(1)} %get-tuple-element.40.a_ref, f32[2,4,144,512]{3,2,1,0:T(8,128)S(1)} %get-tuple-element.39.b_ref, ...), custom_call_target="tpu_custom_call" | custom-call | tf_op jit(solution)/shard_map/pallas_call | solution.py:25
  85.5 9.9 %collective-permute-done.8.rb_ref.far_ref = f32[2,4,144,512]{3,2,1,0:T(8,128)} collective-permute-done((f32[2,4,144,512]{3,2,1,0:T(8,128)S(1)}, f32[2,4,144,512]{3,2,1,0:T(8,128)}, u32[]{:S(2)}, u32[]{:S(2)}) %collective-permute-start.8) | collective-permute-done | bytes 2359328 | tf_op jit(solution)/shard_map/ppermute | solution.py:472
  95.4 6.4 %shard_map.71 = (f32[8,144,512]{2,1,0:T(8,128)S(1)}, f32[4,8,144,512]{3,2,1,0:T(8,128)S(1)}) custom-call(s32[1]{0:T(128)} %bitcast.me_ref, f32[2,4,144,512]{3,2,1,0:T(8,128)S(1)} %get-tuple-element.39.b_ref, f32[2,4,144,512]{3,2,1,0:T(8,128)} %collective-permute-done.8.rb_ref.far_ref, ...), custom_call_target="tpu_custom_call", output_to_operand_aliasing={{0}: (5, {}), {1}: (6, {})} | custom-call | tf_op jit(solution)/shard_map/pallas_call | solution.py:25
  101.8 20.7 %collective-permute-done.2.m2 = f32[2,2,144,512]{3,2,1,0:T(8,128)S(1)} collective-permute-done((f32[2,2,144,512]{3,2,1,0:T(8,128)S(1)}, f32[2,2,144,512]{3,2,1,0:T(8,128)S(1)}, u32[]{:S(2)}, u32[]{:S(2)}) %collective-permute-start.2) | collective-permute-done | bytes 1179680 | tf_op jit(solution)/shard_map/ppermute | solution.py:462
  124.0 3.6 %shard_map.72 = (f32[4,144,512]{2,1,0:T(8,128)S(1)}, f32[4,144,512]{2,1,0:T(8,128)S(1)}, f32[1,1]{1,0:T(1,128)}) custom-call(s32[1]{0:T(128)} %bitcast.me_ref, f32[2,2,144,512]{3,2,1,0:T(8,128)} %copy-done.7, f32[2,2,144,512]{3,2,1,0:T(8,128)} %copy-done.8, f32[2,2,144,512]{3,2,1,0:T(8,128)} %copy-done.9, f32[2,2,144,512]{3,2,1,0:T(8,128)} %copy-done.10, ...), custom_call_target="tpu_custom_call" | custom-call | tf_op jit(solution)/shard_map/pallas_call | solution.py:25
  127.5 2.0 collective-permute-start.16
  129.5 2.0 collective-permute-start.15
  132.2 3.2 %collective-permute-done.10 = f32[1,1]{1,0:T(1,128)} collective-permute-done((f32[1,1]{1,0:T(1,128)}, f32[1,1]{1,0:T(1,128)}, u32[]{:S(2)}, u32[]{:S(2)}) %collective-permute-start.10) | collective-permute-done | bytes 36 | tf_op jit(solution)/shard_map/ppermute | solution.py:436
  136.6 2.4 collective-permute-start.11
  141.9 10.6 %shard_map.73 = (f32[2,2,128,512]{3,2,1,0:T(8,128)S(1)}, f32[2,2,128,512]{3,2,1,0:T(8,128)S(1)}, f32[4,144,512]{2,1,0:T(8,128)S(1)}, f32[4,128,512]{2,1,0:T(8,128)S(1)}, f32[3,2,144,512]{3,2,1,0:T(8,128)S(1)}) custom-call(s32[1]{0:T(128)} %bitcast.me_ref, f32[1,1]{1,0:T(1,128)} %add.20.part_ref, f32[4,144,512]{2,1,0:T(8,128)S(1)} %get-tuple-element.49.a_ref, ...), custom_call_target="tpu_custom_call" | custom-call | tf_op jit(solution)/shard_map/pallas_call | solution.py:25
  153.6 8.5 %shard_map.74 = (f32[2,2,128,512]{3,2,1,0:T(8,128)S(1)}, f32[2,2,128,512]{3,2,1,0:T(8,128)}) custom-call(s32[1]{0:T(128)} %bitcast.me_ref, f32[4,144,512]{2,1,0:T(8,128)S(1)} %get-tuple-element.47.b_ref, f32[4,144,512]{2,1,0:T(8,128)} %copy-done.5, f32[2,4,144,512]{3,2,1,0:T(8,128)} %collective-permute-done.8.rb_ref.far_ref, ...), custom_call_target="tpu_custom_call" | custom-call | tf_op jit(solution)/shard_map/pallas_call | solution.py:25
  162.8 2.6 %collective-permute-start.18 = (f32[2,2,128,512]{3,2,1,0:T(8,128)S(1)}, f32[2,2,128,512]{3,2,1,0:T(8,128)S(1)}, u32[]{:S(2)}, u32[]{:S(2)}) collective-permute-start(f32[2,2,128,512]{3,2,1,0:T(8,128)S(1)} %get-tuple-element.53), channel_id=1, source_target_pairs={{2,0},{6,1},{1,6},{5,7},{10,8},{14,9},{9,14},{13,15},{18,16},{22,1... | collective-permute-start | bytes 3145736 | tf_op jit(solution)/shard_map/ppermute | solution.py:520
  166.1 2.2 collective-permute-start.12
  168.9 2.9 %collective-permute-start.13 = (f32[1,1]{1,0:T(1,128)}, f32[1,1]{1,0:T(1,128)}, u32[]{:S(2)}, u32[]{:S(2)}) collective-permute-start(f32[1,1]{1,0:T(1,128)} %add.21), channel_id=1, source_target_pairs={{0,8},{1,9},{2,10},{3,11},{4,12},{5,13},{6,14},{7,15},{8,0},{9,1},... | collective-permute-start | bytes 20 | tf_op jit(solution)/shard_map/ppermute | solution.py:436
  174.7 5.4 %collective-permute-start.20 = (f32[2,2,128,512]{3,2,1,0:T(8,128)}, f32[2,2,128,512]{3,2,1,0:T(8,128)}, u32[]{:S(2)}, u32[]{:S(2)}) collective-permute-start(f32[2,2,128,512]{3,2,1,0:T(8,128)} %get-tuple-element.54), channel_id=1, source_target_pairs={{6,0},{2,1},{5,6},{1,7},{14,8},{10,9},{13,14},{9,15},{22,16},{18,1... | collective-permute-start | bytes 3145736 | tf_op jit(solution)/shard_map/ppermute | solution.py:520
  183.1 20.1 %collective-permute-start.23 = (f32[2,2,128,512]{3,2,1,0:T(8,128)S(1)}, f32[2,2,128,512]{3,2,1,0:T(8,128)}, u32[]{:S(2)}, u32[]{:S(2)}) collective-permute-start(f32[2,2,128,512]{3,2,1,0:T(8,128)S(1)} %get-tuple-element.56), channel_id=1, source_target_pairs={{6,2},{2,3},{5,4},{1,5},{14,10},{10,11},{13,12},{9,13},{22,18},{18... | collective-permute-start | bytes 3145736 | tf_op jit(solution)/shard_map/ppermute | solution.py:520
  205.3 33.8 %collective-permute-done.23.refs_6_ = f32[2,2,128,512]{3,2,1,0:T(8,128)} collective-permute-done((f32[2,2,128,512]{3,2,1,0:T(8,128)S(1)}, f32[2,2,128,512]{3,2,1,0:T(8,128)}, u32[]{:S(2)}, u32[]{:S(2)}) %collective-permute-start.23) | collective-permute-done | bytes 1048608 | tf_op jit(solution)/shard_map/ppermute | solution.py:520
  239.0 5.7 %shard_map.75 = (f32[2,512,512]{2,1,0:T(8,128)}, f32[2,512,512]{2,1,0:T(8,128)}) custom-call(s32[1]{0:T(128)} %bitcast.me_ref, f32[2]{0:T(128)S(1)} %pad_maximum_fusion.scale_ref, f32[2,2,128,512]{3,2,1,0:T(8,128)} %copy-done.15, f32[2,2,128,512]{3,2,1,0:T(8,128)} %copy-done.16, f32[2,2,128,512]{3,2,1,0:T(8,128)} %copy-done.17, ...), custom_call_target="tpu_custom_call" | custom-call | tf_op jit(solution)/shard_map/pallas_call | solution.py:25
  (72 shorter events, 26.3 us)
Async XLA Ops:
  4.1 6.2 %collective-permute-start.4 = (f32[2,2,144,512]{3,2,1,0:T(8,128)S(1)}, f32[2,2,144,512]{3,2,1,0:T(8,128)S(1)}, u32[]{:S(2)}, u32[]{:S(2)}) collective-permute-start(f32[2,2,144,512]{3,2,1,0:T(8,128)S(1)} %get-tuple-element.35), channel_id=1, source_target_pairs={{0,0},{1,4},{2,2},{3,6},{4,1},{5,5},{6,3},{7,7},{8,8},{9,12},{10,1... | collective-permute-start | bytes 3538952 | tf_op jit(solution)/shard_map/ppermute | solution.py:462
  4.9 27.3 %collective-permute-start.5 = (f32[2,2,144,512]{3,2,1,0:T(8,128)S(1)}, f32[2,2,144,512]{3,2,1,0:T(8,128)S(1)}, u32[]{:S(2)}, u32[]{:S(2)}) collective-permute-start(f32[2,2,144,512]{3,2,1,0:T(8,128)S(1)} %get-tuple-element.36), channel_id=1, source_target_pairs={{0,2},{1,6},{2,0},{3,4},{4,3},{5,7},{6,1},{7,5},{8,10},{9,14},{10,... | collective-permute-start | bytes 3538952 | tf_op jit(solution)/shard_map/ppermute | solution.py:462
  5.5 53.1 %collective-permute-start.6 = (f32[2,2,144,512]{3,2,1,0:T(8,128)S(1)}, f32[2,2,144,512]{3,2,1,0:T(8,128)S(1)}, u32[]{:S(2)}, u32[]{:S(2)}) collective-permute-start(f32[2,2,144,512]{3,2,1,0:T(8,128)S(1)} %get-tuple-element.37), channel_id=1, source_target_pairs={{0,4},{1,0},{2,6},{3,2},{4,5},{5,1},{6,7},{7,3},{8,12},{9,8},{10,1... | collective-permute-start | bytes 3538952 | tf_op jit(solution)/shard_map/ppermute | solution.py:462
  9.4 49.8 %collective-permute-start.7 = (f32[2,2,144,512]{3,2,1,0:T(8,128)S(1)}, f32[2,2,144,512]{3,2,1,0:T(8,128)S(1)}, u32[]{:S(2)}, u32[]{:S(2)}) collective-permute-start(f32[2,2,144,512]{3,2,1,0:T(8,128)S(1)} %get-tuple-element.38), channel_id=1, source_target_pairs={{0,6},{1,2},{2,4},{3,0},{4,7},{5,3},{6,5},{7,1},{8,14},{9,10},{10,... | collective-permute-start | bytes 3538952 | tf_op jit(solution)/shard_map/ppermute | solution.py:462
  64.2 9.1 %collective-permute-start.9 = (f32[2,4,144,512]{3,2,1,0:T(8,128)S(1)}, f32[2,4,144,512]{3,2,1,0:T(8,128)S(1)}, u32[]{:S(2)}, u32[]{:S(2)}) collective-permute-start(f32[2,4,144,512]{3,2,1,0:T(8,128)S(1)} %get-tuple-element.40.a_ref), channel_id=1, source_target_pairs={{0,1},{1,0},{2,3},{3,2},{4,5},{5,4},{6,7},{7,6},{8,9},{9,8},{10,11... | collective-permute-start | bytes 7077896 | tf_op jit(solution)/shard_map/ppermute | solution.py:473
  65.1 30.3 %collective-permute-start.8 = (f32[2,4,144,512]{3,2,1,0:T(8,128)S(1)}, f32[2,4,144,512]{3,2,1,0:T(8,128)}, u32[]{:S(2)}, u32[]{:S(2)}) collective-permute-start(f32[2,4,144,512]{3,2,1,0:T(8,128)S(1)} %get-tuple-element.39.b_ref), channel_id=1, source_target_pairs={{1,8},{8,1},{3,10},{10,3},{5,12},{12,5},{7,14},{14,7},{9,16},{16,9... | collective-permute-start | bytes 7077896 | tf_op jit(solution)/shard_map/ppermute | solution.py:472
  67.5 34.3 %collective-permute-start = (f32[2,2,144,512]{3,2,1,0:T(8,128)S(1)}, f32[2,2,144,512]{3,2,1,0:T(8,128)S(1)}, u32[]{:S(2)}, u32[]{:S(2)}) collective-permute-start(f32[2,2,144,512]{3,2,1,0:T(8,128)S(1)} %get-tuple-element.31), channel_id=1, source_target_pairs={{0,0},{1,4},{2,2},{3,6},{4,1},{5,5},{6,3},{7,7},{8,8},{9,12},{10,1... | collective-permute-start | bytes 3538952 | tf_op jit(solution)/shard_map/ppermute | solution.py:462
  68.2 33.6 %collective-permute-start.1 = (f32[2,2,144,512]{3,2,1,0:T(8,128)S(1)}, f32[2,2,144,512]{3,2,1,0:T(8,128)S(1)}, u32[]{:S(2)}, u32[]{:S(2)}) collective-permute-start(f32[2,2,144,512]{3,2,1,0:T(8,128)S(1)} %get-tuple-element.32), channel_id=1, source_target_pairs={{0,2},{1,6},{2,0},{3,4},{4,3},{5,7},{6,1},{7,5},{8,10},{9,14},{10,... | collective-permute-start | bytes 3538952 | tf_op jit(solution)/shard_map/ppermute | solution.py:462
  68.8 53.7 %collective-permute-start.2 = (f32[2,2,144,512]{3,2,1,0:T(8,128)S(1)}, f32[2,2,144,512]{3,2,1,0:T(8,128)S(1)}, u32[]{:S(2)}, u32[]{:S(2)}) collective-permute-start(f32[2,2,144,512]{3,2,1,0:T(8,128)S(1)} %get-tuple-element.33), channel_id=1, source_target_pairs={{0,4},{1,0},{2,6},{3,2},{4,5},{5,1},{6,7},{7,3},{8,12},{9,8},{10,1... | collective-permute-start | bytes 3538952 | tf_op jit(solution)/shard_map/ppermute | solution.py:462
  74.7 47.8 %collective-permute-start.3 = (f32[2,2,144,512]{3,2,1,0:T(8,128)S(1)}, f32[2,2,144,512]{3,2,1,0:T(8,128)S(1)}, u32[]{:S(2)}, u32[]{:S(2)}) collective-permute-start(f32[2,2,144,512]{3,2,1,0:T(8,128)S(1)} %get-tuple-element.34), channel_id=1, source_target_pairs={{0,6},{1,2},{2,4},{3,0},{4,7},{5,3},{6,5},{7,1},{8,14},{9,10},{10,... | collective-permute-start | bytes 3538952 | tf_op jit(solution)/shard_map/ppermute | solution.py:462
  127.5 13.3 %collective-permute-start.16 = (f32[4,144,512]{2,1,0:T(8,128)S(1)}, f32[4,144,512]{2,1,0:T(8,128)S(1)}, u32[]{:S(2)}, u32[]{:S(2)}) collective-permute-start(f32[4,144,512]{2,1,0:T(8,128)S(1)} %get-tuple-element.49.a_ref), channel_id=1, source_target_pairs={{0,1},{1,0},{2,3},{3,2},{4,5},{5,4},{6,7},{7,6},{8,9},{9,8},{10,11... | collective-permute-start | bytes 3538952 | tf_op jit(solution)/shard_map/ppermute | solution.py:500
  129.5 23.0 %collective-permute-start.15 = (f32[4,144,512]{2,1,0:T(8,128)S(1)}, f32[4,144,512]{2,1,0:T(8,128)S(1)}, u32[]{:S(2)}, u32[]{:S(2)}) collective-permute-start(f32[4,144,512]{2,1,0:T(8,128)S(1)} %get-tuple-element.47.b_ref), channel_id=1, source_target_pairs={{1,8},{8,1},{3,10},{10,3},{5,12},{12,5},{7,14},{14,7},{9,16},{16,9... | collective-permute-start | bytes 3538952 | tf_op jit(solution)/shard_map/ppermute | solution.py:499
  131.5 3.9 %collective-permute-start.10 = (f32[1,1]{1,0:T(1,128)}, f32[1,1]{1,0:T(1,128)}, u32[]{:S(2)}, u32[]{:S(2)}) collective-permute-start(f32[1,1]{1,0:T(1,128)} %get-tuple-element.46), channel_id=1, source_target_pairs={{0,2},{1,3},{2,0},{3,1},{4,6},{5,7},{6,4},{7,5},{8,10},{9,11},{10,... | collective-permute-start | bytes 20 | tf_op jit(solution)/shard_map/ppermute | solution.py:436
  136.6 3.7 %collective-permute-start.11 = (f32[1,1]{1,0:T(1,128)}, f32[1,1]{1,0:T(1,128)}, u32[]{:S(2)}, u32[]{:S(2)}) collective-permute-start(f32[1,1]{1,0:T(1,128)} %add.19), channel_id=1, source_target_pairs={{0,4},{1,5},{2,6},{3,7},{4,0},{5,1},{6,2},{7,3},{8,12},{9,13},{10,... | collective-permute-start | bytes 20 | tf_op jit(solution)/shard_map/ppermute | solution.py:436
  162.0 19.7 %collective-permute-start.17 = (f32[2,2,128,512]{3,2,1,0:T(8,128)S(1)}, f32[2,2,128,512]{3,2,1,0:T(8,128)S(1)}, u32[]{:S(2)}, u32[]{:S(2)}) collective-permute-start(f32[2,2,128,512]{3,2,1,0:T(8,128)S(1)} %get-tuple-element.53), channel_id=1, source_target_pairs={{0,0},{4,1},{3,6},{7,7},{8,8},{12,9},{11,14},{15,15},{16,16},{20,1... | collective-permute-start | bytes 3145736 | tf_op jit(solution)/shard_map/ppermute | solution.py:520
  162.8 20.3 %collective-permute-start.18 = (f32[2,2,128,512]{3,2,1,0:T(8,128)S(1)}, f32[2,2,128,512]{3,2,1,0:T(8,128)S(1)}, u32[]{:S(2)}, u32[]{:S(2)}) collective-permute-start(f32[2,2,128,512]{3,2,1,0:T(8,128)S(1)} %get-tuple-element.53), channel_id=1, source_target_pairs={{2,0},{6,1},{1,6},{5,7},{10,8},{14,9},{9,14},{13,15},{18,16},{22,1... | collective-permute-start | bytes 3145736 | tf_op jit(solution)/shard_map/ppermute | solution.py:520
  165.3 37.8 %collective-permute-start.19 = (f32[2,2,128,512]{3,2,1,0:T(8,128)}, f32[2,2,128,512]{3,2,1,0:T(8,128)S(1)}, u32[]{:S(2)}, u32[]{:S(2)}) collective-permute-start(f32[2,2,128,512]{3,2,1,0:T(8,128)} %get-tuple-element.54), channel_id=1, source_target_pairs={{4,0},{0,1},{7,6},{3,7},{12,8},{8,9},{15,14},{11,15},{20,16},{16,1... | collective-permute-start | bytes 3145736 | tf_op jit(solution)/shard_map/ppermute | solution.py:520
  168.9 3.7 %collective-permute-start.13 = (f32[1,1]{1,0:T(1,128)}, f32[1,1]{1,0:T(1,128)}, u32[]{:S(2)}, u32[]{:S(2)}) collective-permute-start(f32[1,1]{1,0:T(1,128)} %add.21), channel_id=1, source_target_pairs={{0,8},{1,9},{2,10},{3,11},{4,12},{5,13},{6,14},{7,15},{8,0},{9,1},... | collective-permute-start | bytes 20 | tf_op jit(solution)/shard_map/ppermute | solution.py:436
  173.3 6.8 %collective-permute-start.14 = (f32[1,1]{1,0:T(1,128)}, f32[1,1]{1,0:T(1,128)}, u32[]{:S(2)}, u32[]{:S(2)}) collective-permute-start(f32[1,1]{1,0:T(1,128)} %add.22), channel_id=1, source_target_pairs={{0,16},{1,17},{2,18},{3,19},{4,20},{5,21},{6,22},{7,23},{8,24},{9,... | collective-permute-start | bytes 20 | tf_op jit(solution)/shard_map/ppermute | solution.py:436
  174.7 30.6 %collective-permute-start.20 = (f32[2,2,128,512]{3,2,1,0:T(8,128)}, f32[2,2,128,512]{3,2,1,0:T(8,128)}, u32[]{:S(2)}, u32[]{:S(2)}) collective-permute-start(f32[2,2,128,512]{3,2,1,0:T(8,128)} %get-tuple-element.54), channel_id=1, source_target_pairs={{6,0},{2,1},{5,6},{1,7},{14,8},{10,9},{13,14},{9,15},{22,16},{18,1... | collective-permute-start | bytes 3145736 | tf_op jit(solution)/shard_map/ppermute | solution.py:520
  180.1 25.2 %collective-permute-start.21 = (f32[2,2,128,512]{3,2,1,0:T(8,128)S(1)}, f32[2,2,128,512]{3,2,1,0:T(8,128)}, u32[]{:S(2)}, u32[]{:S(2)}) collective-permute-start(f32[2,2,128,512]{3,2,1,0:T(8,128)S(1)} %get-tuple-element.55), channel_id=1, source_target_pairs={{2,2},{6,3},{1,4},{5,5},{10,10},{14,11},{9,12},{13,13},{18,18},{22... | collective-permute-start | bytes 3145736 | tf_op jit(solution)/shard_map/ppermute | solution.py:520
  181.7 23.5 %collective-permute-start.22 = (f32[2,2,128,512]{3,2,1,0:T(8,128)S(1)}, f32[2,2,128,512]{3,2,1,0:T(8,128)}, u32[]{:S(2)}, u32[]{:S(2)}) collective-permute-start(f32[2,2,128,512]{3,2,1,0:T(8,128)S(1)} %get-tuple-element.55), channel_id=1, source_target_pairs={{0,2},{4,3},{3,4},{7,5},{8,10},{12,11},{11,12},{15,13},{16,18},{20... | collective-permute-start | bytes 3145736 | tf_op jit(solution)/shard_map/ppermute | solution.py:520
  183.1 56.0 %collective-permute-start.23 = (f32[2,2,128,512]{3,2,1,0:T(8,128)S(1)}, f32[2,2,128,512]{3,2,1,0:T(8,128)}, u32[]{:S(2)}, u32[]{:S(2)}) collective-permute-start(f32[2,2,128,512]{3,2,1,0:T(8,128)S(1)} %get-tuple-element.56), channel_id=1, source_target_pairs={{6,2},{2,3},{5,4},{1,5},{14,10},{10,11},{13,12},{9,13},{22,18},{18... | collective-permute-start | bytes 3145736 | tf_op jit(solution)/shard_map/ppermute | solution.py:520
  203.2 35.9 %collective-permute-start.24 = (f32[2,2,128,512]{3,2,1,0:T(8,128)S(1)}, f32[2,2,128,512]{3,2,1,0:T(8,128)}, u32[]{:S(2)}, u32[]{:S(2)}) collective-permute-start(f32[2,2,128,512]{3,2,1,0:T(8,128)S(1)} %get-tuple-element.56), channel_id=1, source_target_pairs={{4,2},{0,3},{7,4},{3,5},{12,10},{8,11},{15,12},{11,13},{20,18},{16... | collective-permute-start | bytes 3145736 | tf_op jit(solution)/shard_map/ppermute | solution.py:520
  (19 other events, 224.1 us)

commit v2 on v1

--- a/solution.py
+++ b/solution.py
@@ -12,12 +12,12 @@
 GROUP = 8
 PARTS = 4
 HALO = 8
-ROUNDS = ((0, 0), (0, 1), (1, 0), (1, 1))
+ROUNDS = ((0, 1), (0, 0), (1, 1), (1, 0))
 
 
 VM = pl.BlockSpec(memory_space=pltpu.VMEM)
 SM = pl.BlockSpec(memory_space=pltpu.SMEM)
-PARAMS = pltpu.CompilerParams(vmem_limit_bytes=32 * 1024 * 1024)
+PARAMS = pltpu.CompilerParams(vmem_limit_bytes=14 * 1024 * 1024)
 F32 = jnp.float32
 
 
@@ -55,14 +55,6 @@
         y, x, c = bits(i)
         pairs.append((i, (i & ~7) + 4 * (c ^ r1) + 2 * (x ^ r0) + y))
     return pairs
-
-
-def row_loop(rows, body, step=16):
-    def one(t, carry):
-        body(pl.ds(pl.multiple_of(t * step, 8), step))
-        return carry
-
-    lax.fori_loop(0, rows // step, one, 0)
 
 
 def pack_kernel(me_ref, a_ref, b_ref, *out_refs):
@@ -99,18 +91,37 @@
     return block, jnp.where(c == 0, ahead, 2 * planes - 1 - ahead)
 
 
-def place_kernel(me_ref, m0, m1, m2, m3, a_ref, b_ref):
+def early_kernel(me_ref, m0, m1, early_ref):
     me = me_ref[0]
-    planes, rows = m0.shape[1], m0.shape[2]
+    for r, m in zip(ROUNDS, (m0, m1)):
+        block, _ = slot(me, r, m.shape[1], 0)
+
+        @pl.when(block == 0)
+        def _(m=m):
+            early_ref[...] = m[...]
+
+
+def place_kernel(me_ref, m0, m1, m2, m3, late_ref, a_ref, b_ref):
+    me = me_ref[0]
+    planes = m0.shape[1]
     for r, m in zip(ROUNDS, (m0, m1, m2, m3)):
-        for i in range(planes):
-            block, at = slot(me, r, planes, i)
-            for flag, dst in ((1, a_ref), (0, b_ref)):
-
-                @pl.when(block == flag)
-                def _(dst=dst, m=m, i=i, at=at):
-                    for k in range(2):
-                        row_loop(rows, lambda s, k=k: dst.__setitem__((k, at, s), m[k, i, s]))
+        block, _ = slot(me, r, planes, 0)
+
+        @pl.when(block == 0)
+        def _(r=r, m=m):
+            if r[0]:
+                late_ref[...] = m[...]
+            for i in range(planes):
+                _, at = slot(me, r, planes, i)
+                for k in range(2):
+                    b_ref[k, at] = m[k, i]
+
+        @pl.when(block == 1)
+        def _(r=r, m=m):
+            for i in range(planes):
+                _, at = slot(me, r, planes, i)
+                for k in range(2):
+                    a_ref[k, at] = m[k, i]
 
 
 def edges(shape):
@@ -196,17 +207,22 @@
                 copy_rows(rows, keep)
 
 
-def forward_wedge(me_ref, b_ref, rb_ref, c_ref, saved, u_in, slopes_in, u_out, slopes, w0, w1, cw):
+def forward_wedge(me_ref, early, late, b_ref, c_ref, saved, u_in, slopes_in, u_out, slopes, cw, w0, w1):
+    y, _, c = bits(me_ref[0])
     half, rows = b_ref.shape[1], b_ref.shape[2]
+    planes = early.shape[1]
     clear_rims(w0, rows)
     clear_rims(w1, rows)
-    for i in range(half):
-
-        def fill(r, rh, i=i):
-            w0[i, rh, :] = rb_ref[0, half - 1 - i, r, :]
-            cw[i, r, :] = time_step * rb_ref[1, half - 1 - i, r, :]
-
-        copy_rows(rows, fill)
+    for r1, far in enumerate((early, late)):
+        for i in range(planes):
+            ahead = planes * (y ^ r1) + i
+            s = half - 1 - jnp.where(c == 1, ahead, half - 1 - ahead)
+
+            def fill(r, rh, far=far, i=i, s=s):
+                w0[s, rh, :] = far[0, i, r, :]
+                cw[s, r, :] = time_step * far[1, i, r, :]
+
+            copy_rows(rows, fill)
     for i in range(2):
         copy_rows(rows, lambda r, rh, i=i: w0.__setitem__((half + i, rh), b_ref[0, i, r, :]))
     first, last = edges((CHUNK, b_ref.shape[3]))
@@ -258,24 +274,7 @@
     total_ref[0, 0] = jnp.sum(acc_ref[...])
 
 
-def pack_block(me, g_first, l_first, grad, lam, outs):
-    y, _, c = bits(me)
-    planes, rows = outs[0].shape[1], outs[0].shape[2]
-    for r1, out in enumerate(outs):
-        for i in range(planes):
-            ahead = planes * (y ^ r1) + i
-            at = jnp.where(c == 0, ahead, 2 * planes - 1 - ahead)
-
-            def one(t, carry, out=out, i=i, at=at):
-                r = pl.multiple_of(t * CHUNK, 8)
-                out[0, i, pl.ds(r, CHUNK), :] = grad[g_first + at, pl.ds(r, CHUNK), :]
-                out[1, i, pl.ds(r, CHUNK), :] = lam[l_first + at, pl.ds(r + HALO, CHUNK), :]
-                return carry
-
-            lax.fori_loop(0, rows // CHUNK, one, 0, unroll=True)
-
-
-def backward_main(me_ref, part_ref, a_ref, b_ref, ra_ref, c_ref, slopes, o0, o1, lam_out, grad_out, saved, lam, mv0, mv1, grad):
+def backward_main(me_ref, ra_ref, a_ref, b_ref, c_ref, slopes, lam, grad, saved, mv0, mv1):
     half, rows = a_ref.shape[0], a_ref.shape[1]
     clear_rims(mv0, rows)
     clear_rims(mv1, rows)
@@ -336,19 +335,9 @@
                     saved[j, i, r, :] = new[j + 1 + i, rh, :]
 
                 copy_rows(rows, keep)
-    pack_block(me_ref[0], half, half, grad, lam, (o0, o1))
-    for i in range(half):
-        copy_rows(rows, lambda r, rh, i=i: lam_out.__setitem__((i, r), lam[i, r, :]))
-
-        def one(t, carry, i=i):
-            r = pl.multiple_of(t * CHUNK, 8)
-            grad_out[i, pl.ds(r, CHUNK), :] = grad[i, pl.ds(r, CHUNK), :]
-            return carry
-
-        lax.fori_loop(0, (rows - 2 * HALO) // CHUNK, one, 0)
-
-
-def backward_wedge(me_ref, b_ref, rb_ref, far_ref, c_ref, slopes, saved, lam_in, grad_in, o0, o1, lam, cw, mv0, mv1, grad):
+
+
+def backward_wedge(me_ref, rb_ref, b_ref, cw, c_ref, slopes, saved, lam_in, grad_in, o0, o1, o2, o3, lam, mv0, mv1, grad):
     half, rows = b_ref.shape[0], b_ref.shape[1]
     clear_rims(mv0, rows)
     clear_rims(mv1, rows)
@@ -356,10 +345,8 @@
 
         def fill(r, rh, i=i):
             v = rb_ref[half - 1 - i, r, :]
-            coef = time_step * far_ref[1, half - 1 - i, r, :]
             lam[i, r, :] = v
-            cw[i, r, :] = coef
-            mv0[i, rh, :] = coef * v
+            mv0[i, rh, :] = cw[i, r, :] * v
             lam[half + i, r, :] = lam_in[i, r, :]
 
         copy_rows(rows, fill)
@@ -380,51 +367,49 @@
             for i in range(2):
                 copy_rows(rows, lambda r, rh, i=i: old.__setitem__((half + j + i, rh), saved[j - 1, i, r, :]))
 
-        def plane(s, carry, own, j=j, k=k, old=old, new=new):
-            if own:
-                for r0 in range(HALO, rows - HALO, CHUNK):
-
-                    @pl.when(s < half + j)
-                    def _(r0=r0):
-                        at = slice(r0 - HALO, r0 - HALO + CHUNK)
-                        g = lam[s, r0 : r0 + CHUNK, :] * slopes[k, s - half, r0 : r0 + CHUNK, :]
-                        grad[s - half, at, :] = grad[s - half, at, :] + g
-
+        def plane(s, carry, own, j=j, old=old, new=new):
             for r0 in range(0, rows, CHUNK):
                 change, _ = lap_rows(old, s, r0, CHUNK, first, last)
                 at = slice(r0, r0 + CHUNK)
                 after = lam[s, at, :] + change
-                lam[s, at, :] = after
                 if j < ITERS - 1:
                     coef = c_ref[s - half, at, :] if own else cw[s, at, :]
                     new[s, HALO + r0 : HALO + r0 + CHUNK, :] = coef * after
-            return carry
-
+                lam[s, at, :] = after
+            return carry
+
+        def gain(s, carry, j=j, k=k):
+            for r0 in range(HALO, rows - HALO, CHUNK):
+                at = slice(r0 - HALO, r0 - HALO + CHUNK)
+                g = lam[s, r0 : r0 + CHUNK, :] * slopes[k, s - half, r0 : r0 + CHUNK, :]
+                grad[s - half, at, :] = grad[s - half, at, :] + g
+            return carry
+
+        spans(half, half + j, gain)
         spans(half - ITERS + 1 + j, half, lambda s, c: plane(s, c, False))
         spans(half, half + j + 1, lambda s, c: plane(s, c, True))
-    pack_block(me_ref[0], 0, half, grad, lam, (o0, o1))
-
-
-def home_kernel(me_ref, scale_ref, *refs):
-    msgs, (g_ref, a_ref) = refs[:-2], refs[-2:]
-    y, x, c = bits(me_ref[0])
-    planes, rows = msgs[0].shape[1], msgs[0].shape[2]
-    for flag in (0, 1):
-
-        @pl.when(x ^ y == flag)
-        def _(flag=flag):
-            for (r1, r0), m in zip(ROUNDS, msgs[4 * flag : 4 * flag + 4]):
-                start = part(c ^ r1, x ^ r0) * rows
-                for k, out in enumerate((g_ref, a_ref)):
-                    scale = scale_ref[k]
-                    for i in range(planes):
-
-                        def one(t, carry, m=m, k=k, i=i, out=out, start=start, scale=scale):
-                            s = pl.multiple_of(t * CHUNK, 8)
-                            out[i, pl.ds(pl.multiple_of(start + s, 8), CHUNK), :] = m[k, i, pl.ds(s, CHUNK), :] * scale
-                            return carry
-
-                        lax.fori_loop(0, rows // CHUNK, one, 0, unroll=True)
+    me = me_ref[0]
+    planes = half // 2
+    for r, out in zip(ROUNDS, (o0, o1, o2, o3)):
+        block, _ = slot(me, r, planes, 0)
+        for flag, g_src, l_src in ((0, grad, lam), (1, grad_in, lam_in)):
+
+            @pl.when(block == flag)
+            def _(r=r, out=out, g_src=g_src, l_src=l_src):
+                for i in range(planes):
+                    _, at = slot(me, r, planes, i)
+                    out[0, i] = g_src[at if g_src is grad else half + at]
+                    out[1, i] = l_src[half + at, HALO : rows - HALO, :]
+
+
+def home_kernel(me_ref, scale_ref, m0, m1, m2, m3, g_ref, a_ref):
+    _, x, c = bits(me_ref[0])
+    planes, rows = m0.shape[1], m0.shape[2]
+    for (r1, r0), m in zip(ROUNDS, (m0, m1, m2, m3)):
+        start = pl.multiple_of(part(c ^ r1, x ^ r0) * rows, 8)
+        for k, out in enumerate((g_ref, a_ref)):
+            for i in range(planes):
+                out[i, pl.ds(start, rows), :] = m[k, i] * scale_ref[k]
 
 
 def shape(*dims):
@@ -462,16 +447,19 @@
             got.append(lax.ppermute(m, axis, send_pairs(count, *r)))
         return outside(*got)
 
-    first = regroup(initial_field, coefficient)
-    second = regroup(observed, misfit_weight)
+    first = regroup(*outside(initial_field, coefficient))
+    second = regroup(*outside(observed, misfit_weight))
 
     plane_set = (tall, width)
     padded = (tall + 2 * HALO, width)
     saved_shape = shape(ITERS - 1, 2, *plane_set)
-    blk_a, blk_b = call(place_kernel, [shape(2, half, *plane_set)] * 2, [me], first)
-    far_b = lax.ppermute(blk_b, axis, beyond)
+    quarter = shape(2, planes, *plane_set)
+    (early,) = call(early_kernel, [quarter], [me], first[:2])
+    early = lax.ppermute(early, axis, beyond)
+    late, blk_a, blk_b = call(place_kernel, [quarter] + [shape(2, half, *plane_set)] * 2, [me], first)
+    late = lax.ppermute(late, axis, beyond)
     far_a = lax.ppermute(blk_a, axis, partner)
-    (far_a,), (far_b,) = outside(far_a), outside(far_b)
+    far_a, early, late = outside(far_a, early, late)
     final, coef, slopes, saved = call(
         forward_main,
         [shape(2 * half, *plane_set), shape(3 * half, *plane_set), shape(ITERS, 2 * half, *plane_set), saved_shape],
@@ -479,13 +467,13 @@
         inside(blk_a, blk_b) + [far_a],
         [pltpu.VMEM((3 * half, *padded), F32)] * 2,
     )
-    final, slopes = call(
+    final, slopes, far_coef = call(
         forward_wedge,
-        [shape(2 * half, *plane_set), shape(ITERS, 2 * half, *plane_set)],
+        [shape(2 * half, *plane_set), shape(ITERS, 2 * half, *plane_set), shape(half, *plane_set)],
         [me],
-        inside(blk_b) + [far_b] + inside(coef, saved, final, slopes),
-        [pltpu.VMEM((half + ITERS + 2, *padded), F32)] * 2 + [pltpu.VMEM((half, *plane_set), F32)],
-        input_output_aliases={5: 0, 6: 1},
+        [early, late] + inside(blk_b, coef, saved, final, slopes),
+        [pltpu.VMEM((half + ITERS + 2, *padded), F32)] * 2,
+        input_output_aliases={6: 0, 7: 1},
     )
 
     lam_a, lam_b, part_total = call(
@@ -499,38 +487,29 @@
     far_lb = lax.ppermute(lam_b, axis, beyond)
     far_la = lax.ppermute(lam_a, axis, partner)
     (far_la,), (far_lb,) = outside(far_la), outside(far_lb)
-    near = [2, 4]
     far = [1] + [1 << k for k in range(3, count.bit_length() - 1)]
-    part_total = exchange_sum(part_total, axis, count, near)
-    msg = [shape(2, planes, rows, width)] * 2
-    *outs_a, lam_left, grad_left, saved = call(
+    part_total = exchange_sum(part_total, axis, count, [2])
+    lam, grad, saved = call(
         backward_main,
-        msg + [shape(half, *plane_set), shape(half, rows, width), saved_shape],
-        [me, part_total],
-        inside(lam_a, lam_b) + [far_la] + inside(coef, slopes),
-        [pltpu.VMEM((3 * half, *plane_set), F32)]
-        + [pltpu.VMEM((3 * half, *padded), F32)] * 2
-        + [pltpu.VMEM((2 * half, rows, width), F32)],
+        [shape(3 * half, *plane_set), shape(2 * half, rows, width), saved_shape],
+        [me],
+        [far_la] + inside(lam_a, lam_b, coef, slopes),
+        [pltpu.VMEM((3 * half, *padded), F32)] * 2,
     )
-
-    def send_home(outs, block):
-        got = {}
-        for r1, r0 in sorted(ROUNDS, key=lambda r: (-r[1], r[0])):
-            pairs = [(j, i) for i, j in send_pairs(count, r1, r0) if (i >> 1 ^ i >> 2) & 1 == block]
-            got[r1, r0] = lax.ppermute(outs[r1], axis, pairs)
-        return outside(*[got[r] for r in ROUNDS])
-
-    back_a = send_home(outs_a, 1)
-    outs_b = call(
+    part_total = exchange_sum(part_total, axis, count, [4])
+    outs = call(
         backward_wedge,
-        msg,
+        [shape(2, planes, rows, width)] * 4,
         [me],
-        inside(lam_b) + [far_lb, far_b] + inside(coef, slopes, saved, lam_left, grad_left),
-        [pltpu.VMEM((2 * half, *plane_set), F32), pltpu.VMEM((half, *plane_set), F32)]
+        [far_lb] + inside(lam_b, far_coef, coef, slopes, saved, lam, grad),
+        [pltpu.VMEM((2 * half, *plane_set), F32)]
         + [pltpu.VMEM((half + ITERS + 2, *padded), F32)] * 2
         + [pltpu.VMEM((half, rows, width), F32)],
     )
-    back_b = send_home(outs_b, 0)
+    back = []
+    for m, r in zip(outs, ROUNDS):
+        back.append(lax.ppermute(m, axis, [(j, i) for i, j in send_pairs(count, *r)]))
+    back = outside(*back)
 
     if count & (count - 1):
         total = lax.psum(part_total, axis) / 4
@@ -540,9 +519,7 @@
     misfit = jnp.sqrt(total[0, 0] / cells + 1e-06)
     inverse = 1.0 / misfit
     scale = jnp.stack([time_step * inverse, inverse])
-    gradient, adjoint = call(
-        home_kernel, [jax.ShapeDtypeStruct((planes, height, width), F32)] * 2, [me, scale], back_b + back_a
-    )
+    gradient, adjoint = call(home_kernel, [jax.ShapeDtypeStruct((planes, height, width), F32)] * 2, [me, scale], back)
     return gradient, adjoint, misfit
 
 

time: 246 us -> 233 us (0.947)
  the two profiles are of different devices: /device:TPU:18 before, /device:TPU:0 now
where the time goes in v2:
time: 233 us; the launch traced here: 232 us
  waiting for transfers between devices  115 us (49%)
  starting transfers between devices  53.1 us (23%)
  Pallas kernels  52.1 us (22%)
  between operations  6.18 us (3%)
  local copies, waits for them, and re-layouts  5.32 us (2%)
    ppermute x8, waiting for transfers between devices, regroup(): got.append(lax.ppermute(m, axis, send_pairs(count, *r)))  75.4 us
    pallas_call x10, Pallas kernels, call(): pl.pallas_call(kernel, out_shape=outs, in_specs=[SM] * len(scalars) + [VM...  52.1 us
    ppermute x5, waiting for transfers between devices, exchange_sum(): lax.ppermute(value, axis, [(i, i ^ step) for i in range(count)])  38.2 us
    ppermute x8, starting transfers between devices, regroup(): got.append(lax.ppermute(m, axis, send_pairs(count, *r)))  20.6 us
    ppermute x5, starting transfers between devices, exchange_sum(): lax.ppermute(value, axis, [(i, i ^ step) for i in range(count)])  17.1 us
    ppermute x4, starting transfers between devices, on_device(): lax.ppermute(m, axis, [(j, i) for i, j in send_pairs(count, *r)])  8.41 us
    unnamed x26, local copies, waits for them, and re-layouts  5.32 us
  transfers between devices with their start and end apart: 22, of which 11 were waited for; matrix products, arithmetic and copies ran while one was open for 0% of the time, Pallas kernels for 13%

profile of v2, /device:TPU:0, one launch (start us, length us, event | category | flops | bytes accessed | tf_op | source)
XLA Modules:
  0.0 232.1 jit_solution(3212711046914637053)
XLA Ops:
  0.6 2.5 %shard_map.68 = (f32[2,2,144,512]{3,2,1,0:T(8,128)S(1)}, f32[2,2,144,512]{3,2,1,0:T(8,128)S(1)}, f32[2,2,144,512]{3,2,1,0:T(8,128)S(1)}, f32[2,2,144,512]{3,2,1,0:T(8,128)S(1)}) custom-call(s32[1]{0:T(128)} %bitcast.me_ref, f32[2,512,512]{2,1,0:T(8,128)} %a_ref.3, f32[2,512,512]{2,1,0:T(8,128)} %b_ref.3), custom_call_target="tpu_custom_call" | custom-call | tf_op jit(solution)/shard_map/pallas_call | solution.py:25
  3.2 3.0 %collective-permute-start.4 = (f32[2,2,144,512]{3,2,1,0:T(8,128)S(1)}, f32[2,2,144,512]{3,2,1,0:T(8,128)S(1)}, u32[]{:S(2)}, u32[]{:S(2)}) collective-permute-start(f32[2,2,144,512]{3,2,1,0:T(8,128)S(1)} %get-tuple-element.37), channel_id=1, source_target_pairs={{0,2},{1,6},{2,0},{3,4},{4,3},{5,7},{6,1},{7,5},{8,10},{9,14},{10,... | collective-permute-start | bytes 3538952 | tf_op jit(solution)/shard_map/ppermute | solution.py:447
  6.9 3.9 %collective-permute-start.7 = (f32[2,2,144,512]{3,2,1,0:T(8,128)S(1)}, f32[2,2,144,512]{3,2,1,0:T(8,128)S(1)}, u32[]{:S(2)}, u32[]{:S(2)}) collective-permute-start(f32[2,2,144,512]{3,2,1,0:T(8,128)S(1)} %get-tuple-element.39), channel_id=1, source_target_pairs={{0,6},{1,2},{2,4},{3,0},{4,7},{5,3},{6,5},{7,1},{8,14},{9,10},{10,... | collective-permute-start | bytes 3538952 | tf_op jit(solution)/shard_map/ppermute | solution.py:447
  10.9 21.3 %collective-permute-done.4.m0 = f32[2,2,144,512]{3,2,1,0:T(8,128)S(1)} collective-permute-done((f32[2,2,144,512]{3,2,1,0:T(8,128)S(1)}, f32[2,2,144,512]{3,2,1,0:T(8,128)S(1)}, u32[]{:S(2)}, u32[]{:S(2)}) %collective-permute-start.4) | collective-permute-done | bytes 1179680 | tf_op jit(solution)/shard_map/ppermute | solution.py:447
  32.2 26.2 %collective-permute-done.7.m2 = f32[2,2,144,512]{3,2,1,0:T(8,128)S(1)} collective-permute-done((f32[2,2,144,512]{3,2,1,0:T(8,128)S(1)}, f32[2,2,144,512]{3,2,1,0:T(8,128)S(1)}, u32[]{:S(2)}, u32[]{:S(2)}) %collective-permute-start.7) | collective-permute-done | bytes 1179680 | tf_op jit(solution)/shard_map/ppermute | solution.py:447
  60.4 2.7 %shard_map.70 = (f32[2,2,144,512]{3,2,1,0:T(8,128)S(1)}, f32[2,4,144,512]{3,2,1,0:T(8,128)S(1)}, f32[2,4,144,512]{3,2,1,0:T(8,128)S(1)}) custom-call(s32[1]{0:T(128)} %bitcast.me_ref, f32[2,2,144,512]{3,2,1,0:T(8,128)} %copy-done, f32[2,2,144,512]{3,2,1,0:T(8,128)} %copy-done.1, f32[2,2,144,512]{3,2,1,0:T(8,128)} %copy-done.10, f32[2,2,144,512]{3,2,1,0:T(8,128)} %copy-done.11), custom_call_target="tpu_custom_call" | custom-call | tf_op jit(solution)/shard_map/pallas_call | solution.py:25
  63.2 2.8 %collective-permute-start.10 = (f32[2,4,144,512]{3,2,1,0:T(8,128)S(1)}, f32[2,4,144,512]{3,2,1,0:T(8,128)S(1)}, u32[]{:S(2)}, u32[]{:S(2)}) collective-permute-start(f32[2,4,144,512]{3,2,1,0:T(8,128)S(1)} %get-tuple-element.43.a_ref), channel_id=1, source_target_pairs={{0,1},{1,0},{2,3},{3,2},{4,5},{5,4},{6,7},{7,6},{8,9},{9,8},{10,11... | collective-permute-start | bytes 7077896 | tf_op jit(solution)/shard_map/ppermute | solution.py:461
  66.7 2.6 %shard_map.67 = (f32[2,2,144,512]{3,2,1,0:T(8,128)S(1)}, f32[2,2,144,512]{3,2,1,0:T(8,128)S(1)}, f32[2,2,144,512]{3,2,1,0:T(8,128)S(1)}, f32[2,2,144,512]{3,2,1,0:T(8,128)S(1)}) custom-call(s32[1]{0:T(128)} %bitcast.me_ref, f32[2,512,512]{2,1,0:T(8,128)} %a_ref.2, f32[2,512,512]{2,1,0:T(8,128)} %b_ref.2), custom_call_target="tpu_custom_call" | custom-call | tf_op jit(solution)/shard_map/pallas_call | solution.py:25
  73.5 6.9 %collective-permute-start.2 = (f32[2,2,144,512]{3,2,1,0:T(8,128)S(1)}, f32[2,2,144,512]{3,2,1,0:T(8,128)S(1)}, u32[]{:S(2)}, u32[]{:S(2)}) collective-permute-start(f32[2,2,144,512]{3,2,1,0:T(8,128)S(1)} %get-tuple-element.35), channel_id=1, source_target_pairs={{0,6},{1,2},{2,4},{3,0},{4,7},{5,3},{6,5},{7,1},{8,14},{9,10},{10,... | collective-permute-start | bytes 3538952 | tf_op jit(solution)/shard_map/ppermute | solution.py:447
  80.4 4.2 %collective-permute-start.3 = (f32[2,2,144,512]{3,2,1,0:T(8,128)S(1)}, f32[2,2,144,512]{3,2,1,0:T(8,128)S(1)}, u32[]{:S(2)}, u32[]{:S(2)}) collective-permute-start(f32[2,2,144,512]{3,2,1,0:T(8,128)S(1)} %get-tuple-element.36), channel_id=1, source_target_pairs={{0,4},{1,0},{2,6},{3,2},{4,5},{5,1},{6,7},{7,3},{8,12},{9,8},{10,1... | collective-permute-start | bytes 3538952 | tf_op jit(solution)/shard_map/ppermute | solution.py:447
  84.6 9.8 %shard_map.71 = (f32[8,144,512]{2,1,0:T(8,128)S(1)}, f32[12,144,512]{2,1,0:T(8,128)S(1)}, f32[4,8,144,512]{3,2,1,0:T(8,128)S(1)}, f32[3,2,144,512]{3,2,1,0:T(8,128)S(1)}) custom-call(s32[1]{0:T(128)} %bitcast.me_ref, f32[2,4,144,512]{3,2,1,0:T(8,128)S(1)} %get-tuple-element.43.a_ref, f32[2,4,144,512]{3,2,1,0:T(8,128)S(1)} %get-tuple-element.42.b_ref, ...), custom_call_target="tpu_custom_call" | custom-call | tf_op jit(solution)/shard_map/pallas_call | solution.py:25
  95.4 6.4 %shard_map.72 = (f32[8,144,512]{2,1,0:T(8,128)S(1)}, f32[4,8,144,512]{3,2,1,0:T(8,128)S(1)}, f32[4,144,512]{2,1,0:T(8,128)S(1)}) custom-call(s32[1]{0:T(128)} %bitcast.me_ref, f32[2,2,144,512]{3,2,1,0:T(8,128)} %copy-done.4, f32[2,2,144,512]{3,2,1,0:T(8,128)} %copy-done.3, ...), custom_call_target="tpu_custom_call", output_to_operand_aliasing={{0}: (6, {}), {1}: (7, {})} | custom-call | tf_op jit(solution)/shard_map/pallas_call | solution.py:25
  101.9 24.0 %collective-permute-done.2.m2 = f32[2,2,144,512]{3,2,1,0:T(8,128)S(1)} collective-permute-done((f32[2,2,144,512]{3,2,1,0:T(8,128)S(1)}, f32[2,2,144,512]{3,2,1,0:T(8,128)S(1)}, u32[]{:S(2)}, u32[]{:S(2)}) %collective-permute-start.2) | collective-permute-done | bytes 1179680 | tf_op jit(solution)/shard_map/ppermute | solution.py:447
  125.9 3.1 %collective-permute-done.3.m3 = f32[2,2,144,512]{3,2,1,0:T(8,128)S(1)} collective-permute-done((f32[2,2,144,512]{3,2,1,0:T(8,128)S(1)}, f32[2,2,144,512]{3,2,1,0:T(8,128)S(1)}, u32[]{:S(2)}, u32[]{:S(2)}) %collective-permute-start.3) | collective-permute-done | bytes 1179680 | tf_op jit(solution)/shard_map/ppermute | solution.py:447
  130.1 3.6 %shard_map.73 = (f32[4,144,512]{2,1,0:T(8,128)S(1)}, f32[4,144,512]{2,1,0:T(8,128)S(1)}, f32[1,1]{1,0:T(1,128)}) custom-call(s32[1]{0:T(128)} %bitcast.me_ref, f32[2,2,144,512]{3,2,1,0:T(8,128)} %copy-done.6, f32[2,2,144,512]{3,2,1,0:T(8,128)} %copy-done.7, f32[2,2,144,512]{3,2,1,0:T(8,128)} %copy-done.8, f32[2,2,144,512]{3,2,1,0:T(8,128)} %copy-done.9, ...), custom_call_target="tpu_custom_call" | custom-call | tf_op jit(solution)/shard_map/pallas_call | solution.py:25
  133.6 2.0 collective-permute-start.17
  139.1 10.4 %shard_map.74 = (f32[12,144,512]{2,1,0:T(8,128)S(1)}, f32[8,128,512]{2,1,0:T(8,128)S(1)}, f32[3,2,144,512]{3,2,1,0:T(8,128)S(1)}) custom-call(s32[1]{0:T(128)} %bitcast.me_ref, f32[4,144,512]{2,1,0:T(8,128)} %copy-done.5, f32[4,144,512]{2,1,0:T(8,128)S(1)} %get-tuple-element.53.a_ref, f32[4,144,512]{2,1,0:T(8,128)S(1)} %get-tuple-element.50.b_ref, ...), custom_call_target="tpu_custom_call" | custom-call | tf_op jit(solution)/shard_map/pallas_call | solution.py:25
  150.6 7.9 %shard_map.75 = (f32[2,2,128,512]{3,2,1,0:T(8,128)}, f32[2,2,128,512]{3,2,1,0:T(8,128)S(1)}, f32[2,2,128,512]{3,2,1,0:T(8,128)S(1)}, f32[2,2,128,512]{3,2,1,0:T(8,128)S(1)}) custom-call(s32[1]{0:T(128)} %bitcast.me_ref, f32[4,144,512]{2,1,0:T(8,128)} %copy-done.12, f32[4,144,512]{2,1,0:T(8,128)S(1)} %get-tuple-element.50.b_ref, ...), custom_call_target="tpu_custom_call" | custom-call | tf_op jit(solution)/shard_map/pallas_call | solution.py:25
  161.1 5.8 %collective-permute-start.20 = (f32[2,2,128,512]{3,2,1,0:T(8,128)S(1)}, f32[2,2,128,512]{3,2,1,0:T(8,128)}, u32[]{:S(2)}, u32[]{:S(2)}) collective-permute-start(f32[2,2,128,512]{3,2,1,0:T(8,128)S(1)} %get-tuple-element.59), channel_id=1, source_target_pairs={{6,0},{2,1},{4,2},{0,3},{7,4},{3,5},{5,6},{1,7},{14,8},{10,9},{12,... | collective-permute-start | bytes 3145736 | tf_op jit(solution)/shard_map/ppermute | solution.py:511
  167.9 37.3 %collective-permute-done.11 = f32[1,1]{1,0:T(1,128)} collective-permute-done((f32[1,1]{1,0:T(1,128)}, f32[1,1]{1,0:T(1,128)}, u32[]{:S(2)}, u32[]{:S(2)}) %collective-permute-start.11) | collective-permute-done | bytes 36 | tf_op jit(solution)/shard_map/ppermute | solution.py:421
  206.6 7.0 %collective-permute-start.12 = (f32[1,1]{1,0:T(1,128)}, f32[1,1]{1,0:T(1,128)}, u32[]{:S(2)}, u32[]{:S(2)}) collective-permute-start(f32[1,1]{1,0:T(1,128)} %add.19), channel_id=1, source_target_pairs={{0,4},{1,5},{2,6},{3,7},{4,0},{5,1},{6,2},{7,3},{8,12},{9,13},{10,... | collective-permute-start | bytes 20 | tf_op jit(solution)/shard_map/ppermute | solution.py:421
  216.4 3.8 %collective-permute-start.14 = (f32[1,1]{1,0:T(1,128)}, f32[1,1]{1,0:T(1,128)}, u32[]{:S(2)}, u32[]{:S(2)}) collective-permute-start(f32[1,1]{1,0:T(1,128)} %add.21), channel_id=1, source_target_pairs={{0,8},{1,9},{2,10},{3,11},{4,12},{5,13},{6,14},{7,15},{8,0},{9,1},... | collective-permute-start | bytes 20 | tf_op jit(solution)/shard_map/ppermute | solution.py:421
  221.0 4.4 %collective-permute-start.15 = (f32[1,1]{1,0:T(1,128)}, f32[1,1]{1,0:T(1,128)}, u32[]{:S(2)}, u32[]{:S(2)}) collective-permute-start(f32[1,1]{1,0:T(1,128)} %add.22), channel_id=1, source_target_pairs={{0,16},{1,17},{2,18},{3,19},{4,20},{5,21},{6,22},{7,23},{8,24},{9,... | collective-permute-start | bytes 20 | tf_op jit(solution)/shard_map/ppermute | solution.py:421
  226.5 4.4 %shard_map.76 = (f32[2,512,512]{2,1,0:T(8,128)}, f32[2,512,512]{2,1,0:T(8,128)}) custom-call(s32[1]{0:T(128)} %bitcast.me_ref, f32[2]{0:T(128)S(1)} %pad_maximum_fusion.scale_ref, f32[2,2,128,512]{3,2,1,0:T(8,128)} %collective-permute-done.18.m0, f32[2,2,128,512]{3,2,1,0:T(8,128)} %collective-permute-done.19.m1, ...), custom_call_target="tpu_custom_call" | custom-call | tf_op jit(solution)/shard_map/pallas_call | solution.py:25
  (57 shorter events, 19.9 us)
Async XLA Ops:
  3.2 29.0 %collective-permute-start.4 = (f32[2,2,144,512]{3,2,1,0:T(8,128)S(1)}, f32[2,2,144,512]{3,2,1,0:T(8,128)S(1)}, u32[]{:S(2)}, u32[]{:S(2)}) collective-permute-start(f32[2,2,144,512]{3,2,1,0:T(8,128)S(1)} %get-tuple-element.37), channel_id=1, source_target_pairs={{0,2},{1,6},{2,0},{3,4},{4,3},{5,7},{6,1},{7,5},{8,10},{9,14},{10,... | collective-permute-start | bytes 3538952 | tf_op jit(solution)/shard_map/ppermute | solution.py:447
  6.2 26.0 %collective-permute-start.5 = (f32[2,2,144,512]{3,2,1,0:T(8,128)S(1)}, f32[2,2,144,512]{3,2,1,0:T(8,128)S(1)}, u32[]{:S(2)}, u32[]{:S(2)}) collective-permute-start(f32[2,2,144,512]{3,2,1,0:T(8,128)S(1)} %get-tuple-element.38), channel_id=1, source_target_pairs={{0,0},{1,4},{2,2},{3,6},{4,1},{5,5},{6,3},{7,7},{8,8},{9,12},{10,1... | collective-permute-start | bytes 3538952 | tf_op jit(solution)/shard_map/ppermute | solution.py:447
  6.9 51.4 %collective-permute-start.7 = (f32[2,2,144,512]{3,2,1,0:T(8,128)S(1)}, f32[2,2,144,512]{3,2,1,0:T(8,128)S(1)}, u32[]{:S(2)}, u32[]{:S(2)}) collective-permute-start(f32[2,2,144,512]{3,2,1,0:T(8,128)S(1)} %get-tuple-element.39), channel_id=1, source_target_pairs={{0,6},{1,2},{2,4},{3,0},{4,7},{5,3},{6,5},{7,1},{8,14},{9,10},{10,... | collective-permute-start | bytes 3538952 | tf_op jit(solution)/shard_map/ppermute | solution.py:447
  10.9 48.3 %collective-permute-start.8 = (f32[2,2,144,512]{3,2,1,0:T(8,128)S(1)}, f32[2,2,144,512]{3,2,1,0:T(8,128)S(1)}, u32[]{:S(2)}, u32[]{:S(2)}) collective-permute-start(f32[2,2,144,512]{3,2,1,0:T(8,128)S(1)} %get-tuple-element.40), channel_id=1, source_target_pairs={{0,4},{1,0},{2,6},{3,2},{4,5},{5,1},{6,7},{7,3},{8,12},{9,8},{10,1... | collective-permute-start | bytes 3538952 | tf_op jit(solution)/shard_map/ppermute | solution.py:447
  63.2 17.2 %collective-permute-start.10 = (f32[2,4,144,512]{3,2,1,0:T(8,128)S(1)}, f32[2,4,144,512]{3,2,1,0:T(8,128)S(1)}, u32[]{:S(2)}, u32[]{:S(2)}) collective-permute-start(f32[2,4,144,512]{3,2,1,0:T(8,128)S(1)} %get-tuple-element.43.a_ref), channel_id=1, source_target_pairs={{0,1},{1,0},{2,3},{3,2},{4,5},{5,4},{6,7},{7,6},{8,9},{9,8},{10,11... | collective-permute-start | bytes 7077896 | tf_op jit(solution)/shard_map/ppermute | solution.py:461
  66.0 7.5 %collective-permute-start.9 = (f32[2,2,144,512]{3,2,1,0:T(8,128)S(1)}, f32[2,2,144,512]{3,2,1,0:T(8,128)S(1)}, u32[]{:S(2)}, u32[]{:S(2)}) collective-permute-start(f32[2,2,144,512]{3,2,1,0:T(8,128)S(1)} %get-tuple-element.41), channel_id=1, source_target_pairs={{1,8},{8,1},{3,10},{10,3},{5,12},{12,5},{7,14},{14,7},{9,16},{16,9... | collective-permute-start | bytes 3538952 | tf_op jit(solution)/shard_map/ppermute | solution.py:460
  71.0 23.5 %collective-permute-start.6 = (f32[2,2,144,512]{3,2,1,0:T(8,128)S(1)}, f32[2,2,144,512]{3,2,1,0:T(8,128)S(1)}, u32[]{:S(2)}, u32[]{:S(2)}) collective-permute-start(f32[2,2,144,512]{3,2,1,0:T(8,128)S(1)} %shard_map.69), channel_id=1, source_target_pairs={{1,8},{8,1},{3,10},{10,3},{5,12},{12,5},{7,14},{14,7},{9,16},{16,9... | collective-permute-start | bytes 3538952 | tf_op jit(solution)/shard_map/ppermute | solution.py:458
  71.7 30.2 %collective-permute-start = (f32[2,2,144,512]{3,2,1,0:T(8,128)S(1)}, f32[2,2,144,512]{3,2,1,0:T(8,128)S(1)}, u32[]{:S(2)}, u32[]{:S(2)}) collective-permute-start(f32[2,2,144,512]{3,2,1,0:T(8,128)S(1)} %get-tuple-element.33), channel_id=1, source_target_pairs={{0,2},{1,6},{2,0},{3,4},{4,3},{5,7},{6,1},{7,5},{8,10},{9,14},{10,... | collective-permute-start | bytes 3538952 | tf_op jit(solution)/shard_map/ppermute | solution.py:447
  72.7 29.2 %collective-permute-start.1 = (f32[2,2,144,512]{3,2,1,0:T(8,128)S(1)}, f32[2,2,144,512]{3,2,1,0:T(8,128)S(1)}, u32[]{:S(2)}, u32[]{:S(2)}) collective-permute-start(f32[2,2,144,512]{3,2,1,0:T(8,128)S(1)} %get-tuple-element.34), channel_id=1, source_target_pairs={{0,0},{1,4},{2,2},{3,6},{4,1},{5,5},{6,3},{7,7},{8,8},{9,12},{10,1... | collective-permute-start | bytes 3538952 | tf_op jit(solution)/shard_map/ppermute | solution.py:447
  73.5 52.5 %collective-permute-start.2 = (f32[2,2,144,512]{3,2,1,0:T(8,128)S(1)}, f32[2,2,144,512]{3,2,1,0:T(8,128)S(1)}, u32[]{:S(2)}, u32[]{:S(2)}) collective-permute-start(f32[2,2,144,512]{3,2,1,0:T(8,128)S(1)} %get-tuple-element.35), channel_id=1, source_target_pairs={{0,6},{1,2},{2,4},{3,0},{4,7},{5,3},{6,5},{7,1},{8,14},{9,10},{10,... | collective-permute-start | bytes 3538952 | tf_op jit(solution)/shard_map/ppermute | solution.py:447
  80.4 48.6 %collective-permute-start.3 = (f32[2,2,144,512]{3,2,1,0:T(8,128)S(1)}, f32[2,2,144,512]{3,2,1,0:T(8,128)S(1)}, u32[]{:S(2)}, u32[]{:S(2)}) collective-permute-start(f32[2,2,144,512]{3,2,1,0:T(8,128)S(1)} %get-tuple-element.36), channel_id=1, source_target_pairs={{0,4},{1,0},{2,6},{3,2},{4,5},{5,1},{6,7},{7,3},{8,12},{9,8},{10,1... | collective-permute-start | bytes 3538952 | tf_op jit(solution)/shard_map/ppermute | solution.py:447
  101.9 27.2 %copy-start.6 = (f32[2,2,144,512]{3,2,1,0:T(8,128)}, f32[2,2,144,512]{3,2,1,0:T(8,128)S(1)}, u32[]{:S(2)}) copy-start(f32[2,2,144,512]{3,2,1,0:T(8,128)S(1)} %collective-permute-done.m0) | copy-start | bytes 3538948
  101.9 27.2 %copy-start.7 = (f32[2,2,144,512]{3,2,1,0:T(8,128)}, f32[2,2,144,512]{3,2,1,0:T(8,128)S(1)}, u32[]{:S(2)}) copy-start(f32[2,2,144,512]{3,2,1,0:T(8,128)S(1)} %collective-permute-done.1.m1) | copy-start | bytes 3538948
  133.6 4.5 %collective-permute-start.17 = (f32[4,144,512]{2,1,0:T(8,128)S(1)}, f32[4,144,512]{2,1,0:T(8,128)S(1)}, u32[]{:S(2)}, u32[]{:S(2)}) collective-permute-start(f32[4,144,512]{2,1,0:T(8,128)S(1)} %get-tuple-element.53.a_ref), channel_id=1, source_target_pairs={{0,1},{1,0},{2,3},{3,2},{4,5},{5,4},{6,7},{7,6},{8,9},{9,8},{10,11... | collective-permute-start | bytes 3538952 | tf_op jit(solution)/shard_map/ppermute | solution.py:488
  135.7 13.9 %collective-permute-start.16 = (f32[4,144,512]{2,1,0:T(8,128)S(1)}, f32[4,144,512]{2,1,0:T(8,128)S(1)}, u32[]{:S(2)}, u32[]{:S(2)}) collective-permute-start(f32[4,144,512]{2,1,0:T(8,128)S(1)} %get-tuple-element.50.b_ref), channel_id=1, source_target_pairs={{1,8},{8,1},{3,10},{10,3},{5,12},{12,5},{7,14},{14,7},{9,16},{16,9... | collective-permute-start | bytes 3538952 | tf_op jit(solution)/shard_map/ppermute | solution.py:487
  158.5 68.0 %collective-permute-start.18 = (f32[2,2,128,512]{3,2,1,0:T(8,128)}, f32[2,2,128,512]{3,2,1,0:T(8,128)}, u32[]{:S(2)}, u32[]{:S(2)}) collective-permute-start(f32[2,2,128,512]{3,2,1,0:T(8,128)} %get-tuple-element.57), channel_id=1, source_target_pairs={{2,0},{6,1},{0,2},{4,3},{3,4},{7,5},{1,6},{5,7},{10,8},{14,9},{8,1... | collective-permute-start | bytes 3145736 | tf_op jit(solution)/shard_map/ppermute | solution.py:511
  159.5 67.0 %collective-permute-start.19 = (f32[2,2,128,512]{3,2,1,0:T(8,128)S(1)}, f32[2,2,128,512]{3,2,1,0:T(8,128)}, u32[]{:S(2)}, u32[]{:S(2)}) collective-permute-start(f32[2,2,128,512]{3,2,1,0:T(8,128)S(1)} %get-tuple-element.58), channel_id=1, source_target_pairs={{0,0},{4,1},{2,2},{6,3},{1,4},{5,5},{3,6},{7,7},{8,8},{12,9},{10,1... | collective-permute-start | bytes 3145736 | tf_op jit(solution)/shard_map/ppermute | solution.py:511
  161.1 65.4 %collective-permute-start.20 = (f32[2,2,128,512]{3,2,1,0:T(8,128)S(1)}, f32[2,2,128,512]{3,2,1,0:T(8,128)}, u32[]{:S(2)}, u32[]{:S(2)}) collective-permute-start(f32[2,2,128,512]{3,2,1,0:T(8,128)S(1)} %get-tuple-element.59), channel_id=1, source_target_pairs={{6,0},{2,1},{4,2},{0,3},{7,4},{3,5},{5,6},{1,7},{14,8},{10,9},{12,... | collective-permute-start | bytes 3145736 | tf_op jit(solution)/shard_map/ppermute | solution.py:511
  166.9 59.6 %collective-permute-start.21 = (f32[2,2,128,512]{3,2,1,0:T(8,128)S(1)}, f32[2,2,128,512]{3,2,1,0:T(8,128)}, u32[]{:S(2)}, u32[]{:S(2)}) collective-permute-start(f32[2,2,128,512]{3,2,1,0:T(8,128)S(1)} %get-tuple-element.60), channel_id=1, source_target_pairs={{4,0},{0,1},{6,2},{2,3},{5,4},{1,5},{7,6},{3,7},{12,8},{8,9},{14,1... | collective-permute-start | bytes 3145736 | tf_op jit(solution)/shard_map/ppermute | solution.py:511
  166.9 38.3 %collective-permute-start.11 = (f32[1,1]{1,0:T(1,128)}, f32[1,1]{1,0:T(1,128)}, u32[]{:S(2)}, u32[]{:S(2)}) collective-permute-start(f32[1,1]{1,0:T(1,128)} %get-tuple-element.49), channel_id=1, source_target_pairs={{0,2},{1,3},{2,0},{3,1},{4,6},{5,7},{6,4},{7,5},{8,10},{9,11},{10,... | collective-permute-start | bytes 20 | tf_op jit(solution)/shard_map/ppermute | solution.py:421
  206.6 7.2 %collective-permute-start.12 = (f32[1,1]{1,0:T(1,128)}, f32[1,1]{1,0:T(1,128)}, u32[]{:S(2)}, u32[]{:S(2)}) collective-permute-start(f32[1,1]{1,0:T(1,128)} %add.19), channel_id=1, source_target_pairs={{0,4},{1,5},{2,6},{3,7},{4,0},{5,1},{6,2},{7,3},{8,12},{9,13},{10,... | collective-permute-start | bytes 20 | tf_op jit(solution)/shard_map/ppermute | solution.py:421
  214.5 1.2 collective-permute-start.13
  216.4 4.0 %collective-permute-start.14 = (f32[1,1]{1,0:T(1,128)}, f32[1,1]{1,0:T(1,128)}, u32[]{:S(2)}, u32[]{:S(2)}) collective-permute-start(f32[1,1]{1,0:T(1,128)} %add.21), channel_id=1, source_target_pairs={{0,8},{1,9},{2,10},{3,11},{4,12},{5,13},{6,14},{7,15},{8,0},{9,1},... | collective-permute-start | bytes 20 | tf_op jit(solution)/shard_map/ppermute | solution.py:421
  221.0 4.6 %collective-permute-start.15 = (f32[1,1]{1,0:T(1,128)}, f32[1,1]{1,0:T(1,128)}, u32[]{:S(2)}, u32[]{:S(2)}) collective-permute-start(f32[1,1]{1,0:T(1,128)} %add.22), channel_id=1, source_target_pairs={{0,16},{1,17},{2,18},{3,19},{4,20},{5,21},{6,22},{7,23},{8,24},{9,... | collective-permute-start | bytes 20 | tf_op jit(solution)/shard_map/ppermute | solution.py:421
  (11 other events, 88.3 us)

commit v3 on v2

v3 whole, which is shorter than its diff:
```python
from functools import partial

import jax
import jax.numpy as jnp
from jax import lax
from jax.experimental import pallas as pl
from jax.experimental.pallas import tpu as pltpu
from jax.sharding import PartitionSpec as P


ITERS = 4
time_step = 0.125

GROUP = 8
PARTS = 4
HALO = 8
LANES = 128
ROUNDS = ((0, 1), (0, 0), (1, 1), (1, 0))


VM = pl.BlockSpec(memory_space=pltpu.VMEM)
SM = pl.BlockSpec(memory_space=pltpu.SMEM)
PARAMS = pltpu.CompilerParams(vmem_limit_bytes=14 * 1024 * 1024)
F32 = jnp.float32


def call(kernel, outs, scalars, arrays, scratch=(), total=False, **options):
    return pl.pallas_call(
        kernel,
        out_shape=outs,
        in_specs=[SM] * len(scalars) + [VM] * len(arrays),
        out_specs=[VM] * (len(outs) - total) + [SM] * total,
        scratch_shapes=scratch,
        compiler_params=PARAMS,
        **options,
    )(*scalars, *arrays)


def inside(*arrays):
    return [pltpu.with_memory_space_constraint(a, pltpu.VMEM) for a in arrays]


def outside(*arrays):
    return [pltpu.with_memory_space_constraint(a, pltpu.HBM) for a in arrays]


def bits(me):
    return (me >> 2) & 1, (me >> 1) & 1, me & 1


def part(y, x):
    return 2 * y + x


def send_pairs(count, r1, r0):
    pairs = []
    for i in range(count):
        y, x, c = bits(i)
        pairs.append((i, (i & ~7) + 4 * (c ^ r1) + 2 * (x ^ r0) + y))
    return pairs


def pack_kernel(rim, me_ref, a_ref, b_ref, *out_refs):
    _, x, c = bits(me_ref[0])
    planes, height, width = a_ref.shape
    rows = height // PARTS
    for (r1, r0), out in zip(ROUNDS, out_refs):
        q = part(c ^ r1, x ^ r0)
        start = pl.multiple_of(q * rows, 8)
        above = pl.multiple_of(jnp.maximum(start - HALO, 0), 8)
        below = pl.multiple_of(jnp.minimum(start + rows, height - HALO), 8)
        for k, src in enumerate((a_ref, b_ref)):
            for i in range(planes):
                for b in range(width // LANES):
                    cols = slice(b * LANES, (b + 1) * LANES)
                    top = src[i, pl.ds(above, HALO), cols]
                    out[k, i, b, :rim, :] = jnp.where(q > 0, top[HALO - rim :], 0.0)
                    low = src[i, pl.ds(below, HALO), cols]
                    out[k, i, b, rim + rows :, :] = jnp.where(q < PARTS - 1, low[:rim], 0.0)
                    for at in range(0, rows, HALO):
                        here = pl.ds(pl.multiple_of(start + at, 8), HALO)
                        out[k, i, b, rim + at : rim + at + HALO, :] = src[i, here, cols]


def slot(me, r, planes, i):
    y, x, c = bits(me)
    r1, r0 = r
    from_c = y ^ r1
    block = x ^ r0 ^ c
    ahead = planes * from_c + i
    return block, jnp.where(c == 0, ahead, 2 * planes - 1 - ahead)


def early_kernel(me_ref, m0, m1, early_ref):
    me = me_ref[0]
    for r, m in zip(ROUNDS, (m0, m1)):
        block, _ = slot(me, r, m.shape[1], 0)

        @pl.when(block == 0)
        def _(m=m):
            early_ref[...] = m[...]


def place_kernel(me_ref, m0, m1, m2, m3, late_ref, a_ref, b_ref):
    me = me_ref[0]
    planes = m0.shape[1]
    for r, m in zip(ROUNDS, (m0, m1, m2, m3)):
        block, _ = slot(me, r, planes, 0)

        @pl.when(block == 0)
        def _(r=r, m=m):
            if r[0]:
                late_ref[...] = m[...]
            for i in range(planes):
                _, at = slot(me, r, planes, i)
                for k in range(2):
                    b_ref[k, at] = m[k, i]

        @pl.when(block == 1)
        def _(r=r, m=m):
            for i in range(planes):
                _, at = slot(me, r, planes, i)
                for k in range(2):
                    a_ref[k, at] = m[k, i]


def edges(shape):
    col = lax.broadcasted_iota(jnp.int32, shape, 2)
    return col == 0, col == shape[2] - 1


def lap_rows(ref, s, r0, n, first, last):
    lo = HALO + r0
    mid = ref[s, :, lo : lo + n, :]
    none = jnp.zeros((1,) + mid.shape[1:], F32)
    beside = ref[s + 1, :, lo : lo + n, :] + ref[s - 1, :, lo : lo + n, :]
    beside = beside + (ref[s, :, lo + 1 : lo + n + 1, :] + ref[s, :, lo - 1 : lo + n - 1, :])
    right = pltpu.roll(mid, LANES - 1, 2)
    right = jnp.where(last, jnp.concatenate([right[1:], none], axis=0), right)
    left = pltpu.roll(mid, 1, 2)
    left = jnp.where(first, jnp.concatenate([none, left[:-1]], axis=0), left)
    return beside + (right + left) - 6.0 * mid, mid


def clear_rims(ref, rows):
    none = jnp.zeros((ref.shape[1], HALO, LANES), F32)

    def one(s, carry):
        ref[s, :, :HALO, :] = none
        ref[s, :, HALO + rows :, :] = none
        return carry

    lax.fori_loop(0, ref.shape[0], one, 0)


CHUNK = 16


def copy_rows(rows, move):
    def one(t, carry):
        r = pl.multiple_of(t * CHUNK, 8)
        move(pl.ds(r, CHUNK), pl.ds(r + HALO, CHUNK))
        return carry

    lax.fori_loop(0, rows // CHUNK, one, 0)


def spans(lo, hi, body):
    if hi > lo:
        lax.fori_loop(lo, hi, body, 0)


def forward_main(me_ref, a_ref, b_ref, ra_ref, u_out, c_out, slopes, saved, u0, u1):
    half, blocks, rows = a_ref.shape[1:4]
    clear_rims(u0, rows)
    clear_rims(u1, rows)
    for i in range(half):
        for src, at, t in ((b_ref, i, i), (a_ref, i, half + i), (ra_ref, half - 1 - i, 2 * half + i)):

            def fill(r, rh, src=src, at=at, t=t):
                u0[t, :, rh, :] = src[0, at, :, r, :]
                c_out[t, :, r, :] = time_step * src[1, at, :, r, :]

            copy_rows(rows, fill)
    first, last = edges((blocks, CHUNK, LANES))
    for k in range(ITERS):
        old, new = (u0, u1) if k % 2 == 0 else (u1, u0)

        def plane(t, carry, own, k=k, old=old, new=new):
            for r0 in range(0, rows, CHUNK):
                slope, mid = lap_rows(old, t, r0, CHUNK, first, last)
                moved = mid + c_out[t, :, r0 : r0 + CHUNK, :] * slope
                if own:
                    slopes[k, t, :, r0 : r0 + CHUNK, :] = slope
                if k == ITERS - 1:
                    u_out[t, :, r0 : r0 + CHUNK, :] = moved
                else:
                    new[t, :, HALO + r0 : HALO + r0 + CHUNK, :] = moved
            return carry

        spans(1 + k, 2 * half, lambda t, c: plane(t, c, True))
        spans(2 * half, 2 * half + ITERS - 1 - k, lambda t, c: plane(t, c, False))
        if k < ITERS - 1:
            for i in range(2):

                def keep(r, rh, k=k, i=i, new=new):
                    saved[k, i, :, r, :] = new[k + 1 + i, :, rh, :]

                copy_rows(rows, keep)


def forward_wedge(me_ref, early, late, b_ref, c_ref, saved, u_in, slopes_in, u_out, slopes, cw, w0, w1):
    y, _, c = bits(me_ref[0])
    half, blocks, rows = b_ref.shape[1:4]
    planes = early.shape[1]
    clear_rims(w0, rows)
    clear_rims(w1, rows)
    for r1, far in enumerate((early, late)):
        for i in range(planes):
            ahead = planes * (y ^ r1) + i
            s = half - 1 - jnp.where(c == 1, ahead, half - 1 - ahead)

            def fill(r, rh, far=far, i=i, s=s):
                w0[s, :, rh, :] = far[0, i, :, r, :]
                cw[s, :, r, :] = time_step * far[1, i, :, r, :]

            copy_rows(rows, fill)
    for i in range(2):
        copy_rows(rows, lambda r, rh, i=i: w0.__setitem__((half + i, slice(None), rh), b_ref[0, i, :, r, :]))
    first, last = edges((blocks, CHUNK, LANES))
    for k in range(ITERS):
        old, new = (w0, w1) if k % 2 == 0 else (w1, w0)
        if k:
            for i in range(2):
                copy_rows(rows, lambda r, rh, i=i: old.__setitem__((half + k + i, slice(None), rh), saved[k - 1, i, :, r, :]))

        def plane(s, carry, own, k=k, old=old, new=new):
            for r0 in range(0, rows, CHUNK):
                slope, mid = lap_rows(old, s, r0, CHUNK, first, last)
                at = slice(r0, r0 + CHUNK)
                coef = c_ref[s - half, :, at, :] if own else cw[s, :, at, :]
                moved = mid + coef * slope
                if own:
                    slopes[k, s - half, :, at, :] = slope
                if k == ITERS - 1:
                    u_out[s - half, :, at, :] = moved
                else:
                    new[s, :, HALO + r0 : HALO + r0 + CHUNK, :] = moved
            return carry

        spans(half - ITERS + 1 + k, half, lambda s, c: plane(s, c, False))
        spans(half, half + k + 1, lambda s, c: plane(s, c, True))


def resid_kernel(me_ref, m0, m1, m2, m3, u_ref, a_ref, b_ref, total_ref, acc_ref):
    me = me_ref[0]
    planes, blocks, short = m0.shape[1:4]
    rows = u_ref.shape[2]
    rim = (rows - short) // 2
    shape = (blocks, HALO, LANES)
    row = lax.broadcasted_iota(jnp.int32, shape, 1)
    acc_ref[...] = jnp.zeros(shape, F32)
    for r, m in zip(ROUNDS, (m0, m1, m2, m3)):
        for i in range(planes):
            block, at = slot(me, r, planes, i)
            for flag, dst in ((1, a_ref), (0, b_ref)):

                @pl.when(block == flag)
                def _(m=m, i=i, at=at, dst=dst, flag=flag):
                    acc = acc_ref[...]
                    dst[at, :, :rim, :] = jnp.zeros((blocks, rim, LANES), F32)
                    dst[at, :, rows - rim :, :] = jnp.zeros((blocks, rim, LANES), F32)
                    for lo in range(0, short, HALO):
                        here = slice(lo + rim, lo + rim + HALO)
                        resid = u_ref[2 * planes * flag + at, :, here, :] - m[0, i, :, lo : lo + HALO, :]
                        weighted = m[1, i, :, lo : lo + HALO, :] * resid
                        dst[at, :, here, :] = weighted
                        share = weighted * resid
                        if lo + rim < HALO:
                            share = jnp.where(row >= HALO - rim, share, 0.0)
                        if lo + rim + HALO > rows - HALO:
                            share = jnp.where(row < HALO - rim, share, 0.0)
                        acc = acc + share
                    acc_ref[...] = acc

    total_ref[0, 0] = jnp.sum(acc_ref[...])


def backward_main(me_ref, ra_ref, a_ref, b_ref, c_ref, slopes, lam, grad, saved, mv0, mv1):
    half, blocks, rows = a_ref.shape[:3]
    clear_rims(mv0, rows)
    clear_rims(mv1, rows)
    for i in range(half):
        for src, at, t in ((b_ref, i, i), (a_ref, i, half + i), (ra_ref, half - 1 - i, 2 * half + i)):

            def fill(r, rh, src=src, at=at, t=t):
                v = src[at, :, r, :]
                lam[t, :, r, :] = v
                mv0[t, :, rh, :] = c_ref[t, :, r, :] * v

            copy_rows(rows, fill)
    first, last = edges((blocks, CHUNK, LANES))
    first8, last8 = edges((blocks, HALO, LANES))

    for j in range(ITERS):
        k = ITERS - 1 - j
        old, new = (mv0, mv1) if j % 2 == 0 else (mv1, mv0)

        def gain(t, r0, j=j, k=k):
            g = lam[t, :, r0 : r0 + CHUNK, :] * slopes[k, t, :, r0 : r0 + CHUNK, :]
            at = slice(r0 - HALO, r0 - HALO + CHUNK)
            grad[t, :, at, :] = grad[t, :, at, :] + g if j else g

        def gain_plane(t, carry, gain=gain):
            for r0 in range(HALO, rows - HALO, CHUNK):
                gain(t, r0)
            return carry

        def step(t, r0, n, f, l, j=j, old=old, new=new):
            change, _ = lap_rows(old, t, r0, n, f, l)
            after = lam[t, :, r0 : r0 + n, :] + change
            lam[t, :, r0 : r0 + n, :] = after
            if j < ITERS - 1:
                new[t, :, HALO + r0 : HALO + r0 + n, :] = c_ref[t, :, r0 : r0 + n, :] * after

        def own_plane(t, carry, gain=gain, step=step, j=j):
            for r0 in range(HALO, rows - HALO, CHUNK):
                gain(t, r0)
                step(t, r0, CHUNK, first, last)
            if j < ITERS - 1:
                step(t, 0, HALO, first8, last8)
                step(t, rows - HALO, HALO, first8, last8)
            return carry

        def halo_plane(t, carry, step=step):
            for r0 in range(0, rows, CHUNK):
                step(t, r0, CHUNK, first, last)
            return carry

        gain_plane(j, 0)
        spans(1 + j, 2 * half, own_plane)
        spans(2 * half, 2 * half + ITERS - 1 - j, halo_plane)
        if j < ITERS - 1:
            for i in range(2):

                def keep(r, rh, j=j, i=i, new=new):
                    saved[j, i, :, r, :] = new[j + 1 + i, :, rh, :]

                copy_rows(rows, keep)


def backward_wedge(me_ref, rb_ref, b_ref, cw, c_ref, slopes, saved, lam_in, grad_in, *refs):
    outs, (lam, mv0, mv1, grad) = refs[:-4], refs[-4:]
    half, blocks, rows = b_ref.shape[:3]
    clear_rims(mv0, rows)
    clear_rims(mv1, rows)
    for i in range(half):

        def fill(r, rh, i=i):
            v = rb_ref[half - 1 - i, :, r, :]
            lam[i, :, r, :] = v
            mv0[i, :, rh, :] = cw[i, :, r, :] * v
            lam[half + i, :, r, :] = lam_in[i, :, r, :]

        copy_rows(rows, fill)
        if i < 2:
            copy_rows(rows, lambda r, rh, i=i: mv0.__setitem__((half + i, slice(None), rh), c_ref[i, :, r, :] * b_ref[i, :, r, :]))

        def one(t, carry, i=i):
            r = pl.multiple_of(t * CHUNK, 8)
            grad[i, :, pl.ds(r, CHUNK), :] = grad_in[i, :, pl.ds(r, CHUNK), :]
            return carry

        lax.fori_loop(0, (rows - 2 * HALO) // CHUNK, one, 0)
    first, last = edges((blocks, CHUNK, LANES))
    for j in range(ITERS):
        k = ITERS - 1 - j
        old, new = (mv0, mv1) if j % 2 == 0 else (mv1, mv0)
        if j:
            for i in range(2):
                copy_rows(rows, lambda r, rh, i=i: old.__setitem__((half + j + i, slice(None), rh), saved[j - 1, i, :, r, :]))

        def plane(s, carry, own, j=j, old=old, new=new):
            for r0 in range(0, rows, CHUNK):
                change, _ = lap_rows(old, s, r0, CHUNK, first, last)
                at = slice(r0, r0 + CHUNK)
                after = lam[s, :, at, :] + change
                if j < ITERS - 1:
                    coef = c_ref[s - half, :, at, :] if own else cw[s, :, at, :]
                    new[s, :, HALO + r0 : HALO + r0 + CHUNK, :] = coef * after
                lam[s, :, at, :] = after
            return carry

        def gain(s, carry, j=j, k=k):
            for r0 in range(HALO, rows - HALO, CHUNK):
                at = slice(r0 - HALO, r0 - HALO + CHUNK)
                g = lam[s, :, r0 : r0 + CHUNK, :] * slopes[k, s - half, :, r0 : r0 + CHUNK, :]
                grad[s - half, :, at, :] = grad[s - half, :, at, :] + g
            return carry

        spans(half, half + j, gain)
        spans(half - ITERS + 1 + j, half, lambda s, c: plane(s, c, False))
        spans(half, half + j + 1, lambda s, c: plane(s, c, True))
    me = me_ref[0]
    planes = half // 2
    for n, r in enumerate(ROUNDS):
        block, _ = slot(me, r, planes, 0)
        for flag, g_src, l_src in ((0, grad, lam), (1, grad_in, lam_in)):

            @pl.when(block == flag)
            def _(n=n, r=r, g_src=g_src, l_src=l_src):
                for i in range(planes):
                    _, at = slot(me, r, planes, i)
                    outs[n][i] = g_src[at if g_src is grad else half + at]
                    outs[4 + n][i] = l_src[half + at, :, HALO : rows - HALO, :]


def home_kernel(me_ref, scale_ref, m0, m1, m2, m3, out):
    _, x, c = bits(me_ref[0])
    planes, blocks, rows = m0.shape[:3]
    scale = scale_ref[0, 0]
    for (r1, r0), m in zip(ROUNDS, (m0, m1, m2, m3)):
        start = pl.multiple_of(part(c ^ r1, x ^ r0) * rows, 8)
        for i in range(planes):
            for b in range(blocks):
                out[i, pl.ds(start, rows), b * LANES : (b + 1) * LANES] = m[i, b] * scale


def shape(*dims):
    return pltpu.VMEM(dims, F32)


def exchange_sum(value, axis, count, steps):
    for step in steps:
        value = value + lax.ppermute(value, axis, [(i, i ^ step) for i in range(count)])
    return value


def on_device(coefficient, initial_field, observed, misfit_weight):
    axis = "gz"
    count = lax.axis_size(axis)
    planes, height, width = coefficient.shape
    if count % GROUP or width % LANES or height % (16 * PARTS) or 2 * planes < ITERS or ITERS * 2 > HALO:
        raise ValueError("unsupported sizes")
    rows = height // PARTS
    tall = rows + 2 * HALO
    half = 2 * planes
    blocks = width // LANES
    me = lax.axis_index(axis).astype(jnp.int32).reshape(1)

    partner = [(i, i ^ 1) for i in range(count)]
    beyond = []
    for i in range(count - GROUP + 1):
        if i % 2:
            if i + GROUP - 1 < count:
                beyond += [(i, i + GROUP - 1), (i + GROUP - 1, i)]

    def regroup(a, b, rim):
        message = shape(2, planes, blocks, rows + 2 * rim, LANES)
        msgs = call(partial(pack_kernel, rim), [message] * 4, [me], [a, b])
        got = []
        for m, r in zip(msgs, ROUNDS):
            got.append(lax.ppermute(m, axis, send_pairs(count, *r)))
        return outside(*got)

    first = regroup(*outside(initial_field, coefficient), HALO)
    second = regroup(*outside(observed, misfit_weight), HALO - ITERS)

    plane_set = (blocks, tall, LANES)
    padded = (blocks, tall + 2 * HALO, LANES)
    inner = (blocks, rows, LANES)
    saved_shape = shape(ITERS - 1, 2, *plane_set)
    quarter = shape(2, planes, *plane_set)
    (early,) = call(early_kernel, [quarter], [me], first[:2])
    early = lax.ppermute(early, axis, beyond)
    late, blk_a, blk_b = call(place_kernel, [quarter] + [shape(2, half, *plane_set)] * 2, [me], first)
    late = lax.ppermute(late, axis, beyond)
    far_a = lax.ppermute(blk_a, axis, partner)
    far_a, early, late = outside(far_a, early, late)
    final, coef, slopes, saved = call(
        forward_main,
        [shape(2 * half, *plane_set), shape(3 * half, *plane_set), shape(ITERS, 2 * half, *plane_set), saved_shape],
        [me],
        inside(blk_a, blk_b) + [far_a],
        [pltpu.VMEM((3 * half, *padded), F32)] * 2,
    )
    final, slopes, far_coef = call(
        forward_wedge,
        [shape(2 * half, *plane_set), shape(ITERS, 2 * half, *plane_set), shape(half, *plane_set)],
        [me],
        [early, late] + inside(blk_b, coef, saved, final, slopes),
        [pltpu.VMEM((half + ITERS + 2, *padded), F32)] * 2,
        input_output_aliases={6: 0, 7: 1},
    )

    lam_a, lam_b, part_total = call(
        resid_kernel,
        [shape(half, *plane_set)] * 2 + [jax.ShapeDtypeStruct((1, 1), F32)],
        [me],
        second + inside(final),
        [pltpu.VMEM((blocks, HALO, LANES), F32)],
        total=True,
    )
    far_lb = lax.ppermute(lam_b, axis, beyond)
    far_la = lax.ppermute(lam_a, axis, partner)
    (far_la,), (far_lb,) = outside(far_la), outside(far_lb)
    far = [1] + [1 << k for k in range(3, count.bit_length() - 1)]
    part_total = exchange_sum(part_total, axis, count, [2])
    lam, grad, saved = call(
        backward_main,
        [shape(3 * half, *plane_set), shape(2 * half, *inner), saved_shape],
        [me],
        [far_la] + inside(lam_a, lam_b, coef, slopes),
        [pltpu.VMEM((3 * half, *padded), F32)] * 2,
    )
    part_total = exchange_sum(part_total, axis, count, [4])
    outs = call(
        backward_wedge,
        [shape(planes, *inner)] * 8,
        [me],
        [far_lb] + inside(lam_b, far_coef, coef, slopes, saved, lam, grad),
        [pltpu.VMEM((2 * half, *plane_set), F32)]
        + [pltpu.VMEM((half + ITERS + 2, *padded), F32)] * 2
        + [pltpu.VMEM((half, *inner), F32)],
    )
    back = []
    for m, r in zip(outs, ROUNDS * 2):
        back.append(lax.ppermute(m, axis, [(j, i) for i, j in send_pairs(count, *r)]))
    back = outside(*back)

    if count & (count - 1):
        total = lax.psum(part_total, axis) / 4
    else:
        total = exchange_sum(part_total, axis, count, far)
    cells = count * planes * height * width
    misfit = jnp.sqrt(total[0, 0] / cells + 1e-06)
    inverse = 1.0 / misfit
    whole = [jax.ShapeDtypeStruct((planes, height, width), F32)]
    (gradient,) = call(home_kernel, whole, [me, (time_step * inverse).reshape(1, 1)], back[:4])
    (adjoint,) = call(home_kernel, whole, [me, inverse.reshape(1, 1)], back[4:])
    return gradient, adjoint, misfit


def solution(mesh):
    placed = P("gz", None, None)
    return jax.shard_map(
        on_device,
        mesh=mesh,
        in_specs=(placed,) * 4,
        out_specs=(placed, placed, P()),
        check_vma=False,
    )
```

time: 233 us -> 236 us (1.013)
  starting transfers between devices: 53.1 us -> 59.3 us
    ppermute x5, waiting for transfers between devices: 38.2 us -> 15.4 us  [exchange_sum(): lax.ppermute(value, axis, [(i, i ^ step) for i in range(count)])]
    ppermute x4 -> x8, waiting for transfers between devices: 0.01 us -> 22.6 us  [on_device(): lax.ppermute(m, axis, [(j, i) for i, j in send_pairs(count, *r)])]
    ppermute x4 -> x8, starting transfers between devices: 8.41 us -> 13.7 us  [on_device(): lax.ppermute(m, axis, [(j, i) for i, j in send_pairs(count, *r)])]
    pallas_call x10 -> x11, Pallas kernels: 52.1 us -> 51.5 us  [call(): pl.pallas_call(kernel, out_shape=outs, in_specs=[SM] * len(scalars) + [VM...]
    unnamed x26 -> x32, local copies, waits for them, and re-layouts: 5.32 us -> 5.49 us
  transfers between devices with their start and end apart: 22 -> 26, of which waited for: 11 -> 14; matrix products, arithmetic and copies ran while one was open for 0% -> 0% of each run, Pallas kernels for 13% -> 14%
where the time goes in v3:
time: 236 us; the launch traced here: 235 us
  waiting for transfers between devices  113 us (48%)
  starting transfers between devices  59.3 us (25%)
  Pallas kernels  51.5 us (22%)
  between operations  5.93 us (3%)
  local copies, waits for them, and re-layouts  5.49 us (2%)
    ppermute x8, waiting for transfers between devices, regroup(): got.append(lax.ppermute(m, axis, send_pairs(count, *r)))  73.2 us
    pallas_call x11, Pallas kernels, call(): pl.pallas_call(kernel, out_shape=outs, in_specs=[SM] * len(scalars) + [VM...  51.5 us
    ppermute x8, waiting for transfers between devices, on_device(): lax.ppermute(m, axis, [(j, i) for i, j in send_pairs(count, *r)])  22.6 us
    ppermute x8, starting transfers between devices, regroup(): got.append(lax.ppermute(m, axis, send_pairs(count, *r)))  20.6 us
    ppermute x5, starting transfers between devices, exchange_sum(): lax.ppermute(value, axis, [(i, i ^ step) for i in range(count)])  18 us
    ppermute x5, waiting for transfers between devices, exchange_sum(): lax.ppermute(value, axis, [(i, i ^ step) for i in range(count)])  15.4 us
    ppermute x8, starting transfers between devices, on_device(): lax.ppermute(m, axis, [(j, i) for i, j in send_pairs(count, *r)])  13.7 us
    unnamed x32, local copies, waits for them, and re-layouts  5.49 us
  transfers between devices with their start and end apart: 26, of which 14 were waited for; matrix products, arithmetic and copies ran while one was open for 0% of the time, Pallas kernels for 14%

profile of v3, /device:TPU:0, one launch (start us, length us, event | category | flops | bytes accessed | tf_op | source)
XLA Modules:
  0.0 235.1 jit_solution(1889773399565817897)
XLA Ops:
  3.2 3.0 %collective-permute-start.4 = (f32[2,2,4,144,128]{4,3,2,1,0:T(8,128)S(1)}, f32[2,2,4,144,128]{4,3,2,1,0:T(8,128)S(1)}, u32[]{:S(2)}, u32[]{:S(2)}) collective-permute-start(f32[2,2,4,144,128]{4,3,2,1,0:T(8,128)S(1)} %get-tuple-element.39), channel_id=1, source_target_pairs={{0,2},{1,6},{2,0},{3,4},{4,3},{5,7},{6,1},{7,5},{8,10},{9,14},{10,... | collective-permute-start | bytes 3538952 | tf_op jit(solution)/shard_map/ppermute | solution.py:463
  7.0 3.9 %collective-permute-start.7 = (f32[2,2,4,144,128]{4,3,2,1,0:T(8,128)S(1)}, f32[2,2,4,144,128]{4,3,2,1,0:T(8,128)S(1)}, u32[]{:S(2)}, u32[]{:S(2)}) collective-permute-start(f32[2,2,4,144,128]{4,3,2,1,0:T(8,128)S(1)} %get-tuple-element.41), channel_id=1, source_target_pairs={{0,6},{1,2},{2,4},{3,0},{4,7},{5,3},{6,5},{7,1},{8,14},{9,10},{10,... | collective-permute-start | bytes 3538952 | tf_op jit(solution)/shard_map/ppermute | solution.py:463
  10.9 21.3 %collective-permute-done.4.m0 = f32[2,2,4,144,128]{4,3,2,1,0:T(8,128)S(1)} collective-permute-done((f32[2,2,4,144,128]{4,3,2,1,0:T(8,128)S(1)}, f32[2,2,4,144,128]{4,3,2,1,0:T(8,128)S(1)}, u32[]{:S(2)}, u32[]{:S(2)}) %collective-permute-start.4) | collective-permute-done | bytes 1179680 | tf_op jit(solution)/shard_map/ppermute | solution.py:463
  32.2 26.2 %collective-permute-done.7.m2 = f32[2,2,4,144,128]{4,3,2,1,0:T(8,128)S(1)} collective-permute-done((f32[2,2,4,144,128]{4,3,2,1,0:T(8,128)S(1)}, f32[2,2,4,144,128]{4,3,2,1,0:T(8,128)S(1)}, u32[]{:S(2)}, u32[]{:S(2)}) %collective-permute-start.7) | collective-permute-done | bytes 1179680 | tf_op jit(solution)/shard_map/ppermute | solution.py:463
  63.2 2.8 %collective-permute-start.10 = (f32[2,4,4,144,128]{4,3,2,1,0:T(8,128)S(1)}, f32[2,4,4,144,128]{4,3,2,1,0:T(8,128)S(1)}, u32[]{:S(2)}, u32[]{:S(2)}) collective-permute-start(f32[2,4,4,144,128]{4,3,2,1,0:T(8,128)S(1)} %get-tuple-element.45.a_ref), channel_id=1, source_target_pairs={{0,1},{1,0},{2,3},{3,2},{4,5},{5,4},{6,7},{7,6},{8,9},{9,8},{10,11... | collective-permute-start | bytes 7077896 | tf_op jit(solution)/shard_map/ppermute | solution.py:478
  73.5 6.9 %collective-permute-start.2 = (f32[2,2,4,136,128]{4,3,2,1,0:T(8,128)S(1)}, f32[2,2,4,136,128]{4,3,2,1,0:T(8,128)S(1)}, u32[]{:S(2)}, u32[]{:S(2)}) collective-permute-start(f32[2,2,4,136,128]{4,3,2,1,0:T(8,128)S(1)} %get-tuple-element.37), channel_id=1, source_target_pairs={{0,6},{1,2},{2,4},{3,0},{4,7},{5,3},{6,5},{7,1},{8,14},{9,10},{10,... | collective-permute-start | bytes 3342344 | tf_op jit(solution)/shard_map/ppermute | solution.py:463
  80.4 4.2 %collective-permute-start.3 = (f32[2,2,4,136,128]{4,3,2,1,0:T(8,128)S(1)}, f32[2,2,4,136,128]{4,3,2,1,0:T(8,128)S(1)}, u32[]{:S(2)}, u32[]{:S(2)}) collective-permute-start(f32[2,2,4,136,128]{4,3,2,1,0:T(8,128)S(1)} %get-tuple-element.38), channel_id=1, source_target_pairs={{0,4},{1,0},{2,6},{3,2},{4,5},{5,1},{6,7},{7,3},{8,12},{9,8},{10,1... | collective-permute-start | bytes 3342344 | tf_op jit(solution)/shard_map/ppermute | solution.py:463
  84.6 9.5 %shard_map.71 = (f32[8,4,144,128]{3,2,1,0:T(8,128)S(1)}, f32[12,4,144,128]{3,2,1,0:T(8,128)S(1)}, f32[4,8,4,144,128]{4,3,2,1,0:T(8,128)S(1)}, f32[3,2,4,144,128]{4,3,2,1,0:T(8,128)S(1)}) custom-call(s32[1]{0:T(128)} %bitcast.me_ref, f32[2,4,4,144,128]{4,3,2,1,0:T(8,128)S(1)} %get-tuple-element.45.a_ref, f32[2,4,4,144,128]{4,3,2,1,0:T(8,128)S(1)} %get-tuple-element.44.b_ref, ...), custom_call_target="tpu_custom_call" | custom-call | tf_op jit(solution)/shard_map/pallas_call | solution.py:28
  95.1 6.2 %shard_map.72 = (f32[8,4,144,128]{3,2,1,0:T(8,128)S(1)}, f32[4,8,4,144,128]{4,3,2,1,0:T(8,128)S(1)}, f32[4,4,144,128]{3,2,1,0:T(8,128)S(1)}) custom-call(s32[1]{0:T(128)} %bitcast.me_ref, f32[2,2,4,144,128]{4,3,2,1,0:T(8,128)} %copy-done.4, f32[2,2,4,144,128]{4,3,2,1,0:T(8,128)} %copy-done.3, ...), custom_call_target="tpu_custom_call", output_to_operand_aliasing={{0}: (6, {}), {1}: (7, {})} | custom-call | tf_op jit(solution)/shard_map/pallas_call | solution.py:28
  101.4 21.8 %collective-permute-done.2.m2 = f32[2,2,4,136,128]{4,3,2,1,0:T(8,128)S(1)} collective-permute-done((f32[2,2,4,136,128]{4,3,2,1,0:T(8,128)S(1)}, f32[2,2,4,136,128]{4,3,2,1,0:T(8,128)S(1)}, u32[]{:S(2)}, u32[]{:S(2)}) %collective-permute-start.2) | collective-permute-done | bytes 1114144 | tf_op jit(solution)/shard_map/ppermute | solution.py:463
  123.2 3.1 %collective-permute-done.3.m3 = f32[2,2,4,136,128]{4,3,2,1,0:T(8,128)S(1)} collective-permute-done((f32[2,2,4,136,128]{4,3,2,1,0:T(8,128)S(1)}, f32[2,2,4,136,128]{4,3,2,1,0:T(8,128)S(1)}, u32[]{:S(2)}, u32[]{:S(2)}) %collective-permute-start.3) | collective-permute-done | bytes 1114144 | tf_op jit(solution)/shard_map/ppermute | solution.py:463
  127.3 3.5 %shard_map.73 = (f32[4,4,144,128]{3,2,1,0:T(8,128)S(1)}, f32[4,4,144,128]{3,2,1,0:T(8,128)S(1)}, f32[1,1]{1,0:T(1,128)}) custom-call(s32[1]{0:T(128)} %bitcast.me_ref, f32[2,2,4,136,128]{4,3,2,1,0:T(8,128)} %copy-done.9, f32[2,2,4,136,128]{4,3,2,1,0:T(8,128)} %copy-done.10, f32[2,2,4,136,128]{4,3,2,1,0:T(8,128)} %copy-done.11, ...), custom_call_target="tpu_custom_call" | custom-call | tf_op jit(solution)/shard_map/pallas_call | solution.py:28
  136.3 10.0 %shard_map.74 = (f32[12,4,144,128]{3,2,1,0:T(8,128)S(1)}, f32[8,4,128,128]{3,2,1,0:T(8,128)S(1)}, f32[3,2,4,144,128]{4,3,2,1,0:T(8,128)S(1)}) custom-call(s32[1]{0:T(128)} %bitcast.me_ref, f32[4,4,144,128]{3,2,1,0:T(8,128)} %copy-done.5, f32[4,4,144,128]{3,2,1,0:T(8,128)S(1)} %get-tuple-element.55.a_ref, f32[4,4,144,128]{3,2,1,0:T(8,128)S(1)} %get-tuple-element.52.b_ref, ...), custom_call_target="tpu_custom_call" | custom-call | tf_op jit(solution)/shard_map/pallas_call | solution.py:28
  147.3 6.7 %shard_map.75 = (f32[2,4,128,128]{3,2,1,0:T(8,128)S(1)}, f32[2,4,128,128]{3,2,1,0:T(8,128)S(1)}, f32[2,4,128,128]{3,2,1,0:T(8,128)S(1)}, f32[2,4,128,128]{3,2,1,...) custom-call(s32[1]{0:T(128)} %bitcast.me_ref, ...), custom_call_target="tpu_custom_call" | custom-call | tf_op jit(solution)/shard_map/pallas_call | solution.py:28
  155.8 7.1 %collective-permute-start.24 = (f32[2,4,128,128]{3,2,1,0:T(8,128)S(1)}, f32[2,4,128,128]{3,2,1,0:T(8,128)S(1)}, u32[]{:S(2)}, u32[]{:S(2)}) collective-permute-start(f32[2,4,128,128]{3,2,1,0:T(8,128)S(1)} %get-tuple-element.65), channel_id=1, source_target_pairs={{6,0},{2,1},{4,2},{0,3},{7,4},{3,5},{5,6},{1,7},{14,8},{10,9},{12,... | collective-permute-start | bytes 1572872 | tf_op jit(solution)/shard_map/ppermute | solution.py:528
  163.9 14.0 %collective-permute-done.11 = f32[1,1]{1,0:T(1,128)} collective-permute-done((f32[1,1]{1,0:T(1,128)}, f32[1,1]{1,0:T(1,128)}, u32[]{:S(2)}, u32[]{:S(2)}) %collective-permute-start.11) | collective-permute-done | bytes 36 | tf_op jit(solution)/shard_map/ppermute | solution.py:435
  179.2 7.8 %collective-permute-start.12 = (f32[1,1]{1,0:T(1,128)}, f32[1,1]{1,0:T(1,128)}, u32[]{:S(2)}, u32[]{:S(2)}) collective-permute-start(f32[1,1]{1,0:T(1,128)} %add.19), channel_id=1, source_target_pairs={{0,4},{1,5},{2,6},{3,7},{4,0},{5,1},{6,2},{7,3},{8,12},{9,13},{10,... | collective-permute-start | bytes 20 | tf_op jit(solution)/shard_map/ppermute | solution.py:435
  190.0 3.8 %collective-permute-start.14 = (f32[1,1]{1,0:T(1,128)}, f32[1,1]{1,0:T(1,128)}, u32[]{:S(2)}, u32[]{:S(2)}) collective-permute-start(f32[1,1]{1,0:T(1,128)} %add.21), channel_id=1, source_target_pairs={{0,8},{1,9},{2,10},{3,11},{4,12},{5,13},{6,14},{7,15},{8,0},{9,1},... | collective-permute-start | bytes 20 | tf_op jit(solution)/shard_map/ppermute | solution.py:435
  194.8 4.4 %collective-permute-start.15 = (f32[1,1]{1,0:T(1,128)}, f32[1,1]{1,0:T(1,128)}, u32[]{:S(2)}, u32[]{:S(2)}) collective-permute-start(f32[1,1]{1,0:T(1,128)} %add.22), channel_id=1, source_target_pairs={{0,16},{1,17},{2,18},{3,19},{4,20},{5,21},{6,22},{7,23},{8,24},{9,... | collective-permute-start | bytes 20 | tf_op jit(solution)/shard_map/ppermute | solution.py:435
  205.3 8.4 %collective-permute-done.25.m3 = f32[2,4,128,128]{3,2,1,0:T(8,128)} collective-permute-done((f32[2,4,128,128]{3,2,1,0:T(8,128)S(1)}, f32[2,4,128,128]{3,2,1,0:T(8,128)}, u32[]{:S(2)}, u32[]{:S(2)}) %collective-permute-start.25) | collective-permute-done | bytes 524320 | tf_op jit(solution)/shard_map/ppermute | solution.py:528
  213.6 3.1 %shard_map.77 = f32[2,512,512]{2,1,0:T(8,128)} custom-call(s32[1]{0:T(128)} %bitcast.me_ref, f32[1,1]{1,0:T(1,128)} %bitcast.3.scale_ref, f32[2,4,128,128]{3,2,1,0:T(8,128)} %copy-done.13, f32[2,4,128,128]{3,2,1,0:T(8,128)} %copy-done.14, f32[2,4,128,128]{3,2,1,0:T(8,128)} %copy-done.15, f32[2,4,128,128]{3,2,1,0:T(8,128)} %collective-permute-done.25.m3), custom_call_target="tpu_custom_call" | custom-call | tf_op jit(solution)/shard_map/pallas_call | solution.py:28
  216.7 8.3 %collective-permute-done.20.m2 = f32[2,4,128,128]{3,2,1,0:T(8,128)} collective-permute-done((f32[2,4,128,128]{3,2,1,0:T(8,128)S(1)}, f32[2,4,128,128]{3,2,1,0:T(8,128)}, u32[]{:S(2)}, u32[]{:S(2)}) %collective-permute-start.20) | collective-permute-done | bytes 524320 | tf_op jit(solution)/shard_map/ppermute | solution.py:528
  225.0 5.9 %collective-permute-done.21.m3 = f32[2,4,128,128]{3,2,1,0:T(8,128)} collective-permute-done((f32[2,4,128,128]{3,2,1,0:T(8,128)S(1)}, f32[2,4,128,128]{3,2,1,0:T(8,128)}, u32[]{:S(2)}, u32[]{:S(2)}) %collective-permute-start.21) | collective-permute-done | bytes 524320 | tf_op jit(solution)/shard_map/ppermute | solution.py:528
  230.9 3.1 %shard_map.76 = f32[2,512,512]{2,1,0:T(8,128)} custom-call(s32[1]{0:T(128)} %bitcast.me_ref, f32[1,1]{1,0:T(1,128)} %bitcast.2.scale_ref, f32[2,4,128,128]{3,2,1,0:T(8,128)} %collective-permute-done.18.m0, f32[2,4,128,128]{3,2,1,0:T(8,128)} %collective-permute-done.19.m1, f32[2,4,128,128]{3,2,1,0:T(8,128)} %collective-permute-done.20.m2, ...), custom_call_target="tpu_custom_call" | custom-call | tf_op jit(solution)/shard_map/pallas_call | solution.py:28
  (71 shorter events, 34.4 us)
Async XLA Ops:
  3.2 29.0 %collective-permute-start.4 = (f32[2,2,4,144,128]{4,3,2,1,0:T(8,128)S(1)}, f32[2,2,4,144,128]{4,3,2,1,0:T(8,128)S(1)}, u32[]{:S(2)}, u32[]{:S(2)}) collective-permute-start(f32[2,2,4,144,128]{4,3,2,1,0:T(8,128)S(1)} %get-tuple-element.39), channel_id=1, source_target_pairs={{0,2},{1,6},{2,0},{3,4},{4,3},{5,7},{6,1},{7,5},{8,10},{9,14},{10,... | collective-permute-start | bytes 3538952 | tf_op jit(solution)/shard_map/ppermute | solution.py:463
  6.2 26.0 %collective-permute-start.5 = (f32[2,2,4,144,128]{4,3,2,1,0:T(8,128)S(1)}, f32[2,2,4,144,128]{4,3,2,1,0:T(8,128)S(1)}, u32[]{:S(2)}, u32[]{:S(2)}) collective-permute-start(f32[2,2,4,144,128]{4,3,2,1,0:T(8,128)S(1)} %get-tuple-element.40), channel_id=1, source_target_pairs={{0,0},{1,4},{2,2},{3,6},{4,1},{5,5},{6,3},{7,7},{8,8},{9,12},{10,1... | collective-permute-start | bytes 3538952 | tf_op jit(solution)/shard_map/ppermute | solution.py:463
  7.0 51.4 %collective-permute-start.7 = (f32[2,2,4,144,128]{4,3,2,1,0:T(8,128)S(1)}, f32[2,2,4,144,128]{4,3,2,1,0:T(8,128)S(1)}, u32[]{:S(2)}, u32[]{:S(2)}) collective-permute-start(f32[2,2,4,144,128]{4,3,2,1,0:T(8,128)S(1)} %get-tuple-element.41), channel_id=1, source_target_pairs={{0,6},{1,2},{2,4},{3,0},{4,7},{5,3},{6,5},{7,1},{8,14},{9,10},{10,... | collective-permute-start | bytes 3538952 | tf_op jit(solution)/shard_map/ppermute | solution.py:463
  10.9 48.3 %collective-permute-start.8 = (f32[2,2,4,144,128]{4,3,2,1,0:T(8,128)S(1)}, f32[2,2,4,144,128]{4,3,2,1,0:T(8,128)S(1)}, u32[]{:S(2)}, u32[]{:S(2)}) collective-permute-start(f32[2,2,4,144,128]{4,3,2,1,0:T(8,128)S(1)} %get-tuple-element.42), channel_id=1, source_target_pairs={{0,4},{1,0},{2,6},{3,2},{4,5},{5,1},{6,7},{7,3},{8,12},{9,8},{10,1... | collective-permute-start | bytes 3538952 | tf_op jit(solution)/shard_map/ppermute | solution.py:463
  63.2 17.2 %collective-permute-start.10 = (f32[2,4,4,144,128]{4,3,2,1,0:T(8,128)S(1)}, f32[2,4,4,144,128]{4,3,2,1,0:T(8,128)S(1)}, u32[]{:S(2)}, u32[]{:S(2)}) collective-permute-start(f32[2,4,4,144,128]{4,3,2,1,0:T(8,128)S(1)} %get-tuple-element.45.a_ref), channel_id=1, source_target_pairs={{0,1},{1,0},{2,3},{3,2},{4,5},{5,4},{6,7},{7,6},{8,9},{9,8},{10,11... | collective-permute-start | bytes 7077896 | tf_op jit(solution)/shard_map/ppermute | solution.py:478
  66.0 7.5 %collective-permute-start.9 = (f32[2,2,4,144,128]{4,3,2,1,0:T(8,128)S(1)}, f32[2,2,4,144,128]{4,3,2,1,0:T(8,128)S(1)}, u32[]{:S(2)}, u32[]{:S(2)}) collective-permute-start(f32[2,2,4,144,128]{4,3,2,1,0:T(8,128)S(1)} %get-tuple-element.43), channel_id=1, source_target_pairs={{1,8},{8,1},{3,10},{10,3},{5,12},{12,5},{7,14},{14,7},{9,16},{16,9... | collective-permute-start | bytes 3538952 | tf_op jit(solution)/shard_map/ppermute | solution.py:477
  68.4 25.7 %collective-permute-start.6 = (f32[2,2,4,144,128]{4,3,2,1,0:T(8,128)S(1)}, f32[2,2,4,144,128]{4,3,2,1,0:T(8,128)S(1)}, u32[]{:S(2)}, u32[]{:S(2)}) collective-permute-start(f32[2,2,4,144,128]{4,3,2,1,0:T(8,128)S(1)} %shard_map.69), channel_id=1, source_target_pairs={{1,8},{8,1},{3,10},{10,3},{5,12},{12,5},{7,14},{14,7},{9,16},{16,9... | collective-permute-start | bytes 3538952 | tf_op jit(solution)/shard_map/ppermute | solution.py:475
  71.7 29.6 %collective-permute-start = (f32[2,2,4,136,128]{4,3,2,1,0:T(8,128)S(1)}, f32[2,2,4,136,128]{4,3,2,1,0:T(8,128)S(1)}, u32[]{:S(2)}, u32[]{:S(2)}) collective-permute-start(f32[2,2,4,136,128]{4,3,2,1,0:T(8,128)S(1)} %get-tuple-element.35), channel_id=1, source_target_pairs={{0,2},{1,6},{2,0},{3,4},{4,3},{5,7},{6,1},{7,5},{8,10},{9,14},{10,... | collective-permute-start | bytes 3342344 | tf_op jit(solution)/shard_map/ppermute | solution.py:463
  72.8 28.6 %collective-permute-start.1 = (f32[2,2,4,136,128]{4,3,2,1,0:T(8,128)S(1)}, f32[2,2,4,136,128]{4,3,2,1,0:T(8,128)S(1)}, u32[]{:S(2)}, u32[]{:S(2)}) collective-permute-start(f32[2,2,4,136,128]{4,3,2,1,0:T(8,128)S(1)} %get-tuple-element.36), channel_id=1, source_target_pairs={{0,0},{1,4},{2,2},{3,6},{4,1},{5,5},{6,3},{7,7},{8,8},{9,12},{10,1... | collective-permute-start | bytes 3342344 | tf_op jit(solution)/shard_map/ppermute | solution.py:463
  73.5 49.6 %collective-permute-start.2 = (f32[2,2,4,136,128]{4,3,2,1,0:T(8,128)S(1)}, f32[2,2,4,136,128]{4,3,2,1,0:T(8,128)S(1)}, u32[]{:S(2)}, u32[]{:S(2)}) collective-permute-start(f32[2,2,4,136,128]{4,3,2,1,0:T(8,128)S(1)} %get-tuple-element.37), channel_id=1, source_target_pairs={{0,6},{1,2},{2,4},{3,0},{4,7},{5,3},{6,5},{7,1},{8,14},{9,10},{10,... | collective-permute-start | bytes 3342344 | tf_op jit(solution)/shard_map/ppermute | solution.py:463
  80.4 45.8 %collective-permute-start.3 = (f32[2,2,4,136,128]{4,3,2,1,0:T(8,128)S(1)}, f32[2,2,4,136,128]{4,3,2,1,0:T(8,128)S(1)}, u32[]{:S(2)}, u32[]{:S(2)}) collective-permute-start(f32[2,2,4,136,128]{4,3,2,1,0:T(8,128)S(1)} %get-tuple-element.38), channel_id=1, source_target_pairs={{0,4},{1,0},{2,6},{3,2},{4,5},{5,1},{6,7},{7,3},{8,12},{9,8},{10,1... | collective-permute-start | bytes 3342344 | tf_op jit(solution)/shard_map/ppermute | solution.py:463
  130.8 4.5 %collective-permute-start.17 = (f32[4,4,144,128]{3,2,1,0:T(8,128)S(1)}, f32[4,4,144,128]{3,2,1,0:T(8,128)S(1)}, u32[]{:S(2)}, u32[]{:S(2)}) collective-permute-start(f32[4,4,144,128]{3,2,1,0:T(8,128)S(1)} %get-tuple-element.55.a_ref), channel_id=1, source_target_pairs={{0,1},{1,0},{2,3},{3,2},{4,5},{5,4},{6,7},{7,6},{8,9},{9,8},{10,11... | collective-permute-start | bytes 3538952 | tf_op jit(solution)/shard_map/ppermute | solution.py:505
  132.8 13.5 %collective-permute-start.16 = (f32[4,4,144,128]{3,2,1,0:T(8,128)S(1)}, f32[4,4,144,128]{3,2,1,0:T(8,128)S(1)}, u32[]{:S(2)}, u32[]{:S(2)}) collective-permute-start(f32[4,4,144,128]{3,2,1,0:T(8,128)S(1)} %get-tuple-element.52.b_ref), channel_id=1, source_target_pairs={{1,8},{8,1},{3,10},{10,3},{5,12},{12,5},{7,14},{14,7},{9,16},{16,9... | collective-permute-start | bytes 3538952 | tf_op jit(solution)/shard_map/ppermute | solution.py:504
  154.0 46.5 %collective-permute-start.22 = (f32[2,4,128,128]{3,2,1,0:T(8,128)S(1)}, f32[2,4,128,128]{3,2,1,0:T(8,128)S(1)}, u32[]{:S(2)}, u32[]{:S(2)}) collective-permute-start(f32[2,4,128,128]{3,2,1,0:T(8,128)S(1)} %get-tuple-element.63), channel_id=1, source_target_pairs={{2,0},{6,1},{0,2},{4,3},{3,4},{7,5},{1,6},{5,7},{10,8},{14,9},{8,1... | collective-permute-start | bytes 1572872 | tf_op jit(solution)/shard_map/ppermute | solution.py:528
  155.1 46.9 %collective-permute-start.23 = (f32[2,4,128,128]{3,2,1,0:T(8,128)S(1)}, f32[2,4,128,128]{3,2,1,0:T(8,128)S(1)}, u32[]{:S(2)}, u32[]{:S(2)}) collective-permute-start(f32[2,4,128,128]{3,2,1,0:T(8,128)S(1)} %get-tuple-element.64), channel_id=1, source_target_pairs={{0,0},{4,1},{2,2},{6,3},{1,4},{5,5},{3,6},{7,7},{8,8},{12,9},{10,1... | collective-permute-start | bytes 1572872 | tf_op jit(solution)/shard_map/ppermute | solution.py:528
  155.8 48.6 %collective-permute-start.24 = (f32[2,4,128,128]{3,2,1,0:T(8,128)S(1)}, f32[2,4,128,128]{3,2,1,0:T(8,128)S(1)}, u32[]{:S(2)}, u32[]{:S(2)}) collective-permute-start(f32[2,4,128,128]{3,2,1,0:T(8,128)S(1)} %get-tuple-element.65), channel_id=1, source_target_pairs={{6,0},{2,1},{4,2},{0,3},{7,4},{3,5},{5,6},{1,7},{14,8},{10,9},{12,... | collective-permute-start | bytes 1572872 | tf_op jit(solution)/shard_map/ppermute | solution.py:528
  162.9 15.0 %collective-permute-start.11 = (f32[1,1]{1,0:T(1,128)}, f32[1,1]{1,0:T(1,128)}, u32[]{:S(2)}, u32[]{:S(2)}) collective-permute-start(f32[1,1]{1,0:T(1,128)} %get-tuple-element.51), channel_id=1, source_target_pairs={{0,2},{1,3},{2,0},{3,1},{4,6},{5,7},{6,4},{7,5},{8,10},{9,11},{10,... | collective-permute-start | bytes 20 | tf_op jit(solution)/shard_map/ppermute | solution.py:435
  179.2 8.1 %collective-permute-start.12 = (f32[1,1]{1,0:T(1,128)}, f32[1,1]{1,0:T(1,128)}, u32[]{:S(2)}, u32[]{:S(2)}) collective-permute-start(f32[1,1]{1,0:T(1,128)} %add.19), channel_id=1, source_target_pairs={{0,4},{1,5},{2,6},{3,7},{4,0},{5,1},{6,2},{7,3},{8,12},{9,13},{10,... | collective-permute-start | bytes 20 | tf_op jit(solution)/shard_map/ppermute | solution.py:435
  194.8 4.8 %collective-permute-start.15 = (f32[1,1]{1,0:T(1,128)}, f32[1,1]{1,0:T(1,128)}, u32[]{:S(2)}, u32[]{:S(2)}) collective-permute-start(f32[1,1]{1,0:T(1,128)} %add.22), channel_id=1, source_target_pairs={{0,16},{1,17},{2,18},{3,19},{4,20},{5,21},{6,22},{7,23},{8,24},{9,... | collective-permute-start | bytes 20 | tf_op jit(solution)/shard_map/ppermute | solution.py:435
  199.2 14.5 %collective-permute-start.25 = (f32[2,4,128,128]{3,2,1,0:T(8,128)S(1)}, f32[2,4,128,128]{3,2,1,0:T(8,128)}, u32[]{:S(2)}, u32[]{:S(2)}) collective-permute-start(f32[2,4,128,128]{3,2,1,0:T(8,128)S(1)} %get-tuple-element.66), channel_id=1, source_target_pairs={{4,0},{0,1},{6,2},{2,3},{5,4},{1,5},{7,6},{3,7},{12,8},{8,9},{14,1... | collective-permute-start | bytes 1572872 | tf_op jit(solution)/shard_map/ppermute | solution.py:528
  199.5 17.2 %collective-permute-start.18 = (f32[2,4,128,128]{3,2,1,0:T(8,128)S(1)}, f32[2,4,128,128]{3,2,1,0:T(8,128)}, u32[]{:S(2)}, u32[]{:S(2)}) collective-permute-start(f32[2,4,128,128]{3,2,1,0:T(8,128)S(1)} %get-tuple-element.59), channel_id=1, source_target_pairs={{2,0},{6,1},{0,2},{4,3},{3,4},{7,5},{1,6},{5,7},{10,8},{14,9},{8,1... | collective-permute-start | bytes 1572872 | tf_op jit(solution)/shard_map/ppermute | solution.py:528
  200.5 16.2 %collective-permute-start.19 = (f32[2,4,128,128]{3,2,1,0:T(8,128)S(1)}, f32[2,4,128,128]{3,2,1,0:T(8,128)}, u32[]{:S(2)}, u32[]{:S(2)}) collective-permute-start(f32[2,4,128,128]{3,2,1,0:T(8,128)S(1)} %get-tuple-element.60), channel_id=1, source_target_pairs={{0,0},{4,1},{2,2},{6,3},{1,4},{5,5},{3,6},{7,7},{8,8},{12,9},{10,1... | collective-permute-start | bytes 1572872 | tf_op jit(solution)/shard_map/ppermute | solution.py:528
  202.0 23.1 %collective-permute-start.20 = (f32[2,4,128,128]{3,2,1,0:T(8,128)S(1)}, f32[2,4,128,128]{3,2,1,0:T(8,128)}, u32[]{:S(2)}, u32[]{:S(2)}) collective-permute-start(f32[2,4,128,128]{3,2,1,0:T(8,128)S(1)} %get-tuple-element.61), channel_id=1, source_target_pairs={{6,0},{2,1},{4,2},{0,3},{7,4},{3,5},{5,6},{1,7},{14,8},{10,9},{12,... | collective-permute-start | bytes 1572872 | tf_op jit(solution)/shard_map/ppermute | solution.py:528
  204.4 26.5 %collective-permute-start.21 = (f32[2,4,128,128]{3,2,1,0:T(8,128)S(1)}, f32[2,4,128,128]{3,2,1,0:T(8,128)}, u32[]{:S(2)}, u32[]{:S(2)}) collective-permute-start(f32[2,4,128,128]{3,2,1,0:T(8,128)S(1)} %get-tuple-element.62), channel_id=1, source_target_pairs={{4,0},{0,1},{6,2},{2,3},{5,4},{1,5},{7,6},{3,7},{12,8},{8,9},{14,1... | collective-permute-start | bytes 1572872 | tf_op jit(solution)/shard_map/ppermute | solution.py:528
  (18 other events, 159.7 us)

commit v4 on v3

--- a/solution.py
+++ b/solution.py
@@ -20,18 +20,19 @@
 
 VM = pl.BlockSpec(memory_space=pltpu.VMEM)
 SM = pl.BlockSpec(memory_space=pltpu.SMEM)
-PARAMS = pltpu.CompilerParams(vmem_limit_bytes=14 * 1024 * 1024)
+ANY = pl.BlockSpec(memory_space=pl.ANY)
+SHARE = {"forward_main": 30, "forward_wedge": 30, "backward_main": 14}
 F32 = jnp.float32
 
 
-def call(kernel, outs, scalars, arrays, scratch=(), total=False, **options):
+def call(kernel, name, outs, scalars, arrays, scratch=(), total=False, far=0, **options):
     return pl.pallas_call(
         kernel,
         out_shape=outs,
-        in_specs=[SM] * len(scalars) + [VM] * len(arrays),
+        in_specs=[SM] * len(scalars) + [ANY] * far + [VM] * (len(arrays) - far),
         out_specs=[VM] * (len(outs) - total) + [SM] * total,
         scratch_shapes=scratch,
-        compiler_params=PARAMS,
+        compiler_params=pltpu.CompilerParams(vmem_limit_bytes=SHARE.get(name, 14) << 20),
         **options,
     )(*scalars, *arrays)
 
@@ -252,28 +253,32 @@
         spans(half, half + k + 1, lambda s, c: plane(s, c, True))
 
 
-def resid_kernel(me_ref, m0, m1, m2, m3, u_ref, a_ref, b_ref, total_ref, acc_ref):
+def resid_kernel(me_ref, f0, f1, f2, f3, u_ref, a_ref, b_ref, total_ref, acc_ref, near, sems):
     me = me_ref[0]
-    planes, blocks, short = m0.shape[1:4]
+    copies = [pltpu.make_async_copy(f, near.at[n], sems.at[n]) for n, f in enumerate((f0, f1, f2, f3))]
+    for copy in copies:
+        copy.start()
+    planes, blocks, short = near.shape[2:5]
     rows = u_ref.shape[2]
     rim = (rows - short) // 2
     shape = (blocks, HALO, LANES)
     row = lax.broadcasted_iota(jnp.int32, shape, 1)
     acc_ref[...] = jnp.zeros(shape, F32)
-    for r, m in zip(ROUNDS, (m0, m1, m2, m3)):
+    for n, r in enumerate(ROUNDS):
+        copies[n].wait()
         for i in range(planes):
             block, at = slot(me, r, planes, i)
             for flag, dst in ((1, a_ref), (0, b_ref)):
 
                 @pl.when(block == flag)
-                def _(m=m, i=i, at=at, dst=dst, flag=flag):
-                    acc = acc_ref[...]
+                def _(n=n, i=i, at=at, dst=dst, flag=flag):
                     dst[at, :, :rim, :] = jnp.zeros((blocks, rim, LANES), F32)
                     dst[at, :, rows - rim :, :] = jnp.zeros((blocks, rim, LANES), F32)
+                    acc = jnp.zeros(shape, F32)
                     for lo in range(0, short, HALO):
                         here = slice(lo + rim, lo + rim + HALO)
-                        resid = u_ref[2 * planes * flag + at, :, here, :] - m[0, i, :, lo : lo + HALO, :]
-                        weighted = m[1, i, :, lo : lo + HALO, :] * resid
+                        resid = u_ref[2 * planes * flag + at, :, here, :] - near[n, 0, i, :, lo : lo + HALO, :]
+                        weighted = near[n, 1, i, :, lo : lo + HALO, :] * resid
                         dst[at, :, here, :] = weighted
                         share = weighted * resid
                         if lo + rim < HALO:
@@ -281,7 +286,7 @@
                         if lo + rim + HALO > rows - HALO:
                             share = jnp.where(row < HALO - rim, share, 0.0)
                         acc = acc + share
-                    acc_ref[...] = acc
+                    acc_ref[...] = acc_ref[...] + acc
 
     total_ref[0, 0] = jnp.sum(acc_ref[...])
 
@@ -415,15 +420,26 @@
                     outs[4 + n][i] = l_src[half + at, :, HALO : rows - HALO, :]
 
 
-def home_kernel(me_ref, scale_ref, m0, m1, m2, m3, out):
+def home_kernel(rounds, me_ref, scale_ref, *refs):
+    count = len(rounds)
+    msgs, (out, near, ready, sems, done) = refs[:count], refs[-5:]
     _, x, c = bits(me_ref[0])
-    planes, blocks, rows = m0.shape[:3]
+    planes, blocks, rows = near.shape[1:4]
     scale = scale_ref[0, 0]
-    for (r1, r0), m in zip(ROUNDS, (m0, m1, m2, m3)):
+    come = [pltpu.make_async_copy(m, near.at[n], sems.at[n]) for n, m in enumerate(msgs)]
+    for copy in come:
+        copy.start()
+    go = []
+    for n, (r1, r0) in enumerate(rounds):
         start = pl.multiple_of(part(c ^ r1, x ^ r0) * rows, 8)
+        come[n].wait()
         for i in range(planes):
             for b in range(blocks):
-                out[i, pl.ds(start, rows), b * LANES : (b + 1) * LANES] = m[i, b] * scale
+                ready[n, i, :, b * LANES : (b + 1) * LANES] = near[n, i, b] * scale
+        go.append(pltpu.make_async_copy(ready.at[n], out.at[:, pl.ds(start, rows), :], done.at[n]))
+        go[-1].start()
+    for copy in go:
+        copy.wait()
 
 
 def shape(*dims):
@@ -455,30 +471,31 @@
             if i + GROUP - 1 < count:
                 beyond += [(i, i + GROUP - 1), (i + GROUP - 1, i)]
 
-    def regroup(a, b, rim):
+    def regroup(a, b, rim, name):
         message = shape(2, planes, blocks, rows + 2 * rim, LANES)
-        msgs = call(partial(pack_kernel, rim), [message] * 4, [me], [a, b])
+        msgs = call(partial(pack_kernel, rim), name, [message] * 4, [me], [a, b])
         got = []
         for m, r in zip(msgs, ROUNDS):
             got.append(lax.ppermute(m, axis, send_pairs(count, *r)))
         return outside(*got)
 
-    first = regroup(*outside(initial_field, coefficient), HALO)
-    second = regroup(*outside(observed, misfit_weight), HALO - ITERS)
+    first = regroup(*outside(initial_field, coefficient), HALO, "pack_state")
+    second = regroup(*outside(observed, misfit_weight), HALO - ITERS, "pack_data")
 
     plane_set = (blocks, tall, LANES)
     padded = (blocks, tall + 2 * HALO, LANES)
     inner = (blocks, rows, LANES)
     saved_shape = shape(ITERS - 1, 2, *plane_set)
     quarter = shape(2, planes, *plane_set)
-    (early,) = call(early_kernel, [quarter], [me], first[:2])
+    (early,) = call(early_kernel, "early", [quarter], [me], first[:2])
     early = lax.ppermute(early, axis, beyond)
-    late, blk_a, blk_b = call(place_kernel, [quarter] + [shape(2, half, *plane_set)] * 2, [me], first)
+    late, blk_a, blk_b = call(place_kernel, "place", [quarter] + [shape(2, half, *plane_set)] * 2, [me], first)
     late = lax.ppermute(late, axis, beyond)
     far_a = lax.ppermute(blk_a, axis, partner)
     far_a, early, late = outside(far_a, early, late)
     final, coef, slopes, saved = call(
         forward_main,
+        "forward_main",
         [shape(2 * half, *plane_set), shape(3 * half, *plane_set), shape(ITERS, 2 * half, *plane_set), saved_shape],
         [me],
         inside(blk_a, blk_b) + [far_a],
@@ -486,6 +503,7 @@
     )
     final, slopes, far_coef = call(
         forward_wedge,
+        "forward_wedge",
         [shape(2 * half, *plane_set), shape(ITERS, 2 * half, *plane_set), shape(half, *plane_set)],
         [me],
         [early, late] + inside(blk_b, coef, saved, final, slopes),
@@ -495,11 +513,17 @@
 
     lam_a, lam_b, part_total = call(
         resid_kernel,
+        "resid",
         [shape(half, *plane_set)] * 2 + [jax.ShapeDtypeStruct((1, 1), F32)],
         [me],
         second + inside(final),
-        [pltpu.VMEM((blocks, HALO, LANES), F32)],
+        [
+            pltpu.VMEM((blocks, HALO, LANES), F32),
+            pltpu.VMEM((4,) + second[0].shape, F32),
+            pltpu.SemaphoreType.DMA((4,)),
+        ],
         total=True,
+        far=4,
     )
     far_lb = lax.ppermute(lam_b, axis, beyond)
     far_la = lax.ppermute(lam_a, axis, partner)
@@ -508,6 +532,7 @@
     part_total = exchange_sum(part_total, axis, count, [2])
     lam, grad, saved = call(
         backward_main,
+        "backward_main",
         [shape(3 * half, *plane_set), shape(2 * half, *inner), saved_shape],
         [me],
         [far_la] + inside(lam_a, lam_b, coef, slopes),
@@ -516,6 +541,7 @@
     part_total = exchange_sum(part_total, axis, count, [4])
     outs = call(
         backward_wedge,
+        "backward_wedge",
         [shape(planes, *inner)] * 8,
         [me],
         [far_lb] + inside(lam_b, far_coef, coef, slopes, saved, lam, grad),
@@ -535,9 +561,28 @@
     cells = count * planes * height * width
     misfit = jnp.sqrt(total[0, 0] / cells + 1e-06)
     inverse = 1.0 / misfit
-    whole = [jax.ShapeDtypeStruct((planes, height, width), F32)]
-    (gradient,) = call(home_kernel, whole, [me, (time_step * inverse).reshape(1, 1)], back[:4])
-    (adjoint,) = call(home_kernel, whole, [me, inverse.reshape(1, 1)], back[4:])
+
+    def assemble(scale, msgs):
+        held = ()
+        for n in range(0, 4, 2):
+            held = pl.pallas_call(
+                partial(home_kernel, ROUNDS[n : n + 2]),
+                out_shape=[jax.ShapeDtypeStruct((planes, height, width), F32)],
+                in_specs=[SM, SM, ANY, ANY] + [ANY] * len(held),
+                out_specs=[ANY],
+                scratch_shapes=[
+                    pltpu.VMEM((2, planes, *inner), F32),
+                    pltpu.VMEM((2, planes, rows, width), F32),
+                    pltpu.SemaphoreType.DMA((2,)),
+                    pltpu.SemaphoreType.DMA((2,)),
+                ],
+                input_output_aliases={4: 0} if held else {},
+                compiler_params=pltpu.CompilerParams(vmem_limit_bytes=14 << 20),
+            )(me, scale.reshape(1, 1), *msgs[n : n + 2], *held)
+        return held[0]
+
+    gradient = assemble(time_step * inverse, back[:4])
+    adjoint = assemble(inverse, back[4:])
     return gradient, adjoint, misfit
 
 

time: 236 us -> 233 us (0.987)
  waiting for transfers between devices: 113 us -> 109 us
    ppermute x8, waiting for transfers between devices: 22.6 us -> 19.3 us  [on_device(): lax.ppermute(m, axis, [(j, i) for i, j in send_pairs(count, *r)])]
    pallas_call x11 -> x13, Pallas kernels: 51.5 us -> 53.3 us  [the longest x9 44.9 us: call(): pl.pallas_call(kernel, out_shape=outs, in_specs=[SM] * len(scalars) + [AN...]
    unnamed x32 -> x24, local copies, waits for them, and re-layouts: 5.49 us -> 4.41 us
  transfers between devices with their start and end apart: 26 -> 26, of which waited for: 14 -> 14; matrix products, arithmetic and copies ran while one was open for 0% -> 0% of each run, Pallas kernels for 14% -> 16%
where the time goes in v4:
time: 233 us; the launch traced here: 232 us
  waiting for transfers between devices  109 us (47%)
  starting transfers between devices  59.6 us (26%)
  Pallas kernels  53.3 us (23%)
  between operations  6.13 us (3%)
  local copies, waits for them, and re-layouts  4.41 us (2%)
    ppermute x8, waiting for transfers between devices, regroup(): got.append(lax.ppermute(m, axis, send_pairs(count, *r)))  73.1 us
    pallas_call x9, Pallas kernels, call(): pl.pallas_call(kernel, out_shape=outs, in_specs=[SM] * len(scalars) + [AN...  44.9 us
    ppermute x8, starting transfers between devices, regroup(): got.append(lax.ppermute(m, axis, send_pairs(count, *r)))  20.7 us
    ppermute x8, waiting for transfers between devices, on_device(): lax.ppermute(m, axis, [(j, i) for i, j in send_pairs(count, *r)])  19.3 us
    ppermute x5, starting transfers between devices, exchange_sum(): lax.ppermute(value, axis, [(i, i ^ step) for i in range(count)])  17.9 us
    ppermute x5, waiting for transfers between devices, exchange_sum(): lax.ppermute(value, axis, [(i, i ^ step) for i in range(count)])  14.7 us
    ppermute x8, starting transfers between devices, on_device(): lax.ppermute(m, axis, [(j, i) for i, j in send_pairs(count, *r)])  13.9 us
    pallas_call x4, Pallas kernels, assemble(): pl.pallas_call(partial(home_kernel, ROUNDS[n:n + 2]), out_shape=[jax.Shap...  8.38 us
  transfers between devices with their start and end apart: 26, of which 14 were waited for; matrix products, arithmetic and copies ran while one was open for 0% of the time, Pallas kernels for 16%

profile of v4, /device:TPU:0, one launch (start us, length us, event | category | flops | bytes accessed | tf_op | source)
XLA Modules:
  0.0 232.3 jit_solution(11684756333363858218)
XLA Ops:
  3.2 3.0 %collective-permute-start.4 = (f32[2,2,4,144,128]{4,3,2,1,0:T(8,128)S(1)}, f32[2,2,4,144,128]{4,3,2,1,0:T(8,128)S(1)}, u32[]{:S(2)}, u32[]{:S(2)}) collective-permute-start(f32[2,2,4,144,128]{4,3,2,1,0:T(8,128)S(1)} %get-tuple-element.39), channel_id=1, source_target_pairs={{0,2},{1,6},{2,0},{3,4},{4,3},{5,7},{6,1},{7,5},{8,10},{9,14},{10,... | collective-permute-start | bytes 3538952 | tf_op jit(solution)/shard_map/ppermute | solution.py:479
  7.0 3.9 %collective-permute-start.7 = (f32[2,2,4,144,128]{4,3,2,1,0:T(8,128)S(1)}, f32[2,2,4,144,128]{4,3,2,1,0:T(8,128)S(1)}, u32[]{:S(2)}, u32[]{:S(2)}) collective-permute-start(f32[2,2,4,144,128]{4,3,2,1,0:T(8,128)S(1)} %get-tuple-element.41), channel_id=1, source_target_pairs={{0,6},{1,2},{2,4},{3,0},{4,7},{5,3},{6,5},{7,1},{8,14},{9,10},{10,... | collective-permute-start | bytes 3538952 | tf_op jit(solution)/shard_map/ppermute | solution.py:479
  10.9 21.3 %collective-permute-done.4.m0 = f32[2,2,4,144,128]{4,3,2,1,0:T(8,128)S(1)} collective-permute-done((f32[2,2,4,144,128]{4,3,2,1,0:T(8,128)S(1)}, f32[2,2,4,144,128]{4,3,2,1,0:T(8,128)S(1)}, u32[]{:S(2)}, u32[]{:S(2)}) %collective-permute-start.4) | collective-permute-done | bytes 1179680 | tf_op jit(solution)/shard_map/ppermute | solution.py:479
  32.2 26.2 %collective-permute-done.7.m2 = f32[2,2,4,144,128]{4,3,2,1,0:T(8,128)S(1)} collective-permute-done((f32[2,2,4,144,128]{4,3,2,1,0:T(8,128)S(1)}, f32[2,2,4,144,128]{4,3,2,1,0:T(8,128)S(1)}, u32[]{:S(2)}, u32[]{:S(2)}) %collective-permute-start.7) | collective-permute-done | bytes 1179680 | tf_op jit(solution)/shard_map/ppermute | solution.py:479
  60.4 2.7 %shard_map.70 = (f32[2,2,4,144,128]{4,3,2,1,0:T(8,128)S(1)}, f32[2,4,4,144,128]{4,3,2,1,0:T(8,128)S(1)}, f32[2,4,4,144,128]{4,3,2,1,0:T(8,128)S(1)}) custom-call(s32[1]{0:T(128)} %bitcast.me_ref, f32[2,2,4,144,128]{4,3,2,1,0:T(8,128)} %copy-done, f32[2,2,4,144,128]{4,3,2,1,0:T(8,128)} %copy-done.1, f32[2,2,4,144,128]{4,3,2,1,0:T(8,128)} %copy-done.6, ...), custom_call_target="tpu_custom_call" | custom-call | tf_op jit(solution)/shard_map/pallas_call | solution.py:29
  63.2 2.8 %collective-permute-start.10 = (f32[2,4,4,144,128]{4,3,2,1,0:T(8,128)S(1)}, f32[2,4,4,144,128]{4,3,2,1,0:T(8,128)S(1)}, u32[]{:S(2)}, u32[]{:S(2)}) collective-permute-start(f32[2,4,4,144,128]{4,3,2,1,0:T(8,128)S(1)} %get-tuple-element.45.a_ref), channel_id=1, source_target_pairs={{0,1},{1,0},{2,3},{3,2},{4,5},{5,4},{6,7},{7,6},{8,9},{9,8},{10,11... | collective-permute-start | bytes 7077896 | tf_op jit(solution)/shard_map/ppermute | solution.py:494
  74.4 6.0 %collective-permute-start.2 = (f32[2,2,4,136,128]{4,3,2,1,0:T(8,128)S(1)}, f32[2,2,4,136,128]{4,3,2,1,0:T(8,128)}, u32[]{:S(2)}, u32[]{:S(2)}) collective-permute-start(f32[2,2,4,136,128]{4,3,2,1,0:T(8,128)S(1)} %get-tuple-element.37), channel_id=1, source_target_pairs={{0,6},{1,2},{2,4},{3,0},{4,7},{5,3},{6,5},{7,1},{8,14},{9,10},{10,... | collective-permute-start | bytes 3342344 | tf_op jit(solution)/shard_map/ppermute | solution.py:479
  80.4 4.3 %collective-permute-start.3 = (f32[2,2,4,136,128]{4,3,2,1,0:T(8,128)S(1)}, f32[2,2,4,136,128]{4,3,2,1,0:T(8,128)}, u32[]{:S(2)}, u32[]{:S(2)}) collective-permute-start(f32[2,2,4,136,128]{4,3,2,1,0:T(8,128)S(1)} %get-tuple-element.38), channel_id=1, source_target_pairs={{0,4},{1,0},{2,6},{3,2},{4,5},{5,1},{6,7},{7,3},{8,12},{9,8},{10,1... | collective-permute-start | bytes 3342344 | tf_op jit(solution)/shard_map/ppermute | solution.py:479
  84.7 9.5 %shard_map.71 = (f32[8,4,144,128]{3,2,1,0:T(8,128)S(1)}, f32[12,4,144,128]{3,2,1,0:T(8,128)S(1)}, f32[4,8,4,144,128]{4,3,2,1,0:T(8,128)S(1)}, f32[3,2,4,144,128]{4,3,2,1,0:T(8,128)S(1)}) custom-call(s32[1]{0:T(128)} %bitcast.me_ref, f32[2,4,4,144,128]{4,3,2,1,0:T(8,128)S(1)} %get-tuple-element.45.a_ref, f32[2,4,4,144,128]{4,3,2,1,0:T(8,128)S(1)} %get-tuple-element.44.b_ref, ...), custom_call_target="tpu_custom_call" | custom-call | tf_op jit(solution)/shard_map/pallas_call | solution.py:29
  95.2 6.2 %shard_map.72 = (f32[8,4,144,128]{3,2,1,0:T(8,128)S(1)}, f32[4,8,4,144,128]{4,3,2,1,0:T(8,128)S(1)}, f32[4,4,144,128]{3,2,1,0:T(8,128)S(1)}) custom-call(s32[1]{0:T(128)} %bitcast.me_ref, f32[2,2,4,144,128]{4,3,2,1,0:T(8,128)} %copy-done.4, f32[2,2,4,144,128]{4,3,2,1,0:T(8,128)} %copy-done.3, ...), custom_call_target="tpu_custom_call", output_to_operand_aliasing={{0}: (6, {}), {1}: (7, {})} | custom-call | tf_op jit(solution)/shard_map/pallas_call | solution.py:29
  101.4 21.8 %collective-permute-done.2.f2 = f32[2,2,4,136,128]{4,3,2,1,0:T(8,128)} collective-permute-done((f32[2,2,4,136,128]{4,3,2,1,0:T(8,128)S(1)}, f32[2,2,4,136,128]{4,3,2,1,0:T(8,128)}, u32[]{:S(2)}, u32[]{:S(2)}) %collective-permute-start.2) | collective-permute-done | bytes 1114144 | tf_op jit(solution)/shard_map/ppermute | solution.py:479
  123.2 3.0 %collective-permute-done.3.f3 = f32[2,2,4,136,128]{4,3,2,1,0:T(8,128)} collective-permute-done((f32[2,2,4,136,128]{4,3,2,1,0:T(8,128)S(1)}, f32[2,2,4,136,128]{4,3,2,1,0:T(8,128)}, u32[]{:S(2)}, u32[]{:S(2)}) %collective-permute-start.3) | collective-permute-done | bytes 1114144 | tf_op jit(solution)/shard_map/ppermute | solution.py:479
  126.3 3.0 %shard_map.73 = (f32[4,4,144,128]{3,2,1,0:T(8,128)S(1)}, f32[4,4,144,128]{3,2,1,0:T(8,128)S(1)}, f32[1,1]{1,0:T(1,128)}) custom-call(s32[1]{0:T(128)} %bitcast.me_ref, f32[2,2,4,136,128]{4,3,2,1,0:T(8,128)} %collective-permute-done.f0, f32[2,2,4,136,128]{4,3,2,1,0:T(8,128)} %collective-permute-done.1.f1, f32[2,2,4,136,128]{4,3,2,1,0:T(8,128)} %collective-permute-done.2.f2, ...), custom_call_target="tpu_custom_call" | custom-call | tf_op jit(solution)/shard_map/pallas_call | solution.py:29
  134.9 10.0 %shard_map.74 = (f32[12,4,144,128]{3,2,1,0:T(8,128)S(1)}, f32[8,4,128,128]{3,2,1,0:T(8,128)S(1)}, f32[3,2,4,144,128]{4,3,2,1,0:T(8,128)S(1)}) custom-call(s32[1]{0:T(128)} %bitcast.me_ref, f32[4,4,144,128]{3,2,1,0:T(8,128)} %copy-done.5, f32[4,4,144,128]{3,2,1,0:T(8,128)S(1)} %get-tuple-element.55.a_ref, f32[4,4,144,128]{3,2,1,0:T(8,128)S(1)} %get-tuple-element.52.b_ref, ...), custom_call_target="tpu_custom_call" | custom-call | tf_op jit(solution)/shard_map/pallas_call | solution.py:29
  146.0 6.7 %shard_map.75 = (f32[2,4,128,128]{3,2,1,0:T(8,128)S(1)}, f32[2,4,128,128]{3,2,1,0:T(8,128)S(1)}, f32[2,4,128,128]{3,2,1,0:T(8,128)S(1)}, f32[2,4,128,128]{3,2,1,...) custom-call(s32[1]{0:T(128)} %bitcast.me_ref, ...), custom_call_target="tpu_custom_call" | custom-call | tf_op jit(solution)/shard_map/pallas_call | solution.py:29
  154.4 7.1 %collective-permute-start.22 = (f32[2,4,128,128]{3,2,1,0:T(8,128)S(1)}, f32[2,4,128,128]{3,2,1,0:T(8,128)S(1)}, u32[]{:S(2)}, u32[]{:S(2)}) collective-permute-start(f32[2,4,128,128]{3,2,1,0:T(8,128)S(1)} %get-tuple-element.63), channel_id=1, source_target_pairs={{6,0},{2,1},{4,2},{0,3},{7,4},{3,5},{5,6},{1,7},{14,8},{10,9},{12,... | collective-permute-start | bytes 1572872 | tf_op jit(solution)/shard_map/ppermute | solution.py:554
  162.5 13.8 %collective-permute-done.11 = f32[1,1]{1,0:T(1,128)} collective-permute-done((f32[1,1]{1,0:T(1,128)}, f32[1,1]{1,0:T(1,128)}, u32[]{:S(2)}, u32[]{:S(2)}) %collective-permute-start.11) | collective-permute-done | bytes 36 | tf_op jit(solution)/shard_map/ppermute | solution.py:451
  177.7 7.8 %collective-permute-start.12 = (f32[1,1]{1,0:T(1,128)}, f32[1,1]{1,0:T(1,128)}, u32[]{:S(2)}, u32[]{:S(2)}) collective-permute-start(f32[1,1]{1,0:T(1,128)} %add.19), channel_id=1, source_target_pairs={{0,4},{1,5},{2,6},{3,7},{4,0},{5,1},{6,2},{7,3},{8,12},{9,13},{10,... | collective-permute-start | bytes 20 | tf_op jit(solution)/shard_map/ppermute | solution.py:451
  188.2 3.8 %collective-permute-start.14 = (f32[1,1]{1,0:T(1,128)}, f32[1,1]{1,0:T(1,128)}, u32[]{:S(2)}, u32[]{:S(2)}) collective-permute-start(f32[1,1]{1,0:T(1,128)} %add.21), channel_id=1, source_target_pairs={{0,8},{1,9},{2,10},{3,11},{4,12},{5,13},{6,14},{7,15},{8,0},{9,1},... | collective-permute-start | bytes 20 | tf_op jit(solution)/shard_map/ppermute | solution.py:451
  192.9 4.4 %collective-permute-start.15 = (f32[1,1]{1,0:T(1,128)}, f32[1,1]{1,0:T(1,128)}, u32[]{:S(2)}, u32[]{:S(2)}) collective-permute-start(f32[1,1]{1,0:T(1,128)} %add.22), channel_id=1, source_target_pairs={{0,16},{1,17},{2,18},{3,19},{4,20},{5,21},{6,22},{7,23},{8,24},{9,... | collective-permute-start | bytes 20 | tf_op jit(solution)/shard_map/ppermute | solution.py:451
  200.0 2.6 %collective-permute-start.18 = (f32[2,4,128,128]{3,2,1,0:T(8,128)S(1)}, f32[2,4,128,128]{3,2,1,0:T(8,128)}, u32[]{:S(2)}, u32[]{:S(2)}) collective-permute-start(f32[2,4,128,128]{3,2,1,0:T(8,128)S(1)} %get-tuple-element.59), channel_id=1, source_target_pairs={{6,0},{2,1},{4,2},{0,3},{7,4},{3,5},{5,6},{1,7},{14,8},{10,9},{12,... | collective-permute-start | bytes 1572872 | tf_op jit(solution)/shard_map/ppermute | solution.py:554
  205.5 6.2 %collective-permute-done.23.refs_1_ = f32[2,4,128,128]{3,2,1,0:T(8,128)} collective-permute-done((f32[2,4,128,128]{3,2,1,0:T(8,128)S(1)}, f32[2,4,128,128]{3,2,1,0:T(8,128)}, u32[]{:S(2)}, u32[]{:S(2)}) %collective-permute-start.23) | collective-permute-done | bytes 524320 | tf_op jit(solution)/shard_map/ppermute | solution.py:554
  216.0 7.2 %collective-permute-done.18.refs_0_ = f32[2,4,128,128]{3,2,1,0:T(8,128)} collective-permute-done((f32[2,4,128,128]{3,2,1,0:T(8,128)S(1)}, f32[2,4,128,128]{3,2,1,0:T(8,128)}, u32[]{:S(2)}, u32[]{:S(2)}) %collective-permute-start.18) | collective-permute-done | bytes 524320 | tf_op jit(solution)/shard_map/ppermute | solution.py:554
  223.2 5.9 %collective-permute-done.19.refs_1_ = f32[2,4,128,128]{3,2,1,0:T(8,128)} collective-permute-done((f32[2,4,128,128]{3,2,1,0:T(8,128)S(1)}, f32[2,4,128,128]{3,2,1,0:T(8,128)}, u32[]{:S(2)}, u32[]{:S(2)}) %collective-permute-start.19) | collective-permute-done | bytes 524320 | tf_op jit(solution)/shard_map/ppermute | solution.py:554
  (65 shorter events, 37.0 us)
Async XLA Ops:
  3.2 29.0 %collective-permute-start.4 = (f32[2,2,4,144,128]{4,3,2,1,0:T(8,128)S(1)}, f32[2,2,4,144,128]{4,3,2,1,0:T(8,128)S(1)}, u32[]{:S(2)}, u32[]{:S(2)}) collective-permute-start(f32[2,2,4,144,128]{4,3,2,1,0:T(8,128)S(1)} %get-tuple-element.39), channel_id=1, source_target_pairs={{0,2},{1,6},{2,0},{3,4},{4,3},{5,7},{6,1},{7,5},{8,10},{9,14},{10,... | collective-permute-start | bytes 3538952 | tf_op jit(solution)/shard_map/ppermute | solution.py:479
  6.2 26.0 %collective-permute-start.5 = (f32[2,2,4,144,128]{4,3,2,1,0:T(8,128)S(1)}, f32[2,2,4,144,128]{4,3,2,1,0:T(8,128)S(1)}, u32[]{:S(2)}, u32[]{:S(2)}) collective-permute-start(f32[2,2,4,144,128]{4,3,2,1,0:T(8,128)S(1)} %get-tuple-element.40), channel_id=1, source_target_pairs={{0,0},{1,4},{2,2},{3,6},{4,1},{5,5},{6,3},{7,7},{8,8},{9,12},{10,1... | collective-permute-start | bytes 3538952 | tf_op jit(solution)/shard_map/ppermute | solution.py:479
  7.0 51.4 %collective-permute-start.7 = (f32[2,2,4,144,128]{4,3,2,1,0:T(8,128)S(1)}, f32[2,2,4,144,128]{4,3,2,1,0:T(8,128)S(1)}, u32[]{:S(2)}, u32[]{:S(2)}) collective-permute-start(f32[2,2,4,144,128]{4,3,2,1,0:T(8,128)S(1)} %get-tuple-element.41), channel_id=1, source_target_pairs={{0,6},{1,2},{2,4},{3,0},{4,7},{5,3},{6,5},{7,1},{8,14},{9,10},{10,... | collective-permute-start | bytes 3538952 | tf_op jit(solution)/shard_map/ppermute | solution.py:479
  10.9 48.3 %collective-permute-start.8 = (f32[2,2,4,144,128]{4,3,2,1,0:T(8,128)S(1)}, f32[2,2,4,144,128]{4,3,2,1,0:T(8,128)S(1)}, u32[]{:S(2)}, u32[]{:S(2)}) collective-permute-start(f32[2,2,4,144,128]{4,3,2,1,0:T(8,128)S(1)} %get-tuple-element.42), channel_id=1, source_target_pairs={{0,4},{1,0},{2,6},{3,2},{4,5},{5,1},{6,7},{7,3},{8,12},{9,8},{10,1... | collective-permute-start | bytes 3538952 | tf_op jit(solution)/shard_map/ppermute | solution.py:479
  63.2 17.2 %collective-permute-start.10 = (f32[2,4,4,144,128]{4,3,2,1,0:T(8,128)S(1)}, f32[2,4,4,144,128]{4,3,2,1,0:T(8,128)S(1)}, u32[]{:S(2)}, u32[]{:S(2)}) collective-permute-start(f32[2,4,4,144,128]{4,3,2,1,0:T(8,128)S(1)} %get-tuple-element.45.a_ref), channel_id=1, source_target_pairs={{0,1},{1,0},{2,3},{3,2},{4,5},{5,4},{6,7},{7,6},{8,9},{9,8},{10,11... | collective-permute-start | bytes 7077896 | tf_op jit(solution)/shard_map/ppermute | solution.py:494
  66.0 8.4 %collective-permute-start.9 = (f32[2,2,4,144,128]{4,3,2,1,0:T(8,128)S(1)}, f32[2,2,4,144,128]{4,3,2,1,0:T(8,128)S(1)}, u32[]{:S(2)}, u32[]{:S(2)}) collective-permute-start(f32[2,2,4,144,128]{4,3,2,1,0:T(8,128)S(1)} %get-tuple-element.43), channel_id=1, source_target_pairs={{1,8},{8,1},{3,10},{10,3},{5,12},{12,5},{7,14},{14,7},{9,16},{16,9... | collective-permute-start | bytes 3538952 | tf_op jit(solution)/shard_map/ppermute | solution.py:493
  68.4 25.8 %collective-permute-start.6 = (f32[2,2,4,144,128]{4,3,2,1,0:T(8,128)S(1)}, f32[2,2,4,144,128]{4,3,2,1,0:T(8,128)S(1)}, u32[]{:S(2)}, u32[]{:S(2)}) collective-permute-start(f32[2,2,4,144,128]{4,3,2,1,0:T(8,128)S(1)} %shard_map.69), channel_id=1, source_target_pairs={{1,8},{8,1},{3,10},{10,3},{5,12},{12,5},{7,14},{14,7},{9,16},{16,9... | collective-permute-start | bytes 3538952 | tf_op jit(solution)/shard_map/ppermute | solution.py:491
  71.7 29.7 %collective-permute-start = (f32[2,2,4,136,128]{4,3,2,1,0:T(8,128)S(1)}, f32[2,2,4,136,128]{4,3,2,1,0:T(8,128)}, u32[]{:S(2)}, u32[]{:S(2)}) collective-permute-start(f32[2,2,4,136,128]{4,3,2,1,0:T(8,128)S(1)} %get-tuple-element.35), channel_id=1, source_target_pairs={{0,2},{1,6},{2,0},{3,4},{4,3},{5,7},{6,1},{7,5},{8,10},{9,14},{10,... | collective-permute-start | bytes 3342344 | tf_op jit(solution)/shard_map/ppermute | solution.py:479
  72.7 28.7 %collective-permute-start.1 = (f32[2,2,4,136,128]{4,3,2,1,0:T(8,128)S(1)}, f32[2,2,4,136,128]{4,3,2,1,0:T(8,128)}, u32[]{:S(2)}, u32[]{:S(2)}) collective-permute-start(f32[2,2,4,136,128]{4,3,2,1,0:T(8,128)S(1)} %get-tuple-element.36), channel_id=1, source_target_pairs={{0,0},{1,4},{2,2},{3,6},{4,1},{5,5},{6,3},{7,7},{8,8},{9,12},{10,1... | collective-permute-start | bytes 3342344 | tf_op jit(solution)/shard_map/ppermute | solution.py:479
  74.4 48.9 %collective-permute-start.2 = (f32[2,2,4,136,128]{4,3,2,1,0:T(8,128)S(1)}, f32[2,2,4,136,128]{4,3,2,1,0:T(8,128)}, u32[]{:S(2)}, u32[]{:S(2)}) collective-permute-start(f32[2,2,4,136,128]{4,3,2,1,0:T(8,128)S(1)} %get-tuple-element.37), channel_id=1, source_target_pairs={{0,6},{1,2},{2,4},{3,0},{4,7},{5,3},{6,5},{7,1},{8,14},{9,10},{10,... | collective-permute-start | bytes 3342344 | tf_op jit(solution)/shard_map/ppermute | solution.py:479
  80.4 45.8 %collective-permute-start.3 = (f32[2,2,4,136,128]{4,3,2,1,0:T(8,128)S(1)}, f32[2,2,4,136,128]{4,3,2,1,0:T(8,128)}, u32[]{:S(2)}, u32[]{:S(2)}) collective-permute-start(f32[2,2,4,136,128]{4,3,2,1,0:T(8,128)S(1)} %get-tuple-element.38), channel_id=1, source_target_pairs={{0,4},{1,0},{2,6},{3,2},{4,5},{5,1},{6,7},{7,3},{8,12},{9,8},{10,1... | collective-permute-start | bytes 3342344 | tf_op jit(solution)/shard_map/ppermute | solution.py:479
  129.3 4.6 %collective-permute-start.17 = (f32[4,4,144,128]{3,2,1,0:T(8,128)S(1)}, f32[4,4,144,128]{3,2,1,0:T(8,128)S(1)}, u32[]{:S(2)}, u32[]{:S(2)}) collective-permute-start(f32[4,4,144,128]{3,2,1,0:T(8,128)S(1)} %get-tuple-element.55.a_ref), channel_id=1, source_target_pairs={{0,1},{1,0},{2,3},{3,2},{4,5},{5,4},{6,7},{7,6},{8,9},{9,8},{10,11... | collective-permute-start | bytes 3538952 | tf_op jit(solution)/shard_map/ppermute | solution.py:529
  131.5 13.5 %collective-permute-start.16 = (f32[4,4,144,128]{3,2,1,0:T(8,128)S(1)}, f32[4,4,144,128]{3,2,1,0:T(8,128)S(1)}, u32[]{:S(2)}, u32[]{:S(2)}) collective-permute-start(f32[4,4,144,128]{3,2,1,0:T(8,128)S(1)} %get-tuple-element.52.b_ref), channel_id=1, source_target_pairs={{1,8},{8,1},{3,10},{10,3},{5,12},{12,5},{7,14},{14,7},{9,16},{16,9... | collective-permute-start | bytes 3538952 | tf_op jit(solution)/shard_map/ppermute | solution.py:528
  152.6 45.9 %collective-permute-start.24 = (f32[2,4,128,128]{3,2,1,0:T(8,128)S(1)}, f32[2,4,128,128]{3,2,1,0:T(8,128)S(1)}, u32[]{:S(2)}, u32[]{:S(2)}) collective-permute-start(f32[2,4,128,128]{3,2,1,0:T(8,128)S(1)} %get-tuple-element.65), channel_id=1, source_target_pairs={{2,0},{6,1},{0,2},{4,3},{3,4},{7,5},{1,6},{5,7},{10,8},{14,9},{8,1... | collective-permute-start | bytes 1572872 | tf_op jit(solution)/shard_map/ppermute | solution.py:554
  153.7 46.2 %collective-permute-start.25 = (f32[2,4,128,128]{3,2,1,0:T(8,128)S(1)}, f32[2,4,128,128]{3,2,1,0:T(8,128)S(1)}, u32[]{:S(2)}, u32[]{:S(2)}) collective-permute-start(f32[2,4,128,128]{3,2,1,0:T(8,128)S(1)} %get-tuple-element.66), channel_id=1, source_target_pairs={{0,0},{4,1},{2,2},{6,3},{1,4},{5,5},{3,6},{7,7},{8,8},{12,9},{10,1... | collective-permute-start | bytes 1572872 | tf_op jit(solution)/shard_map/ppermute | solution.py:554
  154.4 48.1 %collective-permute-start.22 = (f32[2,4,128,128]{3,2,1,0:T(8,128)S(1)}, f32[2,4,128,128]{3,2,1,0:T(8,128)S(1)}, u32[]{:S(2)}, u32[]{:S(2)}) collective-permute-start(f32[2,4,128,128]{3,2,1,0:T(8,128)S(1)} %get-tuple-element.63), channel_id=1, source_target_pairs={{6,0},{2,1},{4,2},{0,3},{7,4},{3,5},{5,6},{1,7},{14,8},{10,9},{12,... | collective-permute-start | bytes 1572872 | tf_op jit(solution)/shard_map/ppermute | solution.py:554
  161.5 14.8 %collective-permute-start.11 = (f32[1,1]{1,0:T(1,128)}, f32[1,1]{1,0:T(1,128)}, u32[]{:S(2)}, u32[]{:S(2)}) collective-permute-start(f32[1,1]{1,0:T(1,128)} %get-tuple-element.51), channel_id=1, source_target_pairs={{0,2},{1,3},{2,0},{3,1},{4,6},{5,7},{6,4},{7,5},{8,10},{9,11},{10,... | collective-permute-start | bytes 20 | tf_op jit(solution)/shard_map/ppermute | solution.py:451
  177.7 8.0 %collective-permute-start.12 = (f32[1,1]{1,0:T(1,128)}, f32[1,1]{1,0:T(1,128)}, u32[]{:S(2)}, u32[]{:S(2)}) collective-permute-start(f32[1,1]{1,0:T(1,128)} %add.19), channel_id=1, source_target_pairs={{0,4},{1,5},{2,6},{3,7},{4,0},{5,1},{6,2},{7,3},{8,12},{9,13},{10,... | collective-permute-start | bytes 20 | tf_op jit(solution)/shard_map/ppermute | solution.py:451
  192.9 4.6 %collective-permute-start.15 = (f32[1,1]{1,0:T(1,128)}, f32[1,1]{1,0:T(1,128)}, u32[]{:S(2)}, u32[]{:S(2)}) collective-permute-start(f32[1,1]{1,0:T(1,128)} %add.22), channel_id=1, source_target_pairs={{0,16},{1,17},{2,18},{3,19},{4,20},{5,21},{6,22},{7,23},{8,24},{9,... | collective-permute-start | bytes 20 | tf_op jit(solution)/shard_map/ppermute | solution.py:451
  197.3 14.5 %collective-permute-start.23 = (f32[2,4,128,128]{3,2,1,0:T(8,128)S(1)}, f32[2,4,128,128]{3,2,1,0:T(8,128)}, u32[]{:S(2)}, u32[]{:S(2)}) collective-permute-start(f32[2,4,128,128]{3,2,1,0:T(8,128)S(1)} %get-tuple-element.64), channel_id=1, source_target_pairs={{4,0},{0,1},{6,2},{2,3},{5,4},{1,5},{7,6},{3,7},{12,8},{8,9},{14,1... | collective-permute-start | bytes 1572872 | tf_op jit(solution)/shard_map/ppermute | solution.py:554
  197.5 16.4 %collective-permute-start.20 = (f32[2,4,128,128]{3,2,1,0:T(8,128)S(1)}, f32[2,4,128,128]{3,2,1,0:T(8,128)}, u32[]{:S(2)}, u32[]{:S(2)}) collective-permute-start(f32[2,4,128,128]{3,2,1,0:T(8,128)S(1)} %get-tuple-element.61), channel_id=1, source_target_pairs={{2,0},{6,1},{0,2},{4,3},{3,4},{7,5},{1,6},{5,7},{10,8},{14,9},{8,1... | collective-permute-start | bytes 1572872 | tf_op jit(solution)/shard_map/ppermute | solution.py:554
  198.5 15.4 %collective-permute-start.21 = (f32[2,4,128,128]{3,2,1,0:T(8,128)S(1)}, f32[2,4,128,128]{3,2,1,0:T(8,128)}, u32[]{:S(2)}, u32[]{:S(2)}) collective-permute-start(f32[2,4,128,128]{3,2,1,0:T(8,128)S(1)} %get-tuple-element.62), channel_id=1, source_target_pairs={{0,0},{4,1},{2,2},{6,3},{1,4},{5,5},{3,6},{7,7},{8,8},{12,9},{10,1... | collective-permute-start | bytes 1572872 | tf_op jit(solution)/shard_map/ppermute | solution.py:554
  200.0 23.2 %collective-permute-start.18 = (f32[2,4,128,128]{3,2,1,0:T(8,128)S(1)}, f32[2,4,128,128]{3,2,1,0:T(8,128)}, u32[]{:S(2)}, u32[]{:S(2)}) collective-permute-start(f32[2,4,128,128]{3,2,1,0:T(8,128)S(1)} %get-tuple-element.59), channel_id=1, source_target_pairs={{6,0},{2,1},{4,2},{0,3},{7,4},{3,5},{5,6},{1,7},{14,8},{10,9},{12,... | collective-permute-start | bytes 1572872 | tf_op jit(solution)/shard_map/ppermute | solution.py:554
  202.5 26.5 %collective-permute-start.19 = (f32[2,4,128,128]{3,2,1,0:T(8,128)S(1)}, f32[2,4,128,128]{3,2,1,0:T(8,128)}, u32[]{:S(2)}, u32[]{:S(2)}) collective-permute-start(f32[2,4,128,128]{3,2,1,0:T(8,128)S(1)} %get-tuple-element.60), channel_id=1, source_target_pairs={{4,0},{0,1},{6,2},{2,3},{5,4},{1,5},{7,6},{3,7},{12,8},{8,9},{14,1... | collective-permute-start | bytes 1572872 | tf_op jit(solution)/shard_map/ppermute | solution.py:554
  (14 other events, 96.6 us)

commit v5 on v4

--- a/solution.py
+++ b/solution.py
@@ -354,52 +354,55 @@
                 copy_rows(rows, keep)
 
 
-def backward_wedge(me_ref, rb_ref, b_ref, cw, c_ref, slopes, saved, lam_in, grad_in, *refs):
-    outs, (lam, mv0, mv1, grad) = refs[:-4], refs[-4:]
-    half, blocks, rows = b_ref.shape[:3]
+def backward_wedge(off, me_ref, rb_ref, b_ref, cw, c_ref, slopes, saved, lam_in, grad_in, o0, o1, o2, o3, lam, mv0, mv1, grad):
+    inner = o0.shape[3]
+    rows = inner + 2 * HALO
+    half, blocks = b_ref.shape[:2]
     clear_rims(mv0, rows)
     clear_rims(mv1, rows)
+
+    def there(r):
+        return pl.ds(pl.multiple_of(r.start + off, 8), r.size)
+
     for i in range(half):
 
         def fill(r, rh, i=i):
-            v = rb_ref[half - 1 - i, :, r, :]
+            v = rb_ref[half - 1 - i, :, there(r), :]
             lam[i, :, r, :] = v
-            mv0[i, :, rh, :] = cw[i, :, r, :] * v
-            lam[half + i, :, r, :] = lam_in[i, :, r, :]
+            mv0[i, :, rh, :] = cw[i, :, there(r), :] * v
+            lam[half + i, :, r, :] = lam_in[i, :, there(r), :]
+            if i < 2:
+                mv0[half + i, :, rh, :] = c_ref[i, :, there(r), :] * b_ref[i, :, there(r), :]
 
         copy_rows(rows, fill)
-        if i < 2:
-            copy_rows(rows, lambda r, rh, i=i: mv0.__setitem__((half + i, slice(None), rh), c_ref[i, :, r, :] * b_ref[i, :, r, :]))
-
-        def one(t, carry, i=i):
-            r = pl.multiple_of(t * CHUNK, 8)
-            grad[i, :, pl.ds(r, CHUNK), :] = grad_in[i, :, pl.ds(r, CHUNK), :]
-            return carry
-
-        lax.fori_loop(0, (rows - 2 * HALO) // CHUNK, one, 0)
+        copy_rows(inner, lambda r, rh, i=i: grad.__setitem__((i, slice(None), r), grad_in[i, :, there(r), :]))
     first, last = edges((blocks, CHUNK, LANES))
     for j in range(ITERS):
         k = ITERS - 1 - j
         old, new = (mv0, mv1) if j % 2 == 0 else (mv1, mv0)
         if j:
             for i in range(2):
-                copy_rows(rows, lambda r, rh, i=i: old.__setitem__((half + j + i, slice(None), rh), saved[j - 1, i, :, r, :]))
+
+                def recall(r, rh, j=j, i=i, old=old):
+                    old[half + j + i, :, rh, :] = saved[j - 1, i, :, there(r), :]
+
+                copy_rows(rows, recall)
 
         def plane(s, carry, own, j=j, old=old, new=new):
             for r0 in range(0, rows, CHUNK):
                 change, _ = lap_rows(old, s, r0, CHUNK, first, last)
-                at = slice(r0, r0 + CHUNK)
-                after = lam[s, :, at, :] + change
+                after = lam[s, :, r0 : r0 + CHUNK, :] + change
                 if j < ITERS - 1:
+                    at = slice(off + r0, off + r0 + CHUNK)
                     coef = c_ref[s - half, :, at, :] if own else cw[s, :, at, :]
                     new[s, :, HALO + r0 : HALO + r0 + CHUNK, :] = coef * after
-                lam[s, :, at, :] = after
+                lam[s, :, r0 : r0 + CHUNK, :] = after
             return carry
 
-        def gain(s, carry, j=j, k=k):
+        def gain(s, carry, k=k):
             for r0 in range(HALO, rows - HALO, CHUNK):
                 at = slice(r0 - HALO, r0 - HALO + CHUNK)
-                g = lam[s, :, r0 : r0 + CHUNK, :] * slopes[k, s - half, :, r0 : r0 + CHUNK, :]
+                g = lam[s, :, r0 : r0 + CHUNK, :] * slopes[k, s - half, :, off + r0 : off + r0 + CHUNK, :]
                 grad[s - half, :, at, :] = grad[s - half, :, at, :] + g
             return carry
 
@@ -408,36 +411,44 @@
         spans(half, half + j + 1, lambda s, c: plane(s, c, True))
     me = me_ref[0]
     planes = half // 2
-    for n, r in enumerate(ROUNDS):
+    for r, out in zip(ROUNDS, (o0, o1, o2, o3)):
         block, _ = slot(me, r, planes, 0)
-        for flag, g_src, l_src in ((0, grad, lam), (1, grad_in, lam_in)):
-
-            @pl.when(block == flag)
-            def _(n=n, r=r, g_src=g_src, l_src=l_src):
-                for i in range(planes):
-                    _, at = slot(me, r, planes, i)
-                    outs[n][i] = g_src[at if g_src is grad else half + at]
-                    outs[4 + n][i] = l_src[half + at, :, HALO : rows - HALO, :]
-
-
-def home_kernel(rounds, me_ref, scale_ref, *refs):
+
+        @pl.when(block == 0)
+        def _(r=r, out=out):
+            for i in range(planes):
+                _, at = slot(me, r, planes, i)
+                out[0, i] = grad[at]
+                out[1, i] = lam[half + at, :, HALO : HALO + inner, :]
+
+        @pl.when(block == 1)
+        def _(r=r, out=out):
+            for i in range(planes):
+                _, at = slot(me, r, planes, i)
+                out[0, i] = grad_in[half + at, :, off : off + inner, :]
+                out[1, i] = lam_in[half + at, :, off + HALO : off + HALO + inner, :]
+
+
+def home_kernel(off, rounds, me_ref, scale_ref, *refs):
     count = len(rounds)
-    msgs, (out, near, ready, sems, done) = refs[:count], refs[-5:]
+    msgs, (g_out, a_out, near, ready, sems, done) = refs[:count], refs[-6:]
     _, x, c = bits(me_ref[0])
-    planes, blocks, rows = near.shape[1:4]
-    scale = scale_ref[0, 0]
+    _, planes, blocks, inner = near.shape[1:5]
+    rows = g_out.shape[1] // PARTS
     come = [pltpu.make_async_copy(m, near.at[n], sems.at[n]) for n, m in enumerate(msgs)]
     for copy in come:
         copy.start()
     go = []
     for n, (r1, r0) in enumerate(rounds):
-        start = pl.multiple_of(part(c ^ r1, x ^ r0) * rows, 8)
+        start = pl.multiple_of(part(c ^ r1, x ^ r0) * rows + off, 8)
         come[n].wait()
-        for i in range(planes):
-            for b in range(blocks):
-                ready[n, i, :, b * LANES : (b + 1) * LANES] = near[n, i, b] * scale
-        go.append(pltpu.make_async_copy(ready.at[n], out.at[:, pl.ds(start, rows), :], done.at[n]))
-        go[-1].start()
+        for k, out in enumerate((g_out, a_out)):
+            scale = scale_ref[0, k]
+            for i in range(planes):
+                for b in range(blocks):
+                    ready[n, k, i, :, b * LANES : (b + 1) * LANES] = near[n, k, i, b] * scale
+            go.append(pltpu.make_async_copy(ready.at[n, k], out.at[:, pl.ds(start, inner), :], done.at[n, k]))
+            go[-1].start()
     for copy in go:
         copy.wait()
 
@@ -456,7 +467,7 @@
     axis = "gz"
     count = lax.axis_size(axis)
     planes, height, width = coefficient.shape
-    if count % GROUP or width % LANES or height % (16 * PARTS) or 2 * planes < ITERS or ITERS * 2 > HALO:
+    if count % GROUP or width % LANES or height % (32 * PARTS) or 2 * planes < ITERS or ITERS * 2 > HALO:
         raise ValueError("unsupported sizes")
     rows = height // PARTS
     tall = rows + 2 * HALO
@@ -539,19 +550,21 @@
         [pltpu.VMEM((3 * half, *padded), F32)] * 2,
     )
     part_total = exchange_sum(part_total, axis, count, [4])
-    outs = call(
-        backward_wedge,
-        "backward_wedge",
-        [shape(planes, *inner)] * 8,
-        [me],
-        [far_lb] + inside(lam_b, far_coef, coef, slopes, saved, lam, grad),
-        [pltpu.VMEM((2 * half, *plane_set), F32)]
-        + [pltpu.VMEM((half + ITERS + 2, *padded), F32)] * 2
-        + [pltpu.VMEM((half, *inner), F32)],
-    )
+    strip = rows // 2
     back = []
-    for m, r in zip(outs, ROUNDS * 2):
-        back.append(lax.ppermute(m, axis, [(j, i) for i, j in send_pairs(count, *r)]))
+    for n in range(2):
+        outs = call(
+            partial(backward_wedge, n * strip),
+            f"backward_wedge_{n}",
+            [shape(2, planes, blocks, strip, LANES)] * 4,
+            [me],
+            [far_lb] + inside(lam_b, far_coef, coef, slopes, saved, lam, grad),
+            [pltpu.VMEM((2 * half, blocks, strip + 2 * HALO, LANES), F32)]
+            + [pltpu.VMEM((half + ITERS + 2, blocks, strip + 4 * HALO, LANES), F32)] * 2
+            + [pltpu.VMEM((half, blocks, strip, LANES), F32)],
+        )
+        for m, r in zip(outs, ROUNDS):
+            back.append(lax.ppermute(m, axis, [(j, i) for i, j in send_pairs(count, *r)]))
     back = outside(*back)
 
     if count & (count - 1):
@@ -561,28 +574,24 @@
     cells = count * planes * height * width
     misfit = jnp.sqrt(total[0, 0] / cells + 1e-06)
     inverse = 1.0 / misfit
-
-    def assemble(scale, msgs):
-        held = ()
-        for n in range(0, 4, 2):
-            held = pl.pallas_call(
-                partial(home_kernel, ROUNDS[n : n + 2]),
-                out_shape=[jax.ShapeDtypeStruct((planes, height, width), F32)],
-                in_specs=[SM, SM, ANY, ANY] + [ANY] * len(held),
-                out_specs=[ANY],
-                scratch_shapes=[
-                    pltpu.VMEM((2, planes, *inner), F32),
-                    pltpu.VMEM((2, planes, rows, width), F32),
-                    pltpu.SemaphoreType.DMA((2,)),
-                    pltpu.SemaphoreType.DMA((2,)),
-                ],
-                input_output_aliases={4: 0} if held else {},
-                compiler_params=pltpu.CompilerParams(vmem_limit_bytes=14 << 20),
-            )(me, scale.reshape(1, 1), *msgs[n : n + 2], *held)
-        return held[0]
-
-    gradient = assemble(time_step * inverse, back[:4])
-    adjoint = assemble(inverse, back[4:])
+    scale = jnp.stack([time_step * inverse, inverse]).reshape(1, 2)
+    held = []
+    for n in range(0, 8, 2):
+        held = pl.pallas_call(
+            partial(home_kernel, n // 4 * strip, ROUNDS[n % 4 : n % 4 + 2]),
+            out_shape=[jax.ShapeDtypeStruct((planes, height, width), F32)] * 2,
+            in_specs=[SM, SM, ANY, ANY] + [ANY] * len(held),
+            out_specs=[ANY] * 2,
+            scratch_shapes=[
+                pltpu.VMEM((2, 2, planes, blocks, strip, LANES), F32),
+                pltpu.VMEM((2, 2, planes, strip, width), F32),
+                pltpu.SemaphoreType.DMA((2,)),
+                pltpu.SemaphoreType.DMA((2, 2)),
+            ],
+            input_output_aliases={4: 0, 5: 1} if held else {},
+            compiler_params=pltpu.CompilerParams(vmem_limit_bytes=14 << 20),
+        )(me, scale, *back[n : n + 2], *held)
+    gradient, adjoint = held
     return gradient, adjoint, misfit
 
 

time: 233 us -> 234 us (level)
  Pallas kernels: 53.3 us -> 58.3 us
  waiting for transfers between devices: 109 us -> 104 us
    ppermute x8, waiting for transfers between devices: 19.3 us -> 14.3 us  [on_device(): lax.ppermute(m, axis, [(j, i) for i, j in send_pairs(count, *r)])]
    pallas_call x9 -> x10, Pallas kernels: 44.9 us -> 47.8 us  [call(): pl.pallas_call(kernel, out_shape=outs, in_specs=[SM] * len(scalars) + [AN...]
  transfers between devices with their start and end apart: 26 -> 26, of which waited for: 14 -> 13; matrix products, arithmetic and copies ran while one was open for 0% -> 0% of each run, Pallas kernels for 16% -> 18%
where the time goes in v5:
time: 234 us; the launch traced here: 233 us
  waiting for transfers between devices  104 us (44%)
  starting transfers between devices  60.1 us (26%)
  Pallas kernels  58.3 us (25%)
  between operations  6.01 us (3%)
  local copies, waits for them, and re-layouts  4.44 us (2%)
    ppermute x8, waiting for transfers between devices, regroup(): got.append(lax.ppermute(m, axis, send_pairs(count, *r)))  73.1 us
    pallas_call x10, Pallas kernels, call(): pl.pallas_call(kernel, out_shape=outs, in_specs=[SM] * len(scalars) + [AN...  47.8 us
    ppermute x8, starting transfers between devices, regroup(): got.append(lax.ppermute(m, axis, send_pairs(count, *r)))  20.7 us
    ppermute x5, starting transfers between devices, exchange_sum(): lax.ppermute(value, axis, [(i, i ^ step) for i in range(count)])  18 us
    ppermute x5, waiting for transfers between devices, exchange_sum(): lax.ppermute(value, axis, [(i, i ^ step) for i in range(count)])  14.8 us
    ppermute x8, starting transfers between devices, on_device(): lax.ppermute(m, axis, [(j, i) for i, j in send_pairs(count, *r)])  14.3 us
    ppermute x8, waiting for transfers between devices, on_device(): lax.ppermute(m, axis, [(j, i) for i, j in send_pairs(count, *r)])  14.3 us
    pallas_call x4, Pallas kernels, on_device(): pl.pallas_call(partial(home_kernel, n // 4 * strip, ROUNDS[n % 4:n % 4 +...  10.5 us
  transfers between devices with their start and end apart: 26, of which 13 were waited for; matrix products, arithmetic and copies ran while one was open for 0% of the time, Pallas kernels for 18%

profile of v5, /device:TPU:0, one launch (start us, length us, event | category | flops | bytes accessed | tf_op | source)
XLA Modules:
  0.0 232.9 jit_solution(7368856775226369412)
XLA Ops:
  3.2 3.0 %collective-permute-start.4 = (f32[2,2,4,144,128]{4,3,2,1,0:T(8,128)S(1)}, f32[2,2,4,144,128]{4,3,2,1,0:T(8,128)S(1)}, u32[]{:S(2)}, u32[]{:S(2)}) collective-permute-start(f32[2,2,4,144,128]{4,3,2,1,0:T(8,128)S(1)} %get-tuple-element.47), channel_id=1, source_target_pairs={{0,2},{1,6},{2,0},{3,4},{4,3},{5,7},{6,1},{7,5},{8,10},{9,14},{10,... | collective-permute-start | bytes 3538952 | tf_op jit(solution)/shard_map/ppermute | solution.py:490
  7.0 3.9 %collective-permute-start.7 = (f32[2,2,4,144,128]{4,3,2,1,0:T(8,128)S(1)}, f32[2,2,4,144,128]{4,3,2,1,0:T(8,128)S(1)}, u32[]{:S(2)}, u32[]{:S(2)}) collective-permute-start(f32[2,2,4,144,128]{4,3,2,1,0:T(8,128)S(1)} %get-tuple-element.49), channel_id=1, source_target_pairs={{0,6},{1,2},{2,4},{3,0},{4,7},{5,3},{6,5},{7,1},{8,14},{9,10},{10,... | collective-permute-start | bytes 3538952 | tf_op jit(solution)/shard_map/ppermute | solution.py:490
  10.9 21.3 %collective-permute-done.4.m0 = f32[2,2,4,144,128]{4,3,2,1,0:T(8,128)S(1)} collective-permute-done((f32[2,2,4,144,128]{4,3,2,1,0:T(8,128)S(1)}, f32[2,2,4,144,128]{4,3,2,1,0:T(8,128)S(1)}, u32[]{:S(2)}, u32[]{:S(2)}) %collective-permute-start.4) | collective-permute-done | bytes 1179680 | tf_op jit(solution)/shard_map/ppermute | solution.py:490
  32.2 26.2 %collective-permute-done.7.m2 = f32[2,2,4,144,128]{4,3,2,1,0:T(8,128)S(1)} collective-permute-done((f32[2,2,4,144,128]{4,3,2,1,0:T(8,128)S(1)}, f32[2,2,4,144,128]{4,3,2,1,0:T(8,128)S(1)}, u32[]{:S(2)}, u32[]{:S(2)}) %collective-permute-start.7) | collective-permute-done | bytes 1179680 | tf_op jit(solution)/shard_map/ppermute | solution.py:490
  60.5 2.7 %shard_map.70 = (f32[2,2,4,144,128]{4,3,2,1,0:T(8,128)S(1)}, f32[2,4,4,144,128]{4,3,2,1,0:T(8,128)S(1)}, f32[2,4,4,144,128]{4,3,2,1,0:T(8,128)S(1)}) custom-call(s32[1]{0:T(128)} %bitcast.me_ref, f32[2,2,4,144,128]{4,3,2,1,0:T(8,128)} %copy-done, f32[2,2,4,144,128]{4,3,2,1,0:T(8,128)} %copy-done.1, f32[2,2,4,144,128]{4,3,2,1,0:T(8,128)} %copy-done.7, ...), custom_call_target="tpu_custom_call" | custom-call | tf_op jit(solution)/shard_map/pallas_call | solution.py:29
  63.2 2.8 %collective-permute-start.10 = (f32[2,4,4,144,128]{4,3,2,1,0:T(8,128)S(1)}, f32[2,4,4,144,128]{4,3,2,1,0:T(8,128)S(1)}, u32[]{:S(2)}, u32[]{:S(2)}) collective-permute-start(f32[2,4,4,144,128]{4,3,2,1,0:T(8,128)S(1)} %get-tuple-element.53.a_ref), channel_id=1, source_target_pairs={{0,1},{1,0},{2,3},{3,2},{4,5},{5,4},{6,7},{7,6},{8,9},{9,8},{10,11... | collective-permute-start | bytes 7077896 | tf_op jit(solution)/shard_map/ppermute | solution.py:505
  74.4 6.0 %collective-permute-start.2 = (f32[2,2,4,136,128]{4,3,2,1,0:T(8,128)S(1)}, f32[2,2,4,136,128]{4,3,2,1,0:T(8,128)}, u32[]{:S(2)}, u32[]{:S(2)}) collective-permute-start(f32[2,2,4,136,128]{4,3,2,1,0:T(8,128)S(1)} %get-tuple-element.45), channel_id=1, source_target_pairs={{0,6},{1,2},{2,4},{3,0},{4,7},{5,3},{6,5},{7,1},{8,14},{9,10},{10,... | collective-permute-start | bytes 3342344 | tf_op jit(solution)/shard_map/ppermute | solution.py:490
  80.5 4.3 %collective-permute-start.3 = (f32[2,2,4,136,128]{4,3,2,1,0:T(8,128)S(1)}, f32[2,2,4,136,128]{4,3,2,1,0:T(8,128)}, u32[]{:S(2)}, u32[]{:S(2)}) collective-permute-start(f32[2,2,4,136,128]{4,3,2,1,0:T(8,128)S(1)} %get-tuple-element.46), channel_id=1, source_target_pairs={{0,4},{1,0},{2,6},{3,2},{4,5},{5,1},{6,7},{7,3},{8,12},{9,8},{10,1... | collective-permute-start | bytes 3342344 | tf_op jit(solution)/shard_map/ppermute | solution.py:490
  84.7 9.5 %shard_map.71 = (f32[8,4,144,128]{3,2,1,0:T(8,128)S(1)}, f32[12,4,144,128]{3,2,1,0:T(8,128)S(1)}, f32[4,8,4,144,128]{4,3,2,1,0:T(8,128)S(1)}, f32[3,2,4,144,128]{4,3,2,1,0:T(8,128)S(1)}) custom-call(s32[1]{0:T(128)} %bitcast.me_ref, f32[2,4,4,144,128]{4,3,2,1,0:T(8,128)S(1)} %get-tuple-element.53.a_ref, f32[2,4,4,144,128]{4,3,2,1,0:T(8,128)S(1)} %get-tuple-element.52.b_ref, ...), custom_call_target="tpu_custom_call" | custom-call | tf_op jit(solution)/shard_map/pallas_call | solution.py:29
  95.2 6.2 %shard_map.72 = (f32[8,4,144,128]{3,2,1,0:T(8,128)S(1)}, f32[4,8,4,144,128]{4,3,2,1,0:T(8,128)S(1)}, f32[4,4,144,128]{3,2,1,0:T(8,128)S(1)}) custom-call(s32[1]{0:T(128)} %bitcast.me_ref, f32[2,2,4,144,128]{4,3,2,1,0:T(8,128)} %copy-done.5, f32[2,2,4,144,128]{4,3,2,1,0:T(8,128)} %copy-done.4, ...), custom_call_target="tpu_custom_call", output_to_operand_aliasing={{0}: (6, {}), {1}: (7, {})} | custom-call | tf_op jit(solution)/shard_map/pallas_call | solution.py:29
  101.5 21.8 %collective-permute-done.2.f2 = f32[2,2,4,136,128]{4,3,2,1,0:T(8,128)} collective-permute-done((f32[2,2,4,136,128]{4,3,2,1,0:T(8,128)S(1)}, f32[2,2,4,136,128]{4,3,2,1,0:T(8,128)}, u32[]{:S(2)}, u32[]{:S(2)}) %collective-permute-start.2) | collective-permute-done | bytes 1114144 | tf_op jit(solution)/shard_map/ppermute | solution.py:490
  123.3 3.0 %collective-permute-done.3.f3 = f32[2,2,4,136,128]{4,3,2,1,0:T(8,128)} collective-permute-done((f32[2,2,4,136,128]{4,3,2,1,0:T(8,128)S(1)}, f32[2,2,4,136,128]{4,3,2,1,0:T(8,128)}, u32[]{:S(2)}, u32[]{:S(2)}) %collective-permute-start.3) | collective-permute-done | bytes 1114144 | tf_op jit(solution)/shard_map/ppermute | solution.py:490
  126.3 3.0 %shard_map.73 = (f32[4,4,144,128]{3,2,1,0:T(8,128)S(1)}, f32[4,4,144,128]{3,2,1,0:T(8,128)S(1)}, f32[1,1]{1,0:T(1,128)}) custom-call(s32[1]{0:T(128)} %bitcast.me_ref, f32[2,2,4,136,128]{4,3,2,1,0:T(8,128)} %copy-done.9, f32[2,2,4,136,128]{4,3,2,1,0:T(8,128)} %collective-permute-done.1.f1, f32[2,2,4,136,128]{4,3,2,1,0:T(8,128)} %collective-permute-done.2.f2, ...), custom_call_target="tpu_custom_call" | custom-call | tf_op jit(solution)/shard_map/pallas_call | solution.py:29
  135.0 10.0 %shard_map.74 = (f32[12,4,144,128]{3,2,1,0:T(8,128)S(1)}, f32[8,4,128,128]{3,2,1,0:T(8,128)S(1)}, f32[3,2,4,144,128]{4,3,2,1,0:T(8,128)S(1)}) custom-call(s32[1]{0:T(128)} %bitcast.me_ref, f32[4,4,144,128]{3,2,1,0:T(8,128)} %copy-done.6, f32[4,4,144,128]{3,2,1,0:T(8,128)S(1)} %get-tuple-element.63.a_ref, f32[4,4,144,128]{3,2,1,0:T(8,128)S(1)} %get-tuple-element.60.b_ref, ...), custom_call_target="tpu_custom_call" | custom-call | tf_op jit(solution)/shard_map/pallas_call | solution.py:29
  146.0 4.8 %shard_map.76 = (f32[2,2,4,64,128]{4,3,2,1,0:T(8,128)S(1)}, f32[2,2,4,64,128]{4,3,2,1,0:T(8,128)S(1)}, f32[2,2,4,64,128]{4,3,2,1,0:T(8,128)S(1)}, f32[2,2,4,64,128]{4,3,2,1,0:T(8,128)S(1)}) custom-call(s32[1]{0:T(128)} %bitcast.me_ref, f32[4,4,144,128]{3,2,1,0:T(8,128)} %copy-done.2, f32[4,4,144,128]{3,2,1,0:T(8,128)S(1)} %get-tuple-element.60.b_ref, ...), custom_call_target="tpu_custom_call" | custom-call | tf_op jit(solution)/shard_map/pallas_call | solution.py:29
  152.6 7.3 %collective-permute-start.22 = (f32[2,2,4,64,128]{4,3,2,1,0:T(8,128)S(1)}, f32[2,2,4,64,128]{4,3,2,1,0:T(8,128)S(1)}, u32[]{:S(2)}, u32[]{:S(2)}) collective-permute-start(f32[2,2,4,64,128]{4,3,2,1,0:T(8,128)S(1)} %get-tuple-element.71), channel_id=1, source_target_pairs={{6,0},{2,1},{4,2},{0,3},{7,4},{3,5},{5,6},{1,7},{14,8},{10,9},{12,... | collective-permute-start | bytes 1572872 | tf_op jit(solution)/shard_map/ppermute | solution.py:567
  160.9 13.8 %collective-permute-done.11 = f32[1,1]{1,0:T(1,128)} collective-permute-done((f32[1,1]{1,0:T(1,128)}, f32[1,1]{1,0:T(1,128)}, u32[]{:S(2)}, u32[]{:S(2)}) %collective-permute-start.11) | collective-permute-done | bytes 36 | tf_op jit(solution)/shard_map/ppermute | solution.py:462
  175.9 7.8 %collective-permute-start.12 = (f32[1,1]{1,0:T(1,128)}, f32[1,1]{1,0:T(1,128)}, u32[]{:S(2)}, u32[]{:S(2)}) collective-permute-start(f32[1,1]{1,0:T(1,128)} %add.19), channel_id=1, source_target_pairs={{0,4},{1,5},{2,6},{3,7},{4,0},{5,1},{6,2},{7,3},{8,12},{9,13},{10,... | collective-permute-start | bytes 20 | tf_op jit(solution)/shard_map/ppermute | solution.py:462
  186.7 3.8 %collective-permute-start.14 = (f32[1,1]{1,0:T(1,128)}, f32[1,1]{1,0:T(1,128)}, u32[]{:S(2)}, u32[]{:S(2)}) collective-permute-start(f32[1,1]{1,0:T(1,128)} %add.21), channel_id=1, source_target_pairs={{0,8},{1,9},{2,10},{3,11},{4,12},{5,13},{6,14},{7,15},{8,0},{9,1},... | collective-permute-start | bytes 20 | tf_op jit(solution)/shard_map/ppermute | solution.py:462
  191.5 4.4 %collective-permute-start.15 = (f32[1,1]{1,0:T(1,128)}, f32[1,1]{1,0:T(1,128)}, u32[]{:S(2)}, u32[]{:S(2)}) collective-permute-start(f32[1,1]{1,0:T(1,128)} %add.22), channel_id=1, source_target_pairs={{0,16},{1,17},{2,18},{3,19},{4,20},{5,21},{6,22},{7,23},{8,24},{9,... | collective-permute-start | bytes 20 | tf_op jit(solution)/shard_map/ppermute | solution.py:462
  195.9 4.8 %shard_map.75 = (f32[2,2,4,64,128]{4,3,2,1,0:T(8,128)S(1)}, f32[2,2,4,64,128]{4,3,2,1,0:T(8,128)S(1)}, f32[2,2,4,64,128]{4,3,2,1,0:T(8,128)S(1)}, f32[2,2,4,64,128]{4,3,2,1,0:T(8,128)S(1)}) custom-call(s32[1]{0:T(128)} %bitcast.me_ref, f32[4,4,144,128]{3,2,1,0:T(8,128)} %copy-done.2, f32[4,4,144,128]{3,2,1,0:T(8,128)S(1)} %get-tuple-element.60.b_ref, ...), custom_call_target="tpu_custom_call" | custom-call | tf_op jit(solution)/shard_map/pallas_call | solution.py:29
  203.3 2.7 %collective-permute-start.18 = (f32[2,2,4,64,128]{4,3,2,1,0:T(8,128)S(1)}, f32[2,2,4,64,128]{4,3,2,1,0:T(8,128)}, u32[]{:S(2)}, u32[]{:S(2)}) collective-permute-start(f32[2,2,4,64,128]{4,3,2,1,0:T(8,128)S(1)} %get-tuple-element.67), channel_id=1, source_target_pairs={{6,0},{2,1},{4,2},{0,3},{7,4},{3,5},{5,6},{1,7},{14,8},{10,9},{12,... | collective-permute-start | bytes 1572872 | tf_op jit(solution)/shard_map/ppermute | solution.py:567
  209.6 2.6 %shard_map.78 = (f32[2,512,512]{2,1,0:T(8,128)}, f32[2,512,512]{2,1,0:T(8,128)}) custom-call(s32[1]{0:T(128)} %bitcast.me_ref, f32[1,2]{1,0:T(1,128)S(1)} %maximum_bitcast_fusion.scale_ref, f32[2,2,4,64,128]{4,3,2,1,0:T(8,128)} %copy-done.12, f32[2,2,4,64,128]{4,3,2,1,0:T(8,128)} %collective-permute-done.23.refs_1_, ...), custom_call_target="tpu_custom_call", output_to_operand_aliasing={{0}: (4, {}), {1}: (5, {})} | custom-call | tf_op jit(solution)/shard_map/pallas_call | solution.py:580
  217.4 9.2 %collective-permute-done.18.refs_0_ = f32[2,2,4,64,128]{4,3,2,1,0:T(8,128)} collective-permute-done((f32[2,2,4,64,128]{4,3,2,1,0:T(8,128)S(1)}, f32[2,2,4,64,128]{4,3,2,1,0:T(8,128)}, u32[]{:S(2)}, u32[]{:S(2)}) %collective-permute-start.18) | collective-permute-done | bytes 524320 | tf_op jit(solution)/shard_map/ppermute | solution.py:567
  (69 shorter events, 42.0 us)
Async XLA Ops:
  3.2 29.0 %collective-permute-start.4 = (f32[2,2,4,144,128]{4,3,2,1,0:T(8,128)S(1)}, f32[2,2,4,144,128]{4,3,2,1,0:T(8,128)S(1)}, u32[]{:S(2)}, u32[]{:S(2)}) collective-permute-start(f32[2,2,4,144,128]{4,3,2,1,0:T(8,128)S(1)} %get-tuple-element.47), channel_id=1, source_target_pairs={{0,2},{1,6},{2,0},{3,4},{4,3},{5,7},{6,1},{7,5},{8,10},{9,14},{10,... | collective-permute-start | bytes 3538952 | tf_op jit(solution)/shard_map/ppermute | solution.py:490
  6.2 26.0 %collective-permute-start.5 = (f32[2,2,4,144,128]{4,3,2,1,0:T(8,128)S(1)}, f32[2,2,4,144,128]{4,3,2,1,0:T(8,128)S(1)}, u32[]{:S(2)}, u32[]{:S(2)}) collective-permute-start(f32[2,2,4,144,128]{4,3,2,1,0:T(8,128)S(1)} %get-tuple-element.48), channel_id=1, source_target_pairs={{0,0},{1,4},{2,2},{3,6},{4,1},{5,5},{6,3},{7,7},{8,8},{9,12},{10,1... | collective-permute-start | bytes 3538952 | tf_op jit(solution)/shard_map/ppermute | solution.py:490
  7.0 51.4 %collective-permute-start.7 = (f32[2,2,4,144,128]{4,3,2,1,0:T(8,128)S(1)}, f32[2,2,4,144,128]{4,3,2,1,0:T(8,128)S(1)}, u32[]{:S(2)}, u32[]{:S(2)}) collective-permute-start(f32[2,2,4,144,128]{4,3,2,1,0:T(8,128)S(1)} %get-tuple-element.49), channel_id=1, source_target_pairs={{0,6},{1,2},{2,4},{3,0},{4,7},{5,3},{6,5},{7,1},{8,14},{9,10},{10,... | collective-permute-start | bytes 3538952 | tf_op jit(solution)/shard_map/ppermute | solution.py:490
  10.9 48.3 %collective-permute-start.8 = (f32[2,2,4,144,128]{4,3,2,1,0:T(8,128)S(1)}, f32[2,2,4,144,128]{4,3,2,1,0:T(8,128)S(1)}, u32[]{:S(2)}, u32[]{:S(2)}) collective-permute-start(f32[2,2,4,144,128]{4,3,2,1,0:T(8,128)S(1)} %get-tuple-element.50), channel_id=1, source_target_pairs={{0,4},{1,0},{2,6},{3,2},{4,5},{5,1},{6,7},{7,3},{8,12},{9,8},{10,1... | collective-permute-start | bytes 3538952 | tf_op jit(solution)/shard_map/ppermute | solution.py:490
  63.2 17.2 %collective-permute-start.10 = (f32[2,4,4,144,128]{4,3,2,1,0:T(8,128)S(1)}, f32[2,4,4,144,128]{4,3,2,1,0:T(8,128)S(1)}, u32[]{:S(2)}, u32[]{:S(2)}) collective-permute-start(f32[2,4,4,144,128]{4,3,2,1,0:T(8,128)S(1)} %get-tuple-element.53.a_ref), channel_id=1, source_target_pairs={{0,1},{1,0},{2,3},{3,2},{4,5},{5,4},{6,7},{7,6},{8,9},{9,8},{10,11... | collective-permute-start | bytes 7077896 | tf_op jit(solution)/shard_map/ppermute | solution.py:505
  66.0 8.4 %collective-permute-start.9 = (f32[2,2,4,144,128]{4,3,2,1,0:T(8,128)S(1)}, f32[2,2,4,144,128]{4,3,2,1,0:T(8,128)S(1)}, u32[]{:S(2)}, u32[]{:S(2)}) collective-permute-start(f32[2,2,4,144,128]{4,3,2,1,0:T(8,128)S(1)} %get-tuple-element.51), channel_id=1, source_target_pairs={{1,8},{8,1},{3,10},{10,3},{5,12},{12,5},{7,14},{14,7},{9,16},{16,9... | collective-permute-start | bytes 3538952 | tf_op jit(solution)/shard_map/ppermute | solution.py:504
  68.4 25.8 %collective-permute-start.6 = (f32[2,2,4,144,128]{4,3,2,1,0:T(8,128)S(1)}, f32[2,2,4,144,128]{4,3,2,1,0:T(8,128)S(1)}, u32[]{:S(2)}, u32[]{:S(2)}) collective-permute-start(f32[2,2,4,144,128]{4,3,2,1,0:T(8,128)S(1)} %shard_map.69), channel_id=1, source_target_pairs={{1,8},{8,1},{3,10},{10,3},{5,12},{12,5},{7,14},{14,7},{9,16},{16,9... | collective-permute-start | bytes 3538952 | tf_op jit(solution)/shard_map/ppermute | solution.py:502
  71.7 29.7 %collective-permute-start = (f32[2,2,4,136,128]{4,3,2,1,0:T(8,128)S(1)}, f32[2,2,4,136,128]{4,3,2,1,0:T(8,128)S(1)}, u32[]{:S(2)}, u32[]{:S(2)}) collective-permute-start(f32[2,2,4,136,128]{4,3,2,1,0:T(8,128)S(1)} %get-tuple-element.43), channel_id=1, source_target_pairs={{0,2},{1,6},{2,0},{3,4},{4,3},{5,7},{6,1},{7,5},{8,10},{9,14},{10,... | collective-permute-start | bytes 3342344 | tf_op jit(solution)/shard_map/ppermute | solution.py:490
  72.8 28.7 %collective-permute-start.1 = (f32[2,2,4,136,128]{4,3,2,1,0:T(8,128)S(1)}, f32[2,2,4,136,128]{4,3,2,1,0:T(8,128)}, u32[]{:S(2)}, u32[]{:S(2)}) collective-permute-start(f32[2,2,4,136,128]{4,3,2,1,0:T(8,128)S(1)} %get-tuple-element.44), channel_id=1, source_target_pairs={{0,0},{1,4},{2,2},{3,6},{4,1},{5,5},{6,3},{7,7},{8,8},{9,12},{10,1... | collective-permute-start | bytes 3342344 | tf_op jit(solution)/shard_map/ppermute | solution.py:490
  74.4 48.8 %collective-permute-start.2 = (f32[2,2,4,136,128]{4,3,2,1,0:T(8,128)S(1)}, f32[2,2,4,136,128]{4,3,2,1,0:T(8,128)}, u32[]{:S(2)}, u32[]{:S(2)}) collective-permute-start(f32[2,2,4,136,128]{4,3,2,1,0:T(8,128)S(1)} %get-tuple-element.45), channel_id=1, source_target_pairs={{0,6},{1,2},{2,4},{3,0},{4,7},{5,3},{6,5},{7,1},{8,14},{9,10},{10,... | collective-permute-start | bytes 3342344 | tf_op jit(solution)/shard_map/ppermute | solution.py:490
  80.5 45.8 %collective-permute-start.3 = (f32[2,2,4,136,128]{4,3,2,1,0:T(8,128)S(1)}, f32[2,2,4,136,128]{4,3,2,1,0:T(8,128)}, u32[]{:S(2)}, u32[]{:S(2)}) collective-permute-start(f32[2,2,4,136,128]{4,3,2,1,0:T(8,128)S(1)} %get-tuple-element.46), channel_id=1, source_target_pairs={{0,4},{1,0},{2,6},{3,2},{4,5},{5,1},{6,7},{7,3},{8,12},{9,8},{10,1... | collective-permute-start | bytes 3342344 | tf_op jit(solution)/shard_map/ppermute | solution.py:490
  129.3 4.6 %collective-permute-start.17 = (f32[4,4,144,128]{3,2,1,0:T(8,128)S(1)}, f32[4,4,144,128]{3,2,1,0:T(8,128)S(1)}, u32[]{:S(2)}, u32[]{:S(2)}) collective-permute-start(f32[4,4,144,128]{3,2,1,0:T(8,128)S(1)} %get-tuple-element.63.a_ref), channel_id=1, source_target_pairs={{0,1},{1,0},{2,3},{3,2},{4,5},{5,4},{6,7},{7,6},{8,9},{9,8},{10,11... | collective-permute-start | bytes 3538952 | tf_op jit(solution)/shard_map/ppermute | solution.py:540
  131.5 13.5 %collective-permute-start.16 = (f32[4,4,144,128]{3,2,1,0:T(8,128)S(1)}, f32[4,4,144,128]{3,2,1,0:T(8,128)S(1)}, u32[]{:S(2)}, u32[]{:S(2)}) collective-permute-start(f32[4,4,144,128]{3,2,1,0:T(8,128)S(1)} %get-tuple-element.60.b_ref), channel_id=1, source_target_pairs={{1,8},{8,1},{3,10},{10,3},{5,12},{12,5},{7,14},{14,7},{9,16},{16,9... | collective-permute-start | bytes 3538952 | tf_op jit(solution)/shard_map/ppermute | solution.py:539
  150.8 51.0 %collective-permute-start.24 = (f32[2,2,4,64,128]{4,3,2,1,0:T(8,128)S(1)}, f32[2,2,4,64,128]{4,3,2,1,0:T(8,128)S(1)}, u32[]{:S(2)}, u32[]{:S(2)}) collective-permute-start(f32[2,2,4,64,128]{4,3,2,1,0:T(8,128)S(1)} %get-tuple-element.73), channel_id=1, source_target_pairs={{2,0},{6,1},{0,2},{4,3},{3,4},{7,5},{1,6},{5,7},{10,8},{14,9},{8,1... | collective-permute-start | bytes 1572872 | tf_op jit(solution)/shard_map/ppermute | solution.py:567
  151.9 51.4 %collective-permute-start.25 = (f32[2,2,4,64,128]{4,3,2,1,0:T(8,128)S(1)}, f32[2,2,4,64,128]{4,3,2,1,0:T(8,128)S(1)}, u32[]{:S(2)}, u32[]{:S(2)}) collective-permute-start(f32[2,2,4,64,128]{4,3,2,1,0:T(8,128)S(1)} %get-tuple-element.74), channel_id=1, source_target_pairs={{0,0},{4,1},{2,2},{6,3},{1,4},{5,5},{3,6},{7,7},{8,8},{12,9},{10,1... | collective-permute-start | bytes 1572872 | tf_op jit(solution)/shard_map/ppermute | solution.py:567
  152.6 53.4 %collective-permute-start.22 = (f32[2,2,4,64,128]{4,3,2,1,0:T(8,128)S(1)}, f32[2,2,4,64,128]{4,3,2,1,0:T(8,128)S(1)}, u32[]{:S(2)}, u32[]{:S(2)}) collective-permute-start(f32[2,2,4,64,128]{4,3,2,1,0:T(8,128)S(1)} %get-tuple-element.71), channel_id=1, source_target_pairs={{6,0},{2,1},{4,2},{0,3},{7,4},{3,5},{5,6},{1,7},{14,8},{10,9},{12,... | collective-permute-start | bytes 1572872 | tf_op jit(solution)/shard_map/ppermute | solution.py:567
  159.9 14.8 %collective-permute-start.11 = (f32[1,1]{1,0:T(1,128)}, f32[1,1]{1,0:T(1,128)}, u32[]{:S(2)}, u32[]{:S(2)}) collective-permute-start(f32[1,1]{1,0:T(1,128)} %get-tuple-element.59), channel_id=1, source_target_pairs={{0,2},{1,3},{2,0},{3,1},{4,6},{5,7},{6,4},{7,5},{8,10},{9,11},{10,... | collective-permute-start | bytes 20 | tf_op jit(solution)/shard_map/ppermute | solution.py:462
  175.9 8.1 %collective-permute-start.12 = (f32[1,1]{1,0:T(1,128)}, f32[1,1]{1,0:T(1,128)}, u32[]{:S(2)}, u32[]{:S(2)}) collective-permute-start(f32[1,1]{1,0:T(1,128)} %add.19), channel_id=1, source_target_pairs={{0,4},{1,5},{2,6},{3,7},{4,0},{5,1},{6,2},{7,3},{8,12},{9,13},{10,... | collective-permute-start | bytes 20 | tf_op jit(solution)/shard_map/ppermute | solution.py:462
  191.5 9.2 %collective-permute-start.15 = (f32[1,1]{1,0:T(1,128)}, f32[1,1]{1,0:T(1,128)}, u32[]{:S(2)}, u32[]{:S(2)}) collective-permute-start(f32[1,1]{1,0:T(1,128)} %add.22), channel_id=1, source_target_pairs={{0,16},{1,17},{2,18},{3,19},{4,20},{5,21},{6,22},{7,23},{8,24},{9,... | collective-permute-start | bytes 20 | tf_op jit(solution)/shard_map/ppermute | solution.py:462
  195.9 13.7 %collective-permute-start.23 = (f32[2,2,4,64,128]{4,3,2,1,0:T(8,128)S(1)}, f32[2,2,4,64,128]{4,3,2,1,0:T(8,128)}, u32[]{:S(2)}, u32[]{:S(2)}) collective-permute-start(f32[2,2,4,64,128]{4,3,2,1,0:T(8,128)S(1)} %get-tuple-element.72), channel_id=1, source_target_pairs={{4,0},{0,1},{6,2},{2,3},{5,4},{1,5},{7,6},{3,7},{12,8},{8,9},{14,1... | collective-permute-start | bytes 1572872 | tf_op jit(solution)/shard_map/ppermute | solution.py:567
  200.7 14.1 %collective-permute-start.20 = (f32[2,2,4,64,128]{4,3,2,1,0:T(8,128)S(1)}, f32[2,2,4,64,128]{4,3,2,1,0:T(8,128)}, u32[]{:S(2)}, u32[]{:S(2)}) collective-permute-start(f32[2,2,4,64,128]{4,3,2,1,0:T(8,128)S(1)} %get-tuple-element.69), channel_id=1, source_target_pairs={{2,0},{6,1},{0,2},{4,3},{3,4},{7,5},{1,6},{5,7},{10,8},{14,9},{8,1... | collective-permute-start | bytes 1572872 | tf_op jit(solution)/shard_map/ppermute | solution.py:567
  201.8 13.0 %collective-permute-start.21 = (f32[2,2,4,64,128]{4,3,2,1,0:T(8,128)S(1)}, f32[2,2,4,64,128]{4,3,2,1,0:T(8,128)}, u32[]{:S(2)}, u32[]{:S(2)}) collective-permute-start(f32[2,2,4,64,128]{4,3,2,1,0:T(8,128)S(1)} %get-tuple-element.70), channel_id=1, source_target_pairs={{0,0},{4,1},{2,2},{6,3},{1,4},{5,5},{3,6},{7,7},{8,8},{12,9},{10,1... | collective-permute-start | bytes 1572872 | tf_op jit(solution)/shard_map/ppermute | solution.py:567
  203.3 23.4 %collective-permute-start.18 = (f32[2,2,4,64,128]{4,3,2,1,0:T(8,128)S(1)}, f32[2,2,4,64,128]{4,3,2,1,0:T(8,128)}, u32[]{:S(2)}, u32[]{:S(2)}) collective-permute-start(f32[2,2,4,64,128]{4,3,2,1,0:T(8,128)S(1)} %get-tuple-element.67), channel_id=1, source_target_pairs={{6,0},{2,1},{4,2},{0,3},{7,4},{3,5},{5,6},{1,7},{14,8},{10,9},{12,... | collective-permute-start | bytes 1572872 | tf_op jit(solution)/shard_map/ppermute | solution.py:567
  206.0 23.2 %collective-permute-start.19 = (f32[2,2,4,64,128]{4,3,2,1,0:T(8,128)S(1)}, f32[2,2,4,64,128]{4,3,2,1,0:T(8,128)}, u32[]{:S(2)}, u32[]{:S(2)}) collective-permute-start(f32[2,2,4,64,128]{4,3,2,1,0:T(8,128)S(1)} %get-tuple-element.68), channel_id=1, source_target_pairs={{4,0},{0,1},{6,2},{2,3},{5,4},{1,5},{7,6},{3,7},{12,8},{8,9},{14,1... | collective-permute-start | bytes 1572872 | tf_op jit(solution)/shard_map/ppermute | solution.py:567
  (15 other events, 122.2 us)

commit v6 on v5

--- a/solution.py
+++ b/solution.py
@@ -21,7 +21,7 @@
 VM = pl.BlockSpec(memory_space=pltpu.VMEM)
 SM = pl.BlockSpec(memory_space=pltpu.SMEM)
 ANY = pl.BlockSpec(memory_space=pl.ANY)
-SHARE = {"forward_main": 30, "forward_wedge": 30, "backward_main": 14}
+SHARE = {"forward_main": 30, "forward_wedge": 30, "backward_main": 11, "backward_wedge_0": 9, "backward_wedge_1": 9, "resid": 8}
 F32 = jnp.float32
 
 
@@ -167,8 +167,17 @@
 
 
 def spans(lo, hi, body):
+    if (hi - lo) % 2:
+        body(lo, 0)
+        lo += 1
+
+    def two(t, carry):
+        body(lo + 2 * t, carry)
+        body(lo + 2 * t + 1, carry)
+        return carry
+
     if hi > lo:
-        lax.fori_loop(lo, hi, body, 0)
+        lax.fori_loop(0, (hi - lo) // 2, two, 0)
 
 
 def forward_main(me_ref, a_ref, b_ref, ra_ref, u_out, c_out, slopes, saved, u0, u1):

time: 234 us -> 232 us (level)
  Pallas kernels: 58.3 us -> 54.2 us
    pallas_call x10, Pallas kernels: 47.8 us -> 43.7 us  [call(): pl.pallas_call(kernel, out_shape=outs, in_specs=[SM] * len(scalars) + [AN...]
  transfers between devices with their start and end apart: 26 -> 26, of which waited for: 13 -> 13; matrix products, arithmetic and copies ran while one was open for 0% -> 0% of each run, Pallas kernels for 18% -> 17%
where the time goes in v6:
time: 232 us; the launch traced here: 231 us
  waiting for transfers between devices  104 us (45%)
  starting transfers between devices  62 us (27%)
  Pallas kernels  54.2 us (23%)
  between operations  6.01 us (3%)
  local copies, waits for them, and re-layouts  4.44 us (2%)
    ppermute x8, waiting for transfers between devices, regroup(): got.append(lax.ppermute(m, axis, send_pairs(count, *r)))  74.6 us
    pallas_call x10, Pallas kernels, call(): pl.pallas_call(kernel, out_shape=outs, in_specs=[SM] * len(scalars) + [AN...  43.7 us
    ppermute x8, starting transfers between devices, regroup(): got.append(lax.ppermute(m, axis, send_pairs(count, *r)))  20.7 us
    ppermute x5, starting transfers between devices, exchange_sum(): lax.ppermute(value, axis, [(i, i ^ step) for i in range(count)])  19.1 us
    ppermute x8, starting transfers between devices, on_device(): lax.ppermute(m, axis, [(j, i) for i, j in send_pairs(count, *r)])  14.9 us
    ppermute x8, waiting for transfers between devices, on_device(): lax.ppermute(m, axis, [(j, i) for i, j in send_pairs(count, *r)])  14.3 us
    ppermute x5, waiting for transfers between devices, exchange_sum(): lax.ppermute(value, axis, [(i, i ^ step) for i in range(count)])  13.9 us
    pallas_call x4, Pallas kernels, on_device(): pl.pallas_call(partial(home_kernel, n // 4 * strip, ROUNDS[n % 4:n % 4 +...  10.5 us
  transfers between devices with their start and end apart: 26, of which 13 were waited for; matrix products, arithmetic and copies ran while one was open for 0% of the time, Pallas kernels for 17%

profile of v6, /device:TPU:0, one launch (start us, length us, event | category | flops | bytes accessed | tf_op | source)
XLA Modules:
  0.0 231.1 jit_solution(3254235209287312180)
XLA Ops:
  3.2 3.0 %collective-permute-start.4 = (f32[2,2,4,144,128]{4,3,2,1,0:T(8,128)S(1)}, f32[2,2,4,144,128]{4,3,2,1,0:T(8,128)S(1)}, u32[]{:S(2)}, u32[]{:S(2)}) collective-permute-start(f32[2,2,4,144,128]{4,3,2,1,0:T(8,128)S(1)} %get-tuple-element.47), channel_id=1, source_target_pairs={{0,2},{1,6},{2,0},{3,4},{4,3},{5,7},{6,1},{7,5},{8,10},{9,14},{10,... | collective-permute-start | bytes 3538952 | tf_op jit(solution)/shard_map/ppermute | solution.py:499
  7.0 3.9 %collective-permute-start.7 = (f32[2,2,4,144,128]{4,3,2,1,0:T(8,128)S(1)}, f32[2,2,4,144,128]{4,3,2,1,0:T(8,128)S(1)}, u32[]{:S(2)}, u32[]{:S(2)}) collective-permute-start(f32[2,2,4,144,128]{4,3,2,1,0:T(8,128)S(1)} %get-tuple-element.49), channel_id=1, source_target_pairs={{0,6},{1,2},{2,4},{3,0},{4,7},{5,3},{6,5},{7,1},{8,14},{9,10},{10,... | collective-permute-start | bytes 3538952 | tf_op jit(solution)/shard_map/ppermute | solution.py:499
  10.9 21.3 %collective-permute-done.4.m0 = f32[2,2,4,144,128]{4,3,2,1,0:T(8,128)S(1)} collective-permute-done((f32[2,2,4,144,128]{4,3,2,1,0:T(8,128)S(1)}, f32[2,2,4,144,128]{4,3,2,1,0:T(8,128)S(1)}, u32[]{:S(2)}, u32[]{:S(2)}) %collective-permute-start.4) | collective-permute-done | bytes 1179680 | tf_op jit(solution)/shard_map/ppermute | solution.py:499
  32.2 26.2 %collective-permute-done.7.m2 = f32[2,2,4,144,128]{4,3,2,1,0:T(8,128)S(1)} collective-permute-done((f32[2,2,4,144,128]{4,3,2,1,0:T(8,128)S(1)}, f32[2,2,4,144,128]{4,3,2,1,0:T(8,128)S(1)}, u32[]{:S(2)}, u32[]{:S(2)}) %collective-permute-start.7) | collective-permute-done | bytes 1179680 | tf_op jit(solution)/shard_map/ppermute | solution.py:499
  60.5 2.7 %shard_map.70 = (f32[2,2,4,144,128]{4,3,2,1,0:T(8,128)S(1)}, f32[2,4,4,144,128]{4,3,2,1,0:T(8,128)S(1)}, f32[2,4,4,144,128]{4,3,2,1,0:T(8,128)S(1)}) custom-call(s32[1]{0:T(128)} %bitcast.me_ref, f32[2,2,4,144,128]{4,3,2,1,0:T(8,128)} %copy-done, f32[2,2,4,144,128]{4,3,2,1,0:T(8,128)} %copy-done.1, f32[2,2,4,144,128]{4,3,2,1,0:T(8,128)} %copy-done.7, ...), custom_call_target="tpu_custom_call" | custom-call | tf_op jit(solution)/shard_map/pallas_call | solution.py:29
  63.2 2.8 %collective-permute-start.10 = (f32[2,4,4,144,128]{4,3,2,1,0:T(8,128)S(1)}, f32[2,4,4,144,128]{4,3,2,1,0:T(8,128)S(1)}, u32[]{:S(2)}, u32[]{:S(2)}) collective-permute-start(f32[2,4,4,144,128]{4,3,2,1,0:T(8,128)S(1)} %get-tuple-element.53.a_ref), channel_id=1, source_target_pairs={{0,1},{1,0},{2,3},{3,2},{4,5},{5,4},{6,7},{7,6},{8,9},{9,8},{10,11... | collective-permute-start | bytes 7077896 | tf_op jit(solution)/shard_map/ppermute | solution.py:514
  74.4 6.0 %collective-permute-start.2 = (f32[2,2,4,136,128]{4,3,2,1,0:T(8,128)S(1)}, f32[2,2,4,136,128]{4,3,2,1,0:T(8,128)}, u32[]{:S(2)}, u32[]{:S(2)}) collective-permute-start(f32[2,2,4,136,128]{4,3,2,1,0:T(8,128)S(1)} %get-tuple-element.45), channel_id=1, source_target_pairs={{0,6},{1,2},{2,4},{3,0},{4,7},{5,3},{6,5},{7,1},{8,14},{9,10},{10,... | collective-permute-start | bytes 3342344 | tf_op jit(solution)/shard_map/ppermute | solution.py:499
  80.5 4.3 %collective-permute-start.3 = (f32[2,2,4,136,128]{4,3,2,1,0:T(8,128)S(1)}, f32[2,2,4,136,128]{4,3,2,1,0:T(8,128)}, u32[]{:S(2)}, u32[]{:S(2)}) collective-permute-start(f32[2,2,4,136,128]{4,3,2,1,0:T(8,128)S(1)} %get-tuple-element.46), channel_id=1, source_target_pairs={{0,4},{1,0},{2,6},{3,2},{4,5},{5,1},{6,7},{7,3},{8,12},{9,8},{10,1... | collective-permute-start | bytes 3342344 | tf_op jit(solution)/shard_map/ppermute | solution.py:499
  84.7 8.6 %shard_map.71 = (f32[8,4,144,128]{3,2,1,0:T(8,128)S(1)}, f32[12,4,144,128]{3,2,1,0:T(8,128)S(1)}, f32[4,8,4,144,128]{4,3,2,1,0:T(8,128)S(1)}, f32[3,2,4,144,128]{4,3,2,1,0:T(8,128)S(1)}) custom-call(s32[1]{0:T(128)} %bitcast.me_ref, f32[2,4,4,144,128]{4,3,2,1,0:T(8,128)S(1)} %get-tuple-element.53.a_ref, f32[2,4,4,144,128]{4,3,2,1,0:T(8,128)S(1)} %get-tuple-element.52.b_ref, ...), custom_call_target="tpu_custom_call" | custom-call | tf_op jit(solution)/shard_map/pallas_call | solution.py:29
  94.4 5.5 %shard_map.72 = (f32[8,4,144,128]{3,2,1,0:T(8,128)S(1)}, f32[4,8,4,144,128]{4,3,2,1,0:T(8,128)S(1)}, f32[4,4,144,128]{3,2,1,0:T(8,128)S(1)}) custom-call(s32[1]{0:T(128)} %bitcast.me_ref, f32[2,2,4,144,128]{4,3,2,1,0:T(8,128)} %copy-done.5, f32[2,2,4,144,128]{4,3,2,1,0:T(8,128)} %copy-done.4, ...), custom_call_target="tpu_custom_call", output_to_operand_aliasing={{0}: (6, {}), {1}: (7, {})} | custom-call | tf_op jit(solution)/shard_map/pallas_call | solution.py:29
  99.9 23.4 %collective-permute-done.2.f2 = f32[2,2,4,136,128]{4,3,2,1,0:T(8,128)} collective-permute-done((f32[2,2,4,136,128]{4,3,2,1,0:T(8,128)S(1)}, f32[2,2,4,136,128]{4,3,2,1,0:T(8,128)}, u32[]{:S(2)}, u32[]{:S(2)}) %collective-permute-start.2) | collective-permute-done | bytes 1114144 | tf_op jit(solution)/shard_map/ppermute | solution.py:499
  123.3 3.0 %collective-permute-done.3.f3 = f32[2,2,4,136,128]{4,3,2,1,0:T(8,128)} collective-permute-done((f32[2,2,4,136,128]{4,3,2,1,0:T(8,128)S(1)}, f32[2,2,4,136,128]{4,3,2,1,0:T(8,128)}, u32[]{:S(2)}, u32[]{:S(2)}) %collective-permute-start.3) | collective-permute-done | bytes 1114144 | tf_op jit(solution)/shard_map/ppermute | solution.py:499
  126.3 3.0 %shard_map.73 = (f32[4,4,144,128]{3,2,1,0:T(8,128)S(1)}, f32[4,4,144,128]{3,2,1,0:T(8,128)S(1)}, f32[1,1]{1,0:T(1,128)}) custom-call(s32[1]{0:T(128)} %bitcast.me_ref, f32[2,2,4,136,128]{4,3,2,1,0:T(8,128)} %copy-done.9, f32[2,2,4,136,128]{4,3,2,1,0:T(8,128)} %collective-permute-done.1.f1, f32[2,2,4,136,128]{4,3,2,1,0:T(8,128)} %collective-permute-done.2.f2, ...), custom_call_target="tpu_custom_call" | custom-call | tf_op jit(solution)/shard_map/pallas_call | solution.py:29
  135.0 9.2 %shard_map.74 = (f32[12,4,144,128]{3,2,1,0:T(8,128)S(1)}, f32[8,4,128,128]{3,2,1,0:T(8,128)S(1)}, f32[3,2,4,144,128]{4,3,2,1,0:T(8,128)S(1)}) custom-call(s32[1]{0:T(128)} %bitcast.me_ref, f32[4,4,144,128]{3,2,1,0:T(8,128)} %copy-done.6, f32[4,4,144,128]{3,2,1,0:T(8,128)S(1)} %get-tuple-element.63.a_ref, f32[4,4,144,128]{3,2,1,0:T(8,128)S(1)} %get-tuple-element.60.b_ref, ...), custom_call_target="tpu_custom_call" | custom-call | tf_op jit(solution)/shard_map/pallas_call | solution.py:29
  145.2 3.9 %shard_map.76 = (f32[2,2,4,64,128]{4,3,2,1,0:T(8,128)S(1)}, f32[2,2,4,64,128]{4,3,2,1,0:T(8,128)S(1)}, f32[2,2,4,64,128]{4,3,2,1,0:T(8,128)S(1)}, f32[2,2,4,64,128]{4,3,2,1,0:T(8,128)S(1)}) custom-call(s32[1]{0:T(128)} %bitcast.me_ref, f32[4,4,144,128]{3,2,1,0:T(8,128)} %copy-done.2, f32[4,4,144,128]{3,2,1,0:T(8,128)S(1)} %get-tuple-element.60.b_ref, ...), custom_call_target="tpu_custom_call" | custom-call | tf_op jit(solution)/shard_map/pallas_call | solution.py:29
  150.9 7.9 %collective-permute-start.22 = (f32[2,2,4,64,128]{4,3,2,1,0:T(8,128)S(1)}, f32[2,2,4,64,128]{4,3,2,1,0:T(8,128)S(1)}, u32[]{:S(2)}, u32[]{:S(2)}) collective-permute-start(f32[2,2,4,64,128]{4,3,2,1,0:T(8,128)S(1)} %get-tuple-element.71), channel_id=1, source_target_pairs={{6,0},{2,1},{4,2},{0,3},{7,4},{3,5},{5,6},{1,7},{14,8},{10,9},{12,... | collective-permute-start | bytes 1572872 | tf_op jit(solution)/shard_map/ppermute | solution.py:576
  159.8 12.9 %collective-permute-done.11 = f32[1,1]{1,0:T(1,128)} collective-permute-done((f32[1,1]{1,0:T(1,128)}, f32[1,1]{1,0:T(1,128)}, u32[]{:S(2)}, u32[]{:S(2)}) %collective-permute-start.11) | collective-permute-done | bytes 36 | tf_op jit(solution)/shard_map/ppermute | solution.py:471
  174.0 8.9 %collective-permute-start.12 = (f32[1,1]{1,0:T(1,128)}, f32[1,1]{1,0:T(1,128)}, u32[]{:S(2)}, u32[]{:S(2)}) collective-permute-start(f32[1,1]{1,0:T(1,128)} %add.19), channel_id=1, source_target_pairs={{0,4},{1,5},{2,6},{3,7},{4,0},{5,1},{6,2},{7,3},{8,12},{9,13},{10,... | collective-permute-start | bytes 20 | tf_op jit(solution)/shard_map/ppermute | solution.py:471
  185.8 3.8 %collective-permute-start.14 = (f32[1,1]{1,0:T(1,128)}, f32[1,1]{1,0:T(1,128)}, u32[]{:S(2)}, u32[]{:S(2)}) collective-permute-start(f32[1,1]{1,0:T(1,128)} %add.21), channel_id=1, source_target_pairs={{0,8},{1,9},{2,10},{3,11},{4,12},{5,13},{6,14},{7,15},{8,0},{9,1},... | collective-permute-start | bytes 20 | tf_op jit(solution)/shard_map/ppermute | solution.py:471
  190.6 4.4 %collective-permute-start.15 = (f32[1,1]{1,0:T(1,128)}, f32[1,1]{1,0:T(1,128)}, u32[]{:S(2)}, u32[]{:S(2)}) collective-permute-start(f32[1,1]{1,0:T(1,128)} %add.22), channel_id=1, source_target_pairs={{0,16},{1,17},{2,18},{3,19},{4,20},{5,21},{6,22},{7,23},{8,24},{9,... | collective-permute-start | bytes 20 | tf_op jit(solution)/shard_map/ppermute | solution.py:471
  195.0 3.9 %shard_map.75 = (f32[2,2,4,64,128]{4,3,2,1,0:T(8,128)S(1)}, f32[2,2,4,64,128]{4,3,2,1,0:T(8,128)S(1)}, f32[2,2,4,64,128]{4,3,2,1,0:T(8,128)S(1)}, f32[2,2,4,64,128]{4,3,2,1,0:T(8,128)S(1)}) custom-call(s32[1]{0:T(128)} %bitcast.me_ref, f32[4,4,144,128]{3,2,1,0:T(8,128)} %copy-done.2, f32[4,4,144,128]{3,2,1,0:T(8,128)S(1)} %get-tuple-element.60.b_ref, ...), custom_call_target="tpu_custom_call" | custom-call | tf_op jit(solution)/shard_map/pallas_call | solution.py:29
  201.5 2.7 %collective-permute-start.18 = (f32[2,2,4,64,128]{4,3,2,1,0:T(8,128)S(1)}, f32[2,2,4,64,128]{4,3,2,1,0:T(8,128)}, u32[]{:S(2)}, u32[]{:S(2)}) collective-permute-start(f32[2,2,4,64,128]{4,3,2,1,0:T(8,128)S(1)} %get-tuple-element.67), channel_id=1, source_target_pairs={{6,0},{2,1},{4,2},{0,3},{7,4},{3,5},{5,6},{1,7},{14,8},{10,9},{12,... | collective-permute-start | bytes 1572872 | tf_op jit(solution)/shard_map/ppermute | solution.py:576
  207.8 2.6 %shard_map.78 = (f32[2,512,512]{2,1,0:T(8,128)}, f32[2,512,512]{2,1,0:T(8,128)}) custom-call(s32[1]{0:T(128)} %bitcast.me_ref, f32[1,2]{1,0:T(1,128)S(1)} %maximum_bitcast_fusion.scale_ref, f32[2,2,4,64,128]{4,3,2,1,0:T(8,128)} %copy-done.12, f32[2,2,4,64,128]{4,3,2,1,0:T(8,128)} %collective-permute-done.23.refs_1_, ...), custom_call_target="tpu_custom_call", output_to_operand_aliasing={{0}: (4, {}), {1}: (5, {})} | custom-call | tf_op jit(solution)/shard_map/pallas_call | solution.py:589
  215.7 9.2 %collective-permute-done.18.refs_0_ = f32[2,2,4,64,128]{4,3,2,1,0:T(8,128)} collective-permute-done((f32[2,2,4,64,128]{4,3,2,1,0:T(8,128)S(1)}, f32[2,2,4,64,128]{4,3,2,1,0:T(8,128)}, u32[]{:S(2)}, u32[]{:S(2)}) %collective-permute-start.18) | collective-permute-done | bytes 524320 | tf_op jit(solution)/shard_map/ppermute | solution.py:576
  (69 shorter events, 42.0 us)
Async XLA Ops:
  3.2 29.0 %collective-permute-start.4 = (f32[2,2,4,144,128]{4,3,2,1,0:T(8,128)S(1)}, f32[2,2,4,144,128]{4,3,2,1,0:T(8,128)S(1)}, u32[]{:S(2)}, u32[]{:S(2)}) collective-permute-start(f32[2,2,4,144,128]{4,3,2,1,0:T(8,128)S(1)} %get-tuple-element.47), channel_id=1, source_target_pairs={{0,2},{1,6},{2,0},{3,4},{4,3},{5,7},{6,1},{7,5},{8,10},{9,14},{10,... | collective-permute-start | bytes 3538952 | tf_op jit(solution)/shard_map/ppermute | solution.py:499
  6.2 26.0 %collective-permute-start.5 = (f32[2,2,4,144,128]{4,3,2,1,0:T(8,128)S(1)}, f32[2,2,4,144,128]{4,3,2,1,0:T(8,128)S(1)}, u32[]{:S(2)}, u32[]{:S(2)}) collective-permute-start(f32[2,2,4,144,128]{4,3,2,1,0:T(8,128)S(1)} %get-tuple-element.48), channel_id=1, source_target_pairs={{0,0},{1,4},{2,2},{3,6},{4,1},{5,5},{6,3},{7,7},{8,8},{9,12},{10,1... | collective-permute-start | bytes 3538952 | tf_op jit(solution)/shard_map/ppermute | solution.py:499
  7.0 51.4 %collective-permute-start.7 = (f32[2,2,4,144,128]{4,3,2,1,0:T(8,128)S(1)}, f32[2,2,4,144,128]{4,3,2,1,0:T(8,128)S(1)}, u32[]{:S(2)}, u32[]{:S(2)}) collective-permute-start(f32[2,2,4,144,128]{4,3,2,1,0:T(8,128)S(1)} %get-tuple-element.49), channel_id=1, source_target_pairs={{0,6},{1,2},{2,4},{3,0},{4,7},{5,3},{6,5},{7,1},{8,14},{9,10},{10,... | collective-permute-start | bytes 3538952 | tf_op jit(solution)/shard_map/ppermute | solution.py:499
  10.9 48.3 %collective-permute-start.8 = (f32[2,2,4,144,128]{4,3,2,1,0:T(8,128)S(1)}, f32[2,2,4,144,128]{4,3,2,1,0:T(8,128)S(1)}, u32[]{:S(2)}, u32[]{:S(2)}) collective-permute-start(f32[2,2,4,144,128]{4,3,2,1,0:T(8,128)S(1)} %get-tuple-element.50), channel_id=1, source_target_pairs={{0,4},{1,0},{2,6},{3,2},{4,5},{5,1},{6,7},{7,3},{8,12},{9,8},{10,1... | collective-permute-start | bytes 3538952 | tf_op jit(solution)/shard_map/ppermute | solution.py:499
  63.2 17.2 %collective-permute-start.10 = (f32[2,4,4,144,128]{4,3,2,1,0:T(8,128)S(1)}, f32[2,4,4,144,128]{4,3,2,1,0:T(8,128)S(1)}, u32[]{:S(2)}, u32[]{:S(2)}) collective-permute-start(f32[2,4,4,144,128]{4,3,2,1,0:T(8,128)S(1)} %get-tuple-element.53.a_ref), channel_id=1, source_target_pairs={{0,1},{1,0},{2,3},{3,2},{4,5},{5,4},{6,7},{7,6},{8,9},{9,8},{10,11... | collective-permute-start | bytes 7077896 | tf_op jit(solution)/shard_map/ppermute | solution.py:514
  66.0 8.4 %collective-permute-start.9 = (f32[2,2,4,144,128]{4,3,2,1,0:T(8,128)S(1)}, f32[2,2,4,144,128]{4,3,2,1,0:T(8,128)S(1)}, u32[]{:S(2)}, u32[]{:S(2)}) collective-permute-start(f32[2,2,4,144,128]{4,3,2,1,0:T(8,128)S(1)} %get-tuple-element.51), channel_id=1, source_target_pairs={{1,8},{8,1},{3,10},{10,3},{5,12},{12,5},{7,14},{14,7},{9,16},{16,9... | collective-permute-start | bytes 3538952 | tf_op jit(solution)/shard_map/ppermute | solution.py:513
  68.4 24.9 %collective-permute-start.6 = (f32[2,2,4,144,128]{4,3,2,1,0:T(8,128)S(1)}, f32[2,2,4,144,128]{4,3,2,1,0:T(8,128)S(1)}, u32[]{:S(2)}, u32[]{:S(2)}) collective-permute-start(f32[2,2,4,144,128]{4,3,2,1,0:T(8,128)S(1)} %shard_map.69), channel_id=1, source_target_pairs={{1,8},{8,1},{3,10},{10,3},{5,12},{12,5},{7,14},{14,7},{9,16},{16,9... | collective-permute-start | bytes 3538952 | tf_op jit(solution)/shard_map/ppermute | solution.py:511
  71.7 28.1 %collective-permute-start = (f32[2,2,4,136,128]{4,3,2,1,0:T(8,128)S(1)}, f32[2,2,4,136,128]{4,3,2,1,0:T(8,128)S(1)}, u32[]{:S(2)}, u32[]{:S(2)}) collective-permute-start(f32[2,2,4,136,128]{4,3,2,1,0:T(8,128)S(1)} %get-tuple-element.43), channel_id=1, source_target_pairs={{0,2},{1,6},{2,0},{3,4},{4,3},{5,7},{6,1},{7,5},{8,10},{9,14},{10,... | collective-permute-start | bytes 3342344 | tf_op jit(solution)/shard_map/ppermute | solution.py:499
  72.8 27.1 %collective-permute-start.1 = (f32[2,2,4,136,128]{4,3,2,1,0:T(8,128)S(1)}, f32[2,2,4,136,128]{4,3,2,1,0:T(8,128)}, u32[]{:S(2)}, u32[]{:S(2)}) collective-permute-start(f32[2,2,4,136,128]{4,3,2,1,0:T(8,128)S(1)} %get-tuple-element.44), channel_id=1, source_target_pairs={{0,0},{1,4},{2,2},{3,6},{4,1},{5,5},{6,3},{7,7},{8,8},{9,12},{10,1... | collective-permute-start | bytes 3342344 | tf_op jit(solution)/shard_map/ppermute | solution.py:499
  74.4 48.8 %collective-permute-start.2 = (f32[2,2,4,136,128]{4,3,2,1,0:T(8,128)S(1)}, f32[2,2,4,136,128]{4,3,2,1,0:T(8,128)}, u32[]{:S(2)}, u32[]{:S(2)}) collective-permute-start(f32[2,2,4,136,128]{4,3,2,1,0:T(8,128)S(1)} %get-tuple-element.45), channel_id=1, source_target_pairs={{0,6},{1,2},{2,4},{3,0},{4,7},{5,3},{6,5},{7,1},{8,14},{9,10},{10,... | collective-permute-start | bytes 3342344 | tf_op jit(solution)/shard_map/ppermute | solution.py:499
  80.5 45.8 %collective-permute-start.3 = (f32[2,2,4,136,128]{4,3,2,1,0:T(8,128)S(1)}, f32[2,2,4,136,128]{4,3,2,1,0:T(8,128)}, u32[]{:S(2)}, u32[]{:S(2)}) collective-permute-start(f32[2,2,4,136,128]{4,3,2,1,0:T(8,128)S(1)} %get-tuple-element.46), channel_id=1, source_target_pairs={{0,4},{1,0},{2,6},{3,2},{4,5},{5,1},{6,7},{7,3},{8,12},{9,8},{10,1... | collective-permute-start | bytes 3342344 | tf_op jit(solution)/shard_map/ppermute | solution.py:499
  129.3 4.6 %collective-permute-start.17 = (f32[4,4,144,128]{3,2,1,0:T(8,128)S(1)}, f32[4,4,144,128]{3,2,1,0:T(8,128)S(1)}, u32[]{:S(2)}, u32[]{:S(2)}) collective-permute-start(f32[4,4,144,128]{3,2,1,0:T(8,128)S(1)} %get-tuple-element.63.a_ref), channel_id=1, source_target_pairs={{0,1},{1,0},{2,3},{3,2},{4,5},{5,4},{6,7},{7,6},{8,9},{9,8},{10,11... | collective-permute-start | bytes 3538952 | tf_op jit(solution)/shard_map/ppermute | solution.py:549
  131.5 12.7 %collective-permute-start.16 = (f32[4,4,144,128]{3,2,1,0:T(8,128)S(1)}, f32[4,4,144,128]{3,2,1,0:T(8,128)S(1)}, u32[]{:S(2)}, u32[]{:S(2)}) collective-permute-start(f32[4,4,144,128]{3,2,1,0:T(8,128)S(1)} %get-tuple-element.60.b_ref), channel_id=1, source_target_pairs={{1,8},{8,1},{3,10},{10,3},{5,12},{12,5},{7,14},{14,7},{9,16},{16,9... | collective-permute-start | bytes 3538952 | tf_op jit(solution)/shard_map/ppermute | solution.py:548
  149.1 50.9 %collective-permute-start.24 = (f32[2,2,4,64,128]{4,3,2,1,0:T(8,128)S(1)}, f32[2,2,4,64,128]{4,3,2,1,0:T(8,128)S(1)}, u32[]{:S(2)}, u32[]{:S(2)}) collective-permute-start(f32[2,2,4,64,128]{4,3,2,1,0:T(8,128)S(1)} %get-tuple-element.73), channel_id=1, source_target_pairs={{2,0},{6,1},{0,2},{4,3},{3,4},{7,5},{1,6},{5,7},{10,8},{14,9},{8,1... | collective-permute-start | bytes 1572872 | tf_op jit(solution)/shard_map/ppermute | solution.py:576
  150.2 51.3 %collective-permute-start.25 = (f32[2,2,4,64,128]{4,3,2,1,0:T(8,128)S(1)}, f32[2,2,4,64,128]{4,3,2,1,0:T(8,128)S(1)}, u32[]{:S(2)}, u32[]{:S(2)}) collective-permute-start(f32[2,2,4,64,128]{4,3,2,1,0:T(8,128)S(1)} %get-tuple-element.74), channel_id=1, source_target_pairs={{0,0},{4,1},{2,2},{6,3},{1,4},{5,5},{3,6},{7,7},{8,8},{12,9},{10,1... | collective-permute-start | bytes 1572872 | tf_op jit(solution)/shard_map/ppermute | solution.py:576
  150.9 53.3 %collective-permute-start.22 = (f32[2,2,4,64,128]{4,3,2,1,0:T(8,128)S(1)}, f32[2,2,4,64,128]{4,3,2,1,0:T(8,128)S(1)}, u32[]{:S(2)}, u32[]{:S(2)}) collective-permute-start(f32[2,2,4,64,128]{4,3,2,1,0:T(8,128)S(1)} %get-tuple-element.71), channel_id=1, source_target_pairs={{6,0},{2,1},{4,2},{0,3},{7,4},{3,5},{5,6},{1,7},{14,8},{10,9},{12,... | collective-permute-start | bytes 1572872 | tf_op jit(solution)/shard_map/ppermute | solution.py:576
  158.8 13.9 %collective-permute-start.11 = (f32[1,1]{1,0:T(1,128)}, f32[1,1]{1,0:T(1,128)}, u32[]{:S(2)}, u32[]{:S(2)}) collective-permute-start(f32[1,1]{1,0:T(1,128)} %get-tuple-element.59), channel_id=1, source_target_pairs={{0,2},{1,3},{2,0},{3,1},{4,6},{5,7},{6,4},{7,5},{8,10},{9,11},{10,... | collective-permute-start | bytes 20 | tf_op jit(solution)/shard_map/ppermute | solution.py:471
  174.0 9.2 %collective-permute-start.12 = (f32[1,1]{1,0:T(1,128)}, f32[1,1]{1,0:T(1,128)}, u32[]{:S(2)}, u32[]{:S(2)}) collective-permute-start(f32[1,1]{1,0:T(1,128)} %add.19), channel_id=1, source_target_pairs={{0,4},{1,5},{2,6},{3,7},{4,0},{5,1},{6,2},{7,3},{8,12},{9,13},{10,... | collective-permute-start | bytes 20 | tf_op jit(solution)/shard_map/ppermute | solution.py:471
  190.6 8.3 %collective-permute-start.15 = (f32[1,1]{1,0:T(1,128)}, f32[1,1]{1,0:T(1,128)}, u32[]{:S(2)}, u32[]{:S(2)}) collective-permute-start(f32[1,1]{1,0:T(1,128)} %add.22), channel_id=1, source_target_pairs={{0,16},{1,17},{2,18},{3,19},{4,20},{5,21},{6,22},{7,23},{8,24},{9,... | collective-permute-start | bytes 20 | tf_op jit(solution)/shard_map/ppermute | solution.py:471
  195.0 12.8 %collective-permute-start.23 = (f32[2,2,4,64,128]{4,3,2,1,0:T(8,128)S(1)}, f32[2,2,4,64,128]{4,3,2,1,0:T(8,128)}, u32[]{:S(2)}, u32[]{:S(2)}) collective-permute-start(f32[2,2,4,64,128]{4,3,2,1,0:T(8,128)S(1)} %get-tuple-element.72), channel_id=1, source_target_pairs={{4,0},{0,1},{6,2},{2,3},{5,4},{1,5},{7,6},{3,7},{12,8},{8,9},{14,1... | collective-permute-start | bytes 1572872 | tf_op jit(solution)/shard_map/ppermute | solution.py:576
  199.0 14.1 %collective-permute-start.20 = (f32[2,2,4,64,128]{4,3,2,1,0:T(8,128)S(1)}, f32[2,2,4,64,128]{4,3,2,1,0:T(8,128)}, u32[]{:S(2)}, u32[]{:S(2)}) collective-permute-start(f32[2,2,4,64,128]{4,3,2,1,0:T(8,128)S(1)} %get-tuple-element.69), channel_id=1, source_target_pairs={{2,0},{6,1},{0,2},{4,3},{3,4},{7,5},{1,6},{5,7},{10,8},{14,9},{8,1... | collective-permute-start | bytes 1572872 | tf_op jit(solution)/shard_map/ppermute | solution.py:576
  200.0 13.0 %collective-permute-start.21 = (f32[2,2,4,64,128]{4,3,2,1,0:T(8,128)S(1)}, f32[2,2,4,64,128]{4,3,2,1,0:T(8,128)}, u32[]{:S(2)}, u32[]{:S(2)}) collective-permute-start(f32[2,2,4,64,128]{4,3,2,1,0:T(8,128)S(1)} %get-tuple-element.70), channel_id=1, source_target_pairs={{0,0},{4,1},{2,2},{6,3},{1,4},{5,5},{3,6},{7,7},{8,8},{12,9},{10,1... | collective-permute-start | bytes 1572872 | tf_op jit(solution)/shard_map/ppermute | solution.py:576
  201.5 23.4 %collective-permute-start.18 = (f32[2,2,4,64,128]{4,3,2,1,0:T(8,128)S(1)}, f32[2,2,4,64,128]{4,3,2,1,0:T(8,128)}, u32[]{:S(2)}, u32[]{:S(2)}) collective-permute-start(f32[2,2,4,64,128]{4,3,2,1,0:T(8,128)S(1)} %get-tuple-element.67), channel_id=1, source_target_pairs={{6,0},{2,1},{4,2},{0,3},{7,4},{3,5},{5,6},{1,7},{14,8},{10,9},{12,... | collective-permute-start | bytes 1572872 | tf_op jit(solution)/shard_map/ppermute | solution.py:576
  204.2 23.2 %collective-permute-start.19 = (f32[2,2,4,64,128]{4,3,2,1,0:T(8,128)S(1)}, f32[2,2,4,64,128]{4,3,2,1,0:T(8,128)}, u32[]{:S(2)}, u32[]{:S(2)}) collective-permute-start(f32[2,2,4,64,128]{4,3,2,1,0:T(8,128)S(1)} %get-tuple-element.68), channel_id=1, source_target_pairs={{4,0},{0,1},{6,2},{2,3},{5,4},{1,5},{7,6},{3,7},{12,8},{8,9},{14,1... | collective-permute-start | bytes 1572872 | tf_op jit(solution)/shard_map/ppermute | solution.py:576
  (15 other events, 123.0 us)

commit v7 on v6

--- a/solution.py
+++ b/solution.py
@@ -585,21 +585,21 @@
     inverse = 1.0 / misfit
     scale = jnp.stack([time_step * inverse, inverse]).reshape(1, 2)
     held = []
-    for n in range(0, 8, 2):
+    for n, size in ((0, 2), (2, 2), (4, 2), (6, 1), (7, 1)):
         held = pl.pallas_call(
-            partial(home_kernel, n // 4 * strip, ROUNDS[n % 4 : n % 4 + 2]),
+            partial(home_kernel, n // 4 * strip, ROUNDS[n % 4 : n % 4 + size]),
             out_shape=[jax.ShapeDtypeStruct((planes, height, width), F32)] * 2,
-            in_specs=[SM, SM, ANY, ANY] + [ANY] * len(held),
+            in_specs=[SM, SM] + [ANY] * (size + len(held)),
             out_specs=[ANY] * 2,
             scratch_shapes=[
-                pltpu.VMEM((2, 2, planes, blocks, strip, LANES), F32),
-                pltpu.VMEM((2, 2, planes, strip, width), F32),
-                pltpu.SemaphoreType.DMA((2,)),
-                pltpu.SemaphoreType.DMA((2, 2)),
+                pltpu.VMEM((size, 2, planes, blocks, strip, LANES), F32),
+                pltpu.VMEM((size, 2, planes, strip, width), F32),
+                pltpu.SemaphoreType.DMA((size,)),
+                pltpu.SemaphoreType.DMA((size, 2)),
             ],
-            input_output_aliases={4: 0, 5: 1} if held else {},
+            input_output_aliases={2 + size: 0, 3 + size: 1} if held else {},
             compiler_params=pltpu.CompilerParams(vmem_limit_bytes=14 << 20),
-        )(me, scale, *back[n : n + 2], *held)
+        )(me, scale, *back[n : n + size], *held)
     gradient, adjoint = held
     return gradient, adjoint, misfit
 

time: 232 us -> 232 us (level)
    ppermute x8, waiting for transfers between devices: 14.3 us -> 11.8 us  [on_device(): lax.ppermute(m, axis, [(j, i) for i, j in send_pairs(count, *r)])]
    pallas_call x4 -> x5, Pallas kernels: 10.5 us -> 12.7 us  [on_device(): pl.pallas_call(partial(home_kernel, n // 4 * strip, ROUNDS[n % 4:n % 4 +...]
    unnamed x26 -> x28, local copies, waits for them, and re-layouts: 4.44 us -> 5.2 us
  transfers between devices with their start and end apart: 26 -> 26, of which waited for: 13 -> 12; matrix products, arithmetic and copies ran while one was open for 0% -> 0% of each run, Pallas kernels for 17% -> 18%
where the time goes in v7:
time: 232 us; the launch traced here: 231 us
  waiting for transfers between devices  102 us (44%)
  starting transfers between devices  62 us (27%)
  Pallas kernels  56.4 us (24%)
  between operations  5.71 us (2%)
  local copies, waits for them, and re-layouts  5.2 us (2%)
    ppermute x8, waiting for transfers between devices, regroup(): got.append(lax.ppermute(m, axis, send_pairs(count, *r)))  74.6 us
    pallas_call x10, Pallas kernels, call(): pl.pallas_call(kernel, out_shape=outs, in_specs=[SM] * len(scalars) + [AN...  43.7 us
    ppermute x8, starting transfers between devices, regroup(): got.append(lax.ppermute(m, axis, send_pairs(count, *r)))  20.7 us
    ppermute x5, starting transfers between devices, exchange_sum(): lax.ppermute(value, axis, [(i, i ^ step) for i in range(count)])  19.1 us
    ppermute x8, starting transfers between devices, on_device(): lax.ppermute(m, axis, [(j, i) for i, j in send_pairs(count, *r)])  14.9 us
    ppermute x5, waiting for transfers between devices, exchange_sum(): lax.ppermute(value, axis, [(i, i ^ step) for i in range(count)])  13.9 us
    pallas_call x5, Pallas kernels, on_device(): pl.pallas_call(partial(home_kernel, n // 4 * strip, ROUNDS[n % 4:n % 4 +...  12.7 us
    ppermute x8, waiting for transfers between devices, on_device(): lax.ppermute(m, axis, [(j, i) for i, j in send_pairs(count, *r)])  11.8 us
  transfers between devices with their start and end apart: 26, of which 12 were waited for; matrix products, arithmetic and copies ran while one was open for 0% of the time, Pallas kernels for 18%

profile of v7, /device:TPU:0, one launch (start us, length us, event | category | flops | bytes accessed | tf_op | source)
XLA Modules:
  0.0 231.4 jit_solution(13594516194215285645)
XLA Ops:
  3.2 3.0 %collective-permute-start.4 = (f32[2,2,4,144,128]{4,3,2,1,0:T(8,128)S(1)}, f32[2,2,4,144,128]{4,3,2,1,0:T(8,128)S(1)}, u32[]{:S(2)}, u32[]{:S(2)}) collective-permute-start(f32[2,2,4,144,128]{4,3,2,1,0:T(8,128)S(1)} %get-tuple-element.49), channel_id=1, source_target_pairs={{0,2},{1,6},{2,0},{3,4},{4,3},{5,7},{6,1},{7,5},{8,10},{9,14},{10,... | collective-permute-start | bytes 3538952 | tf_op jit(solution)/shard_map/ppermute | solution.py:499
  7.0 3.9 %collective-permute-start.7 = (f32[2,2,4,144,128]{4,3,2,1,0:T(8,128)S(1)}, f32[2,2,4,144,128]{4,3,2,1,0:T(8,128)S(1)}, u32[]{:S(2)}, u32[]{:S(2)}) collective-permute-start(f32[2,2,4,144,128]{4,3,2,1,0:T(8,128)S(1)} %get-tuple-element.51), channel_id=1, source_target_pairs={{0,6},{1,2},{2,4},{3,0},{4,7},{5,3},{6,5},{7,1},{8,14},{9,10},{10,... | collective-permute-start | bytes 3538952 | tf_op jit(solution)/shard_map/ppermute | solution.py:499
  10.9 21.3 %collective-permute-done.4.m0 = f32[2,2,4,144,128]{4,3,2,1,0:T(8,128)S(1)} collective-permute-done((f32[2,2,4,144,128]{4,3,2,1,0:T(8,128)S(1)}, f32[2,2,4,144,128]{4,3,2,1,0:T(8,128)S(1)}, u32[]{:S(2)}, u32[]{:S(2)}) %collective-permute-start.4) | collective-permute-done | bytes 1179680 | tf_op jit(solution)/shard_map/ppermute | solution.py:499
  32.2 26.2 %collective-permute-done.7.m2 = f32[2,2,4,144,128]{4,3,2,1,0:T(8,128)S(1)} collective-permute-done((f32[2,2,4,144,128]{4,3,2,1,0:T(8,128)S(1)}, f32[2,2,4,144,128]{4,3,2,1,0:T(8,128)S(1)}, u32[]{:S(2)}, u32[]{:S(2)}) %collective-permute-start.7) | collective-permute-done | bytes 1179680 | tf_op jit(solution)/shard_map/ppermute | solution.py:499
  60.5 2.7 %shard_map.70 = (f32[2,2,4,144,128]{4,3,2,1,0:T(8,128)S(1)}, f32[2,4,4,144,128]{4,3,2,1,0:T(8,128)S(1)}, f32[2,4,4,144,128]{4,3,2,1,0:T(8,128)S(1)}) custom-call(s32[1]{0:T(128)} %bitcast.me_ref, f32[2,2,4,144,128]{4,3,2,1,0:T(8,128)} %copy-done, f32[2,2,4,144,128]{4,3,2,1,0:T(8,128)} %copy-done.1, f32[2,2,4,144,128]{4,3,2,1,0:T(8,128)} %copy-done.7, ...), custom_call_target="tpu_custom_call" | custom-call | tf_op jit(solution)/shard_map/pallas_call | solution.py:29
  63.2 2.8 %collective-permute-start.10 = (f32[2,4,4,144,128]{4,3,2,1,0:T(8,128)S(1)}, f32[2,4,4,144,128]{4,3,2,1,0:T(8,128)S(1)}, u32[]{:S(2)}, u32[]{:S(2)}) collective-permute-start(f32[2,4,4,144,128]{4,3,2,1,0:T(8,128)S(1)} %get-tuple-element.55.a_ref), channel_id=1, source_target_pairs={{0,1},{1,0},{2,3},{3,2},{4,5},{5,4},{6,7},{7,6},{8,9},{9,8},{10,11... | collective-permute-start | bytes 7077896 | tf_op jit(solution)/shard_map/ppermute | solution.py:514
  74.4 6.0 %collective-permute-start.2 = (f32[2,2,4,136,128]{4,3,2,1,0:T(8,128)S(1)}, f32[2,2,4,136,128]{4,3,2,1,0:T(8,128)}, u32[]{:S(2)}, u32[]{:S(2)}) collective-permute-start(f32[2,2,4,136,128]{4,3,2,1,0:T(8,128)S(1)} %get-tuple-element.47), channel_id=1, source_target_pairs={{0,6},{1,2},{2,4},{3,0},{4,7},{5,3},{6,5},{7,1},{8,14},{9,10},{10,... | collective-permute-start | bytes 3342344 | tf_op jit(solution)/shard_map/ppermute | solution.py:499
  80.5 4.3 %collective-permute-start.3 = (f32[2,2,4,136,128]{4,3,2,1,0:T(8,128)S(1)}, f32[2,2,4,136,128]{4,3,2,1,0:T(8,128)}, u32[]{:S(2)}, u32[]{:S(2)}) collective-permute-start(f32[2,2,4,136,128]{4,3,2,1,0:T(8,128)S(1)} %get-tuple-element.48), channel_id=1, source_target_pairs={{0,4},{1,0},{2,6},{3,2},{4,5},{5,1},{6,7},{7,3},{8,12},{9,8},{10,1... | collective-permute-start | bytes 3342344 | tf_op jit(solution)/shard_map/ppermute | solution.py:499
  84.7 8.6 %shard_map.71 = (f32[8,4,144,128]{3,2,1,0:T(8,128)S(1)}, f32[12,4,144,128]{3,2,1,0:T(8,128)S(1)}, f32[4,8,4,144,128]{4,3,2,1,0:T(8,128)S(1)}, f32[3,2,4,144,128]{4,3,2,1,0:T(8,128)S(1)}) custom-call(s32[1]{0:T(128)} %bitcast.me_ref, f32[2,4,4,144,128]{4,3,2,1,0:T(8,128)S(1)} %get-tuple-element.55.a_ref, f32[2,4,4,144,128]{4,3,2,1,0:T(8,128)S(1)} %get-tuple-element.54.b_ref, ...), custom_call_target="tpu_custom_call" | custom-call | tf_op jit(solution)/shard_map/pallas_call | solution.py:29
  94.4 5.5 %shard_map.72 = (f32[8,4,144,128]{3,2,1,0:T(8,128)S(1)}, f32[4,8,4,144,128]{4,3,2,1,0:T(8,128)S(1)}, f32[4,4,144,128]{3,2,1,0:T(8,128)S(1)}) custom-call(s32[1]{0:T(128)} %bitcast.me_ref, f32[2,2,4,144,128]{4,3,2,1,0:T(8,128)} %copy-done.5, f32[2,2,4,144,128]{4,3,2,1,0:T(8,128)} %copy-done.4, ...), custom_call_target="tpu_custom_call", output_to_operand_aliasing={{0}: (6, {}), {1}: (7, {})} | custom-call | tf_op jit(solution)/shard_map/pallas_call | solution.py:29
  99.9 23.4 %collective-permute-done.2.f2 = f32[2,2,4,136,128]{4,3,2,1,0:T(8,128)} collective-permute-done((f32[2,2,4,136,128]{4,3,2,1,0:T(8,128)S(1)}, f32[2,2,4,136,128]{4,3,2,1,0:T(8,128)}, u32[]{:S(2)}, u32[]{:S(2)}) %collective-permute-start.2) | collective-permute-done | bytes 1114144 | tf_op jit(solution)/shard_map/ppermute | solution.py:499
  123.3 3.0 %collective-permute-done.3.f3 = f32[2,2,4,136,128]{4,3,2,1,0:T(8,128)} collective-permute-done((f32[2,2,4,136,128]{4,3,2,1,0:T(8,128)S(1)}, f32[2,2,4,136,128]{4,3,2,1,0:T(8,128)}, u32[]{:S(2)}, u32[]{:S(2)}) %collective-permute-start.3) | collective-permute-done | bytes 1114144 | tf_op jit(solution)/shard_map/ppermute | solution.py:499
  126.3 3.0 %shard_map.73 = (f32[4,4,144,128]{3,2,1,0:T(8,128)S(1)}, f32[4,4,144,128]{3,2,1,0:T(8,128)S(1)}, f32[1,1]{1,0:T(1,128)}) custom-call(s32[1]{0:T(128)} %bitcast.me_ref, f32[2,2,4,136,128]{4,3,2,1,0:T(8,128)} %copy-done.9, f32[2,2,4,136,128]{4,3,2,1,0:T(8,128)} %collective-permute-done.1.f1, f32[2,2,4,136,128]{4,3,2,1,0:T(8,128)} %collective-permute-done.2.f2, ...), custom_call_target="tpu_custom_call" | custom-call | tf_op jit(solution)/shard_map/pallas_call | solution.py:29
  135.0 9.2 %shard_map.74 = (f32[12,4,144,128]{3,2,1,0:T(8,128)S(1)}, f32[8,4,128,128]{3,2,1,0:T(8,128)S(1)}, f32[3,2,4,144,128]{4,3,2,1,0:T(8,128)S(1)}) custom-call(s32[1]{0:T(128)} %bitcast.me_ref, f32[4,4,144,128]{3,2,1,0:T(8,128)} %copy-done.6, f32[4,4,144,128]{3,2,1,0:T(8,128)S(1)} %get-tuple-element.65.a_ref, f32[4,4,144,128]{3,2,1,0:T(8,128)S(1)} %get-tuple-element.62.b_ref, ...), custom_call_target="tpu_custom_call" | custom-call | tf_op jit(solution)/shard_map/pallas_call | solution.py:29
  145.2 3.9 %shard_map.76 = (f32[2,2,4,64,128]{4,3,2,1,0:T(8,128)S(1)}, f32[2,2,4,64,128]{4,3,2,1,0:T(8,128)S(1)}, f32[2,2,4,64,128]{4,3,2,1,0:T(8,128)S(1)}, f32[2,2,4,64,128]{4,3,2,1,0:T(8,128)S(1)}) custom-call(s32[1]{0:T(128)} %bitcast.me_ref, f32[4,4,144,128]{3,2,1,0:T(8,128)} %copy-done.2, f32[4,4,144,128]{3,2,1,0:T(8,128)S(1)} %get-tuple-element.62.b_ref, ...), custom_call_target="tpu_custom_call" | custom-call | tf_op jit(solution)/shard_map/pallas_call | solution.py:29
  150.9 7.9 %collective-permute-start.22 = (f32[2,2,4,64,128]{4,3,2,1,0:T(8,128)S(1)}, f32[2,2,4,64,128]{4,3,2,1,0:T(8,128)S(1)}, u32[]{:S(2)}, u32[]{:S(2)}) collective-permute-start(f32[2,2,4,64,128]{4,3,2,1,0:T(8,128)S(1)} %get-tuple-element.73), channel_id=1, source_target_pairs={{6,0},{2,1},{4,2},{0,3},{7,4},{3,5},{5,6},{1,7},{14,8},{10,9},{12,... | collective-permute-start | bytes 1572872 | tf_op jit(solution)/shard_map/ppermute | solution.py:576
  159.8 12.9 %collective-permute-done.11 = f32[1,1]{1,0:T(1,128)} collective-permute-done((f32[1,1]{1,0:T(1,128)}, f32[1,1]{1,0:T(1,128)}, u32[]{:S(2)}, u32[]{:S(2)}) %collective-permute-start.11) | collective-permute-done | bytes 36 | tf_op jit(solution)/shard_map/ppermute | solution.py:471
  173.9 8.9 %collective-permute-start.12 = (f32[1,1]{1,0:T(1,128)}, f32[1,1]{1,0:T(1,128)}, u32[]{:S(2)}, u32[]{:S(2)}) collective-permute-start(f32[1,1]{1,0:T(1,128)} %add.19), channel_id=1, source_target_pairs={{0,4},{1,5},{2,6},{3,7},{4,0},{5,1},{6,2},{7,3},{8,12},{9,13},{10,... | collective-permute-start | bytes 20 | tf_op jit(solution)/shard_map/ppermute | solution.py:471
  185.6 3.8 %collective-permute-start.14 = (f32[1,1]{1,0:T(1,128)}, f32[1,1]{1,0:T(1,128)}, u32[]{:S(2)}, u32[]{:S(2)}) collective-permute-start(f32[1,1]{1,0:T(1,128)} %add.21), channel_id=1, source_target_pairs={{0,8},{1,9},{2,10},{3,11},{4,12},{5,13},{6,14},{7,15},{8,0},{9,1},... | collective-permute-start | bytes 20 | tf_op jit(solution)/shard_map/ppermute | solution.py:471
  190.3 4.4 %collective-permute-start.15 = (f32[1,1]{1,0:T(1,128)}, f32[1,1]{1,0:T(1,128)}, u32[]{:S(2)}, u32[]{:S(2)}) collective-permute-start(f32[1,1]{1,0:T(1,128)} %add.22), channel_id=1, source_target_pairs={{0,16},{1,17},{2,18},{3,19},{4,20},{5,21},{6,22},{7,23},{8,24},{9,... | collective-permute-start | bytes 20 | tf_op jit(solution)/shard_map/ppermute | solution.py:471
  194.7 3.9 %shard_map.75 = (f32[2,2,4,64,128]{4,3,2,1,0:T(8,128)S(1)}, f32[2,2,4,64,128]{4,3,2,1,0:T(8,128)S(1)}, f32[2,2,4,64,128]{4,3,2,1,0:T(8,128)S(1)}, f32[2,2,4,64,128]{4,3,2,1,0:T(8,128)S(1)}) custom-call(s32[1]{0:T(128)} %bitcast.me_ref, f32[4,4,144,128]{3,2,1,0:T(8,128)} %copy-done.2, f32[4,4,144,128]{3,2,1,0:T(8,128)S(1)} %get-tuple-element.62.b_ref, ...), custom_call_target="tpu_custom_call" | custom-call | tf_op jit(solution)/shard_map/pallas_call | solution.py:29
  201.2 2.8 %collective-permute-start.19 = (f32[2,2,4,64,128]{4,3,2,1,0:T(8,128)S(1)}, f32[2,2,4,64,128]{4,3,2,1,0:T(8,128)}, u32[]{:S(2)}, u32[]{:S(2)}) collective-permute-start(f32[2,2,4,64,128]{4,3,2,1,0:T(8,128)S(1)} %get-tuple-element.70), channel_id=1, source_target_pairs={{6,0},{2,1},{4,2},{0,3},{7,4},{3,5},{5,6},{1,7},{14,8},{10,9},{12,... | collective-permute-start | bytes 1572872 | tf_op jit(solution)/shard_map/ppermute | solution.py:576
  207.5 2.6 %shard_map.78 = (f32[2,512,512]{2,1,0:T(8,128)}, f32[2,512,512]{2,1,0:T(8,128)}) custom-call(s32[1]{0:T(128)} %bitcast.me_ref, f32[1,2]{1,0:T(1,128)S(1)} %maximum_bitcast_fusion.scale_ref, f32[2,2,4,64,128]{4,3,2,1,0:T(8,128)} %copy-done.13, f32[2,2,4,64,128]{4,3,2,1,0:T(8,128)} %collective-permute-done.23.refs_1_, ...), custom_call_target="tpu_custom_call", output_to_operand_aliasing={{0}: (4, {}), {1}: (5, {})} | custom-call | tf_op jit(solution)/shard_map/pallas_call | solution.py:589
  215.4 9.2 %collective-permute-done.19.refs_0_ = f32[2,2,4,64,128]{4,3,2,1,0:T(8,128)} collective-permute-done((f32[2,2,4,64,128]{4,3,2,1,0:T(8,128)S(1)}, f32[2,2,4,64,128]{4,3,2,1,0:T(8,128)}, u32[]{:S(2)}, u32[]{:S(2)}) %collective-permute-start.19) | collective-permute-done | bytes 524320 | tf_op jit(solution)/shard_map/ppermute | solution.py:576
  (72 shorter events, 42.5 us)
Async XLA Ops:
  3.2 29.0 %collective-permute-start.4 = (f32[2,2,4,144,128]{4,3,2,1,0:T(8,128)S(1)}, f32[2,2,4,144,128]{4,3,2,1,0:T(8,128)S(1)}, u32[]{:S(2)}, u32[]{:S(2)}) collective-permute-start(f32[2,2,4,144,128]{4,3,2,1,0:T(8,128)S(1)} %get-tuple-element.49), channel_id=1, source_target_pairs={{0,2},{1,6},{2,0},{3,4},{4,3},{5,7},{6,1},{7,5},{8,10},{9,14},{10,... | collective-permute-start | bytes 3538952 | tf_op jit(solution)/shard_map/ppermute | solution.py:499
  6.2 26.0 %collective-permute-start.5 = (f32[2,2,4,144,128]{4,3,2,1,0:T(8,128)S(1)}, f32[2,2,4,144,128]{4,3,2,1,0:T(8,128)S(1)}, u32[]{:S(2)}, u32[]{:S(2)}) collective-permute-start(f32[2,2,4,144,128]{4,3,2,1,0:T(8,128)S(1)} %get-tuple-element.50), channel_id=1, source_target_pairs={{0,0},{1,4},{2,2},{3,6},{4,1},{5,5},{6,3},{7,7},{8,8},{9,12},{10,1... | collective-permute-start | bytes 3538952 | tf_op jit(solution)/shard_map/ppermute | solution.py:499
  7.0 51.4 %collective-permute-start.7 = (f32[2,2,4,144,128]{4,3,2,1,0:T(8,128)S(1)}, f32[2,2,4,144,128]{4,3,2,1,0:T(8,128)S(1)}, u32[]{:S(2)}, u32[]{:S(2)}) collective-permute-start(f32[2,2,4,144,128]{4,3,2,1,0:T(8,128)S(1)} %get-tuple-element.51), channel_id=1, source_target_pairs={{0,6},{1,2},{2,4},{3,0},{4,7},{5,3},{6,5},{7,1},{8,14},{9,10},{10,... | collective-permute-start | bytes 3538952 | tf_op jit(solution)/shard_map/ppermute | solution.py:499
  10.9 48.3 %collective-permute-start.8 = (f32[2,2,4,144,128]{4,3,2,1,0:T(8,128)S(1)}, f32[2,2,4,144,128]{4,3,2,1,0:T(8,128)S(1)}, u32[]{:S(2)}, u32[]{:S(2)}) collective-permute-start(f32[2,2,4,144,128]{4,3,2,1,0:T(8,128)S(1)} %get-tuple-element.52), channel_id=1, source_target_pairs={{0,4},{1,0},{2,6},{3,2},{4,5},{5,1},{6,7},{7,3},{8,12},{9,8},{10,1... | collective-permute-start | bytes 3538952 | tf_op jit(solution)/shard_map/ppermute | solution.py:499
  63.2 17.2 %collective-permute-start.10 = (f32[2,4,4,144,128]{4,3,2,1,0:T(8,128)S(1)}, f32[2,4,4,144,128]{4,3,2,1,0:T(8,128)S(1)}, u32[]{:S(2)}, u32[]{:S(2)}) collective-permute-start(f32[2,4,4,144,128]{4,3,2,1,0:T(8,128)S(1)} %get-tuple-element.55.a_ref), channel_id=1, source_target_pairs={{0,1},{1,0},{2,3},{3,2},{4,5},{5,4},{6,7},{7,6},{8,9},{9,8},{10,11... | collective-permute-start | bytes 7077896 | tf_op jit(solution)/shard_map/ppermute | solution.py:514
  66.0 8.4 %collective-permute-start.9 = (f32[2,2,4,144,128]{4,3,2,1,0:T(8,128)S(1)}, f32[2,2,4,144,128]{4,3,2,1,0:T(8,128)S(1)}, u32[]{:S(2)}, u32[]{:S(2)}) collective-permute-start(f32[2,2,4,144,128]{4,3,2,1,0:T(8,128)S(1)} %get-tuple-element.53), channel_id=1, source_target_pairs={{1,8},{8,1},{3,10},{10,3},{5,12},{12,5},{7,14},{14,7},{9,16},{16,9... | collective-permute-start | bytes 3538952 | tf_op jit(solution)/shard_map/ppermute | solution.py:513
  68.4 24.9 %collective-permute-start.6 = (f32[2,2,4,144,128]{4,3,2,1,0:T(8,128)S(1)}, f32[2,2,4,144,128]{4,3,2,1,0:T(8,128)S(1)}, u32[]{:S(2)}, u32[]{:S(2)}) collective-permute-start(f32[2,2,4,144,128]{4,3,2,1,0:T(8,128)S(1)} %shard_map.69), channel_id=1, source_target_pairs={{1,8},{8,1},{3,10},{10,3},{5,12},{12,5},{7,14},{14,7},{9,16},{16,9... | collective-permute-start | bytes 3538952 | tf_op jit(solution)/shard_map/ppermute | solution.py:511
  71.7 28.1 %collective-permute-start = (f32[2,2,4,136,128]{4,3,2,1,0:T(8,128)S(1)}, f32[2,2,4,136,128]{4,3,2,1,0:T(8,128)S(1)}, u32[]{:S(2)}, u32[]{:S(2)}) collective-permute-start(f32[2,2,4,136,128]{4,3,2,1,0:T(8,128)S(1)} %get-tuple-element.45), channel_id=1, source_target_pairs={{0,2},{1,6},{2,0},{3,4},{4,3},{5,7},{6,1},{7,5},{8,10},{9,14},{10,... | collective-permute-start | bytes 3342344 | tf_op jit(solution)/shard_map/ppermute | solution.py:499
  72.8 27.1 %collective-permute-start.1 = (f32[2,2,4,136,128]{4,3,2,1,0:T(8,128)S(1)}, f32[2,2,4,136,128]{4,3,2,1,0:T(8,128)}, u32[]{:S(2)}, u32[]{:S(2)}) collective-permute-start(f32[2,2,4,136,128]{4,3,2,1,0:T(8,128)S(1)} %get-tuple-element.46), channel_id=1, source_target_pairs={{0,0},{1,4},{2,2},{3,6},{4,1},{5,5},{6,3},{7,7},{8,8},{9,12},{10,1... | collective-permute-start | bytes 3342344 | tf_op jit(solution)/shard_map/ppermute | solution.py:499
  74.4 48.8 %collective-permute-start.2 = (f32[2,2,4,136,128]{4,3,2,1,0:T(8,128)S(1)}, f32[2,2,4,136,128]{4,3,2,1,0:T(8,128)}, u32[]{:S(2)}, u32[]{:S(2)}) collective-permute-start(f32[2,2,4,136,128]{4,3,2,1,0:T(8,128)S(1)} %get-tuple-element.47), channel_id=1, source_target_pairs={{0,6},{1,2},{2,4},{3,0},{4,7},{5,3},{6,5},{7,1},{8,14},{9,10},{10,... | collective-permute-start | bytes 3342344 | tf_op jit(solution)/shard_map/ppermute | solution.py:499
  80.5 45.8 %collective-permute-start.3 = (f32[2,2,4,136,128]{4,3,2,1,0:T(8,128)S(1)}, f32[2,2,4,136,128]{4,3,2,1,0:T(8,128)}, u32[]{:S(2)}, u32[]{:S(2)}) collective-permute-start(f32[2,2,4,136,128]{4,3,2,1,0:T(8,128)S(1)} %get-tuple-element.48), channel_id=1, source_target_pairs={{0,4},{1,0},{2,6},{3,2},{4,5},{5,1},{6,7},{7,3},{8,12},{9,8},{10,1... | collective-permute-start | bytes 3342344 | tf_op jit(solution)/shard_map/ppermute | solution.py:499
  129.3 4.6 %collective-permute-start.17 = (f32[4,4,144,128]{3,2,1,0:T(8,128)S(1)}, f32[4,4,144,128]{3,2,1,0:T(8,128)S(1)}, u32[]{:S(2)}, u32[]{:S(2)}) collective-permute-start(f32[4,4,144,128]{3,2,1,0:T(8,128)S(1)} %get-tuple-element.65.a_ref), channel_id=1, source_target_pairs={{0,1},{1,0},{2,3},{3,2},{4,5},{5,4},{6,7},{7,6},{8,9},{9,8},{10,11... | collective-permute-start | bytes 3538952 | tf_op jit(solution)/shard_map/ppermute | solution.py:549
  131.5 12.7 %collective-permute-start.16 = (f32[4,4,144,128]{3,2,1,0:T(8,128)S(1)}, f32[4,4,144,128]{3,2,1,0:T(8,128)S(1)}, u32[]{:S(2)}, u32[]{:S(2)}) collective-permute-start(f32[4,4,144,128]{3,2,1,0:T(8,128)S(1)} %get-tuple-element.62.b_ref), channel_id=1, source_target_pairs={{1,8},{8,1},{3,10},{10,3},{5,12},{12,5},{7,14},{14,7},{9,16},{16,9... | collective-permute-start | bytes 3538952 | tf_op jit(solution)/shard_map/ppermute | solution.py:548
  149.1 50.6 %collective-permute-start.24 = (f32[2,2,4,64,128]{4,3,2,1,0:T(8,128)S(1)}, f32[2,2,4,64,128]{4,3,2,1,0:T(8,128)S(1)}, u32[]{:S(2)}, u32[]{:S(2)}) collective-permute-start(f32[2,2,4,64,128]{4,3,2,1,0:T(8,128)S(1)} %get-tuple-element.75), channel_id=1, source_target_pairs={{2,0},{6,1},{0,2},{4,3},{3,4},{7,5},{1,6},{5,7},{10,8},{14,9},{8,1... | collective-permute-start | bytes 1572872 | tf_op jit(solution)/shard_map/ppermute | solution.py:576
  150.2 50.9 %collective-permute-start.25 = (f32[2,2,4,64,128]{4,3,2,1,0:T(8,128)S(1)}, f32[2,2,4,64,128]{4,3,2,1,0:T(8,128)S(1)}, u32[]{:S(2)}, u32[]{:S(2)}) collective-permute-start(f32[2,2,4,64,128]{4,3,2,1,0:T(8,128)S(1)} %get-tuple-element.76), channel_id=1, source_target_pairs={{0,0},{4,1},{2,2},{6,3},{1,4},{5,5},{3,6},{7,7},{8,8},{12,9},{10,1... | collective-permute-start | bytes 1572872 | tf_op jit(solution)/shard_map/ppermute | solution.py:576
  150.9 53.0 %collective-permute-start.22 = (f32[2,2,4,64,128]{4,3,2,1,0:T(8,128)S(1)}, f32[2,2,4,64,128]{4,3,2,1,0:T(8,128)S(1)}, u32[]{:S(2)}, u32[]{:S(2)}) collective-permute-start(f32[2,2,4,64,128]{4,3,2,1,0:T(8,128)S(1)} %get-tuple-element.73), channel_id=1, source_target_pairs={{6,0},{2,1},{4,2},{0,3},{7,4},{3,5},{5,6},{1,7},{14,8},{10,9},{12,... | collective-permute-start | bytes 1572872 | tf_op jit(solution)/shard_map/ppermute | solution.py:576
  158.8 13.9 %collective-permute-start.11 = (f32[1,1]{1,0:T(1,128)}, f32[1,1]{1,0:T(1,128)}, u32[]{:S(2)}, u32[]{:S(2)}) collective-permute-start(f32[1,1]{1,0:T(1,128)} %get-tuple-element.61), channel_id=1, source_target_pairs={{0,2},{1,3},{2,0},{3,1},{4,6},{5,7},{6,4},{7,5},{8,10},{9,11},{10,... | collective-permute-start | bytes 20 | tf_op jit(solution)/shard_map/ppermute | solution.py:471
  173.9 9.2 %collective-permute-start.12 = (f32[1,1]{1,0:T(1,128)}, f32[1,1]{1,0:T(1,128)}, u32[]{:S(2)}, u32[]{:S(2)}) collective-permute-start(f32[1,1]{1,0:T(1,128)} %add.19), channel_id=1, source_target_pairs={{0,4},{1,5},{2,6},{3,7},{4,0},{5,1},{6,2},{7,3},{8,12},{9,13},{10,... | collective-permute-start | bytes 20 | tf_op jit(solution)/shard_map/ppermute | solution.py:471
  190.3 8.3 %collective-permute-start.15 = (f32[1,1]{1,0:T(1,128)}, f32[1,1]{1,0:T(1,128)}, u32[]{:S(2)}, u32[]{:S(2)}) collective-permute-start(f32[1,1]{1,0:T(1,128)} %add.22), channel_id=1, source_target_pairs={{0,16},{1,17},{2,18},{3,19},{4,20},{5,21},{6,22},{7,23},{8,24},{9,... | collective-permute-start | bytes 20 | tf_op jit(solution)/shard_map/ppermute | solution.py:471
  194.7 12.8 %collective-permute-start.23 = (f32[2,2,4,64,128]{4,3,2,1,0:T(8,128)S(1)}, f32[2,2,4,64,128]{4,3,2,1,0:T(8,128)}, u32[]{:S(2)}, u32[]{:S(2)}) collective-permute-start(f32[2,2,4,64,128]{4,3,2,1,0:T(8,128)S(1)} %get-tuple-element.74), channel_id=1, source_target_pairs={{4,0},{0,1},{6,2},{2,3},{5,4},{1,5},{7,6},{3,7},{12,8},{8,9},{14,1... | collective-permute-start | bytes 1572872 | tf_op jit(solution)/shard_map/ppermute | solution.py:576
  198.6 14.1 %collective-permute-start.20 = (f32[2,2,4,64,128]{4,3,2,1,0:T(8,128)S(1)}, f32[2,2,4,64,128]{4,3,2,1,0:T(8,128)}, u32[]{:S(2)}, u32[]{:S(2)}) collective-permute-start(f32[2,2,4,64,128]{4,3,2,1,0:T(8,128)S(1)} %get-tuple-element.71), channel_id=1, source_target_pairs={{2,0},{6,1},{0,2},{4,3},{3,4},{7,5},{1,6},{5,7},{10,8},{14,9},{8,1... | collective-permute-start | bytes 1572872 | tf_op jit(solution)/shard_map/ppermute | solution.py:576
  199.7 13.0 %collective-permute-start.21 = (f32[2,2,4,64,128]{4,3,2,1,0:T(8,128)S(1)}, f32[2,2,4,64,128]{4,3,2,1,0:T(8,128)}, u32[]{:S(2)}, u32[]{:S(2)}) collective-permute-start(f32[2,2,4,64,128]{4,3,2,1,0:T(8,128)S(1)} %get-tuple-element.72), channel_id=1, source_target_pairs={{0,0},{4,1},{2,2},{6,3},{1,4},{5,5},{3,6},{7,7},{8,8},{12,9},{10,1... | collective-permute-start | bytes 1572872 | tf_op jit(solution)/shard_map/ppermute | solution.py:576
  201.2 23.4 %collective-permute-start.19 = (f32[2,2,4,64,128]{4,3,2,1,0:T(8,128)S(1)}, f32[2,2,4,64,128]{4,3,2,1,0:T(8,128)}, u32[]{:S(2)}, u32[]{:S(2)}) collective-permute-start(f32[2,2,4,64,128]{4,3,2,1,0:T(8,128)S(1)} %get-tuple-element.70), channel_id=1, source_target_pairs={{6,0},{2,1},{4,2},{0,3},{7,4},{3,5},{5,6},{1,7},{14,8},{10,9},{12,... | collective-permute-start | bytes 1572872 | tf_op jit(solution)/shard_map/ppermute | solution.py:576
  203.9 23.1 %collective-permute-start.18 = (f32[2,2,4,64,128]{4,3,2,1,0:T(8,128)S(1)}, f32[2,2,4,64,128]{4,3,2,1,0:T(8,128)S(1)}, u32[]{:S(2)}, u32[]{:S(2)}) collective-permute-start(f32[2,2,4,64,128]{4,3,2,1,0:T(8,128)S(1)} %get-tuple-element.69), channel_id=1, source_target_pairs={{4,0},{0,1},{6,2},{2,3},{5,4},{1,5},{7,6},{3,7},{12,8},{8,9},{14,1... | collective-permute-start | bytes 1572872 | tf_op jit(solution)/shard_map/ppermute | solution.py:576
  (16 other events, 123.5 us)

commit v8 on v6

--- a/solution.py
+++ b/solution.py
@@ -559,11 +559,12 @@
         [pltpu.VMEM((3 * half, *padded), F32)] * 2,
     )
     part_total = exchange_sum(part_total, axis, count, [4])
-    strip = rows // 2
+    cut = max(CHUNK, rows * 3 // 8 // CHUNK * CHUNK)
+    strips = ((0, cut), (cut, rows - cut))
     back = []
-    for n in range(2):
+    for n, (off, strip) in enumerate(strips):
         outs = call(
-            partial(backward_wedge, n * strip),
+            partial(backward_wedge, off),
             f"backward_wedge_{n}",
             [shape(2, planes, blocks, strip, LANES)] * 4,
             [me],
@@ -586,8 +587,9 @@
     scale = jnp.stack([time_step * inverse, inverse]).reshape(1, 2)
     held = []
     for n in range(0, 8, 2):
+        off, strip = strips[n // 4]
         held = pl.pallas_call(
-            partial(home_kernel, n // 4 * strip, ROUNDS[n % 4 : n % 4 + 2]),
+            partial(home_kernel, off, ROUNDS[n % 4 : n % 4 + 2]),
             out_shape=[jax.ShapeDtypeStruct((planes, height, width), F32)] * 2,
             in_specs=[SM, SM, ANY, ANY] + [ANY] * len(held),
             out_specs=[ANY] * 2,

time: 232 us -> 240 us (1.034)
  waiting for transfers between devices: 104 us -> 115 us
    ppermute x8, waiting for transfers between devices: 14.3 us -> 27.8 us  [on_device(): lax.ppermute(m, axis, [(j, i) for i, j in send_pairs(count, *r)])]
    ppermute x5, waiting for transfers between devices: 13.9 us -> 11 us  [exchange_sum(): lax.ppermute(value, axis, [(i, i ^ step) for i in range(count)])]
    ppermute x5, starting transfers between devices: 19.1 us -> 16.4 us  [exchange_sum(): lax.ppermute(value, axis, [(i, i ^ step) for i in range(count)])]
  transfers between devices with their start and end apart: 26 -> 26, of which waited for: 13 -> 11; matrix products, arithmetic and copies ran while one was open for 0% -> 0% of each run, Pallas kernels for 17% -> 17%
where the time goes in v8:
time: 240 us; the launch traced here: 239 us
  waiting for transfers between devices  115 us (48%)
  starting transfers between devices  59.8 us (25%)
  Pallas kernels  54.2 us (23%)
  between operations  6.04 us (3%)
  local copies, waits for them, and re-layouts  4.35 us (2%)
    ppermute x8, waiting for transfers between devices, regroup(): got.append(lax.ppermute(m, axis, send_pairs(count, *r)))  74.6 us
    pallas_call x10, Pallas kernels, call(): pl.pallas_call(kernel, out_shape=outs, in_specs=[SM] * len(scalars) + [AN...  43.7 us
    ppermute x8, waiting for transfers between devices, on_device(): lax.ppermute(m, axis, [(j, i) for i, j in send_pairs(count, *r)])  27.8 us
    ppermute x8, starting transfers between devices, regroup(): got.append(lax.ppermute(m, axis, send_pairs(count, *r)))  20.7 us
    ppermute x5, starting transfers between devices, exchange_sum(): lax.ppermute(value, axis, [(i, i ^ step) for i in range(count)])  16.4 us
    ppermute x8, starting transfers between devices, on_device(): lax.ppermute(m, axis, [(j, i) for i, j in send_pairs(count, *r)])  15.4 us
    ppermute x5, waiting for transfers between devices, exchange_sum(): lax.ppermute(value, axis, [(i, i ^ step) for i in range(count)])  11 us
    pallas_call x4, Pallas kernels, on_device(): pl.pallas_call(partial(home_kernel, off, ROUNDS[n % 4:n % 4 + 2]), out_sh...  10.5 us
  transfers between devices with their start and end apart: 26, of which 11 were waited for; matrix products, arithmetic and copies ran while one was open for 0% of the time, Pallas kernels for 17%

profile of v8, /device:TPU:0, one launch (start us, length us, event | category | flops | bytes accessed | tf_op | source)
XLA Modules:
  0.0 239.4 jit_solution(7430203691396519009)
XLA Ops:
  3.2 3.0 %collective-permute-start.4 = (f32[2,2,4,144,128]{4,3,2,1,0:T(8,128)S(1)}, f32[2,2,4,144,128]{4,3,2,1,0:T(8,128)S(1)}, u32[]{:S(2)}, u32[]{:S(2)}) collective-permute-start(f32[2,2,4,144,128]{4,3,2,1,0:T(8,128)S(1)} %get-tuple-element.47), channel_id=1, source_target_pairs={{0,2},{1,6},{2,0},{3,4},{4,3},{5,7},{6,1},{7,5},{8,10},{9,14},{10,... | collective-permute-start | bytes 3538952 | tf_op jit(solution)/shard_map/ppermute | solution.py:499
  7.0 3.9 %collective-permute-start.7 = (f32[2,2,4,144,128]{4,3,2,1,0:T(8,128)S(1)}, f32[2,2,4,144,128]{4,3,2,1,0:T(8,128)S(1)}, u32[]{:S(2)}, u32[]{:S(2)}) collective-permute-start(f32[2,2,4,144,128]{4,3,2,1,0:T(8,128)S(1)} %get-tuple-element.49), channel_id=1, source_target_pairs={{0,6},{1,2},{2,4},{3,0},{4,7},{5,3},{6,5},{7,1},{8,14},{9,10},{10,... | collective-permute-start | bytes 3538952 | tf_op jit(solution)/shard_map/ppermute | solution.py:499
  10.9 21.3 %collective-permute-done.4.m0 = f32[2,2,4,144,128]{4,3,2,1,0:T(8,128)S(1)} collective-permute-done((f32[2,2,4,144,128]{4,3,2,1,0:T(8,128)S(1)}, f32[2,2,4,144,128]{4,3,2,1,0:T(8,128)S(1)}, u32[]{:S(2)}, u32[]{:S(2)}) %collective-permute-start.4) | collective-permute-done | bytes 1179680 | tf_op jit(solution)/shard_map/ppermute | solution.py:499
  32.2 26.2 %collective-permute-done.7.m2 = f32[2,2,4,144,128]{4,3,2,1,0:T(8,128)S(1)} collective-permute-done((f32[2,2,4,144,128]{4,3,2,1,0:T(8,128)S(1)}, f32[2,2,4,144,128]{4,3,2,1,0:T(8,128)S(1)}, u32[]{:S(2)}, u32[]{:S(2)}) %collective-permute-start.7) | collective-permute-done | bytes 1179680 | tf_op jit(solution)/shard_map/ppermute | solution.py:499
  60.5 2.7 %shard_map.70 = (f32[2,2,4,144,128]{4,3,2,1,0:T(8,128)S(1)}, f32[2,4,4,144,128]{4,3,2,1,0:T(8,128)S(1)}, f32[2,4,4,144,128]{4,3,2,1,0:T(8,128)S(1)}) custom-call(s32[1]{0:T(128)} %bitcast.me_ref, f32[2,2,4,144,128]{4,3,2,1,0:T(8,128)} %copy-done, f32[2,2,4,144,128]{4,3,2,1,0:T(8,128)} %copy-done.1, f32[2,2,4,144,128]{4,3,2,1,0:T(8,128)} %copy-done.7, ...), custom_call_target="tpu_custom_call" | custom-call | tf_op jit(solution)/shard_map/pallas_call | solution.py:29
  63.2 2.8 %collective-permute-start.10 = (f32[2,4,4,144,128]{4,3,2,1,0:T(8,128)S(1)}, f32[2,4,4,144,128]{4,3,2,1,0:T(8,128)S(1)}, u32[]{:S(2)}, u32[]{:S(2)}) collective-permute-start(f32[2,4,4,144,128]{4,3,2,1,0:T(8,128)S(1)} %get-tuple-element.53.a_ref), channel_id=1, source_target_pairs={{0,1},{1,0},{2,3},{3,2},{4,5},{5,4},{6,7},{7,6},{8,9},{9,8},{10,11... | collective-permute-start | bytes 7077896 | tf_op jit(solution)/shard_map/ppermute | solution.py:514
  74.4 6.0 %collective-permute-start.2 = (f32[2,2,4,136,128]{4,3,2,1,0:T(8,128)S(1)}, f32[2,2,4,136,128]{4,3,2,1,0:T(8,128)}, u32[]{:S(2)}, u32[]{:S(2)}) collective-permute-start(f32[2,2,4,136,128]{4,3,2,1,0:T(8,128)S(1)} %get-tuple-element.45), channel_id=1, source_target_pairs={{0,6},{1,2},{2,4},{3,0},{4,7},{5,3},{6,5},{7,1},{8,14},{9,10},{10,... | collective-permute-start | bytes 3342344 | tf_op jit(solution)/shard_map/ppermute | solution.py:499
  80.5 4.3 %collective-permute-start.3 = (f32[2,2,4,136,128]{4,3,2,1,0:T(8,128)S(1)}, f32[2,2,4,136,128]{4,3,2,1,0:T(8,128)}, u32[]{:S(2)}, u32[]{:S(2)}) collective-permute-start(f32[2,2,4,136,128]{4,3,2,1,0:T(8,128)S(1)} %get-tuple-element.46), channel_id=1, source_target_pairs={{0,4},{1,0},{2,6},{3,2},{4,5},{5,1},{6,7},{7,3},{8,12},{9,8},{10,1... | collective-permute-start | bytes 3342344 | tf_op jit(solution)/shard_map/ppermute | solution.py:499
  84.7 8.6 %shard_map.71 = (f32[8,4,144,128]{3,2,1,0:T(8,128)S(1)}, f32[12,4,144,128]{3,2,1,0:T(8,128)S(1)}, f32[4,8,4,144,128]{4,3,2,1,0:T(8,128)S(1)}, f32[3,2,4,144,128]{4,3,2,1,0:T(8,128)S(1)}) custom-call(s32[1]{0:T(128)} %bitcast.me_ref, f32[2,4,4,144,128]{4,3,2,1,0:T(8,128)S(1)} %get-tuple-element.53.a_ref, f32[2,4,4,144,128]{4,3,2,1,0:T(8,128)S(1)} %get-tuple-element.52.b_ref, ...), custom_call_target="tpu_custom_call" | custom-call | tf_op jit(solution)/shard_map/pallas_call | solution.py:29
  94.4 5.5 %shard_map.72 = (f32[8,4,144,128]{3,2,1,0:T(8,128)S(1)}, f32[4,8,4,144,128]{4,3,2,1,0:T(8,128)S(1)}, f32[4,4,144,128]{3,2,1,0:T(8,128)S(1)}) custom-call(s32[1]{0:T(128)} %bitcast.me_ref, f32[2,2,4,144,128]{4,3,2,1,0:T(8,128)} %copy-done.5, f32[2,2,4,144,128]{4,3,2,1,0:T(8,128)} %copy-done.4, ...), custom_call_target="tpu_custom_call", output_to_operand_aliasing={{0}: (6, {}), {1}: (7, {})} | custom-call | tf_op jit(solution)/shard_map/pallas_call | solution.py:29
  99.9 23.4 %collective-permute-done.2.f2 = f32[2,2,4,136,128]{4,3,2,1,0:T(8,128)} collective-permute-done((f32[2,2,4,136,128]{4,3,2,1,0:T(8,128)S(1)}, f32[2,2,4,136,128]{4,3,2,1,0:T(8,128)}, u32[]{:S(2)}, u32[]{:S(2)}) %collective-permute-start.2) | collective-permute-done | bytes 1114144 | tf_op jit(solution)/shard_map/ppermute | solution.py:499
  123.3 3.0 %collective-permute-done.3.f3 = f32[2,2,4,136,128]{4,3,2,1,0:T(8,128)} collective-permute-done((f32[2,2,4,136,128]{4,3,2,1,0:T(8,128)S(1)}, f32[2,2,4,136,128]{4,3,2,1,0:T(8,128)}, u32[]{:S(2)}, u32[]{:S(2)}) %collective-permute-start.3) | collective-permute-done | bytes 1114144 | tf_op jit(solution)/shard_map/ppermute | solution.py:499
  126.3 3.0 %shard_map.73 = (f32[4,4,144,128]{3,2,1,0:T(8,128)S(1)}, f32[4,4,144,128]{3,2,1,0:T(8,128)S(1)}, f32[1,1]{1,0:T(1,128)}) custom-call(s32[1]{0:T(128)} %bitcast.me_ref, f32[2,2,4,136,128]{4,3,2,1,0:T(8,128)} %copy-done.9, f32[2,2,4,136,128]{4,3,2,1,0:T(8,128)} %collective-permute-done.1.f1, f32[2,2,4,136,128]{4,3,2,1,0:T(8,128)} %collective-permute-done.2.f2, ...), custom_call_target="tpu_custom_call" | custom-call | tf_op jit(solution)/shard_map/pallas_call | solution.py:29
  135.0 9.2 %shard_map.74 = (f32[12,4,144,128]{3,2,1,0:T(8,128)S(1)}, f32[8,4,128,128]{3,2,1,0:T(8,128)S(1)}, f32[3,2,4,144,128]{4,3,2,1,0:T(8,128)S(1)}) custom-call(s32[1]{0:T(128)} %bitcast.me_ref, f32[4,4,144,128]{3,2,1,0:T(8,128)} %copy-done.6, f32[4,4,144,128]{3,2,1,0:T(8,128)S(1)} %get-tuple-element.63.a_ref, f32[4,4,144,128]{3,2,1,0:T(8,128)S(1)} %get-tuple-element.60.b_ref, ...), custom_call_target="tpu_custom_call" | custom-call | tf_op jit(solution)/shard_map/pallas_call | solution.py:29
  145.2 3.5 %shard_map.76 = (f32[2,2,4,48,128]{4,3,2,1,0:T(8,128)S(1)}, f32[2,2,4,48,128]{4,3,2,1,0:T(8,128)S(1)}, f32[2,2,4,48,128]{4,3,2,1,0:T(8,128)S(1)}, f32[2,2,4,48,128]{4,3,2,1,0:T(8,128)S(1)}) custom-call(s32[1]{0:T(128)} %bitcast.me_ref, f32[4,4,144,128]{3,2,1,0:T(8,128)} %copy-done.2, f32[4,4,144,128]{3,2,1,0:T(8,128)S(1)} %get-tuple-element.60.b_ref, ...), custom_call_target="tpu_custom_call" | custom-call | tf_op jit(solution)/shard_map/pallas_call | solution.py:29
  150.4 7.9 %collective-permute-start.22 = (f32[2,2,4,48,128]{4,3,2,1,0:T(8,128)S(1)}, f32[2,2,4,48,128]{4,3,2,1,0:T(8,128)S(1)}, u32[]{:S(2)}, u32[]{:S(2)}) collective-permute-start(f32[2,2,4,48,128]{4,3,2,1,0:T(8,128)S(1)} %get-tuple-element.71), channel_id=1, source_target_pairs={{6,0},{2,1},{4,2},{0,3},{7,4},{3,5},{5,6},{1,7},{14,8},{10,9},{12,... | collective-permute-start | bytes 1179656 | tf_op jit(solution)/shard_map/ppermute | solution.py:577
  159.4 9.9 %collective-permute-done.11 = f32[1,1]{1,0:T(1,128)} collective-permute-done((f32[1,1]{1,0:T(1,128)}, f32[1,1]{1,0:T(1,128)}, u32[]{:S(2)}, u32[]{:S(2)}) %collective-permute-start.11) | collective-permute-done | bytes 36 | tf_op jit(solution)/shard_map/ppermute | solution.py:471
  170.6 6.2 %collective-permute-start.12 = (f32[1,1]{1,0:T(1,128)}, f32[1,1]{1,0:T(1,128)}, u32[]{:S(2)}, u32[]{:S(2)}) collective-permute-start(f32[1,1]{1,0:T(1,128)} %add.19), channel_id=1, source_target_pairs={{0,4},{1,5},{2,6},{3,7},{4,0},{5,1},{6,2},{7,3},{8,12},{9,13},{10,... | collective-permute-start | bytes 20 | tf_op jit(solution)/shard_map/ppermute | solution.py:471
  179.8 3.8 %collective-permute-start.14 = (f32[1,1]{1,0:T(1,128)}, f32[1,1]{1,0:T(1,128)}, u32[]{:S(2)}, u32[]{:S(2)}) collective-permute-start(f32[1,1]{1,0:T(1,128)} %add.21), channel_id=1, source_target_pairs={{0,8},{1,9},{2,10},{3,11},{4,12},{5,13},{6,14},{7,15},{8,0},{9,1},... | collective-permute-start | bytes 20 | tf_op jit(solution)/shard_map/ppermute | solution.py:471
  184.6 4.4 %collective-permute-start.15 = (f32[1,1]{1,0:T(1,128)}, f32[1,1]{1,0:T(1,128)}, u32[]{:S(2)}, u32[]{:S(2)}) collective-permute-start(f32[1,1]{1,0:T(1,128)} %add.22), channel_id=1, source_target_pairs={{0,16},{1,17},{2,18},{3,19},{4,20},{5,21},{6,22},{7,23},{8,24},{9,... | collective-permute-start | bytes 20 | tf_op jit(solution)/shard_map/ppermute | solution.py:471
  189.0 4.4 %shard_map.75 = (f32[2,2,4,80,128]{4,3,2,1,0:T(8,128)S(1)}, f32[2,2,4,80,128]{4,3,2,1,0:T(8,128)S(1)}, f32[2,2,4,80,128]{4,3,2,1,0:T(8,128)S(1)}, f32[2,2,4,80,128]{4,3,2,1,0:T(8,128)S(1)}) custom-call(s32[1]{0:T(128)} %bitcast.me_ref, f32[4,4,144,128]{3,2,1,0:T(8,128)} %copy-done.2, f32[4,4,144,128]{3,2,1,0:T(8,128)S(1)} %get-tuple-element.60.b_ref, ...), custom_call_target="tpu_custom_call" | custom-call | tf_op jit(solution)/shard_map/pallas_call | solution.py:29
  202.5 27.8 %collective-permute-done.23.refs_1_ = f32[2,2,4,48,128]{4,3,2,1,0:T(8,128)} collective-permute-done((f32[2,2,4,48,128]{4,3,2,1,0:T(8,128)S(1)}, f32[2,2,4,48,128]{4,3,2,1,0:T(8,128)}, u32[]{:S(2)}, u32[]{:S(2)}) %collective-permute-start.23) | collective-permute-done | bytes 393248 | tf_op jit(solution)/shard_map/ppermute | solution.py:577
  232.7 2.8 %shard_map.79 = (f32[2,512,512]{2,1,0:T(8,128)}, f32[2,512,512]{2,1,0:T(8,128)}) custom-call(s32[1]{0:T(128)} %bitcast.me_ref, f32[1,2]{1,0:T(1,128)S(1)} %maximum_bitcast_fusion.scale_ref, f32[2,2,4,80,128]{4,3,2,1,0:T(8,128)} %collective-permute-done.20.refs_0_, ...), custom_call_target="tpu_custom_call", output_to_operand_aliasing={{0}: (4, {}), {1}: (5, {})} | custom-call | tf_op jit(solution)/shard_map/pallas_call | solution.py:591
  235.5 2.8 %shard_map.80 = (f32[2,512,512]{2,1,0:T(8,128)}, f32[2,512,512]{2,1,0:T(8,128)}) custom-call(s32[1]{0:T(128)} %bitcast.me_ref, f32[1,2]{1,0:T(1,128)S(1)} %maximum_bitcast_fusion.scale_ref, f32[2,2,4,80,128]{4,3,2,1,0:T(8,128)} %collective-permute-done.18.refs_0_, ...), custom_call_target="tpu_custom_call", output_to_operand_aliasing={{0}: (4, {}), {1}: (5, {})} | custom-call | tf_op jit(solution)/shard_map/pallas_call | solution.py:591
  (69 shorter events, 37.1 us)
Async XLA Ops:
  3.2 29.0 %collective-permute-start.4 = (f32[2,2,4,144,128]{4,3,2,1,0:T(8,128)S(1)}, f32[2,2,4,144,128]{4,3,2,1,0:T(8,128)S(1)}, u32[]{:S(2)}, u32[]{:S(2)}) collective-permute-start(f32[2,2,4,144,128]{4,3,2,1,0:T(8,128)S(1)} %get-tuple-element.47), channel_id=1, source_target_pairs={{0,2},{1,6},{2,0},{3,4},{4,3},{5,7},{6,1},{7,5},{8,10},{9,14},{10,... | collective-permute-start | bytes 3538952 | tf_op jit(solution)/shard_map/ppermute | solution.py:499
  6.2 26.0 %collective-permute-start.5 = (f32[2,2,4,144,128]{4,3,2,1,0:T(8,128)S(1)}, f32[2,2,4,144,128]{4,3,2,1,0:T(8,128)S(1)}, u32[]{:S(2)}, u32[]{:S(2)}) collective-permute-start(f32[2,2,4,144,128]{4,3,2,1,0:T(8,128)S(1)} %get-tuple-element.48), channel_id=1, source_target_pairs={{0,0},{1,4},{2,2},{3,6},{4,1},{5,5},{6,3},{7,7},{8,8},{9,12},{10,1... | collective-permute-start | bytes 3538952 | tf_op jit(solution)/shard_map/ppermute | solution.py:499
  7.0 51.4 %collective-permute-start.7 = (f32[2,2,4,144,128]{4,3,2,1,0:T(8,128)S(1)}, f32[2,2,4,144,128]{4,3,2,1,0:T(8,128)S(1)}, u32[]{:S(2)}, u32[]{:S(2)}) collective-permute-start(f32[2,2,4,144,128]{4,3,2,1,0:T(8,128)S(1)} %get-tuple-element.49), channel_id=1, source_target_pairs={{0,6},{1,2},{2,4},{3,0},{4,7},{5,3},{6,5},{7,1},{8,14},{9,10},{10,... | collective-permute-start | bytes 3538952 | tf_op jit(solution)/shard_map/ppermute | solution.py:499
  10.9 48.3 %collective-permute-start.8 = (f32[2,2,4,144,128]{4,3,2,1,0:T(8,128)S(1)}, f32[2,2,4,144,128]{4,3,2,1,0:T(8,128)S(1)}, u32[]{:S(2)}, u32[]{:S(2)}) collective-permute-start(f32[2,2,4,144,128]{4,3,2,1,0:T(8,128)S(1)} %get-tuple-element.50), channel_id=1, source_target_pairs={{0,4},{1,0},{2,6},{3,2},{4,5},{5,1},{6,7},{7,3},{8,12},{9,8},{10,1... | collective-permute-start | bytes 3538952 | tf_op jit(solution)/shard_map/ppermute | solution.py:499
  63.2 17.2 %collective-permute-start.10 = (f32[2,4,4,144,128]{4,3,2,1,0:T(8,128)S(1)}, f32[2,4,4,144,128]{4,3,2,1,0:T(8,128)S(1)}, u32[]{:S(2)}, u32[]{:S(2)}) collective-permute-start(f32[2,4,4,144,128]{4,3,2,1,0:T(8,128)S(1)} %get-tuple-element.53.a_ref), channel_id=1, source_target_pairs={{0,1},{1,0},{2,3},{3,2},{4,5},{5,4},{6,7},{7,6},{8,9},{9,8},{10,11... | collective-permute-start | bytes 7077896 | tf_op jit(solution)/shard_map/ppermute | solution.py:514
  66.0 8.4 %collective-permute-start.9 = (f32[2,2,4,144,128]{4,3,2,1,0:T(8,128)S(1)}, f32[2,2,4,144,128]{4,3,2,1,0:T(8,128)S(1)}, u32[]{:S(2)}, u32[]{:S(2)}) collective-permute-start(f32[2,2,4,144,128]{4,3,2,1,0:T(8,128)S(1)} %get-tuple-element.51), channel_id=1, source_target_pairs={{1,8},{8,1},{3,10},{10,3},{5,12},{12,5},{7,14},{14,7},{9,16},{16,9... | collective-permute-start | bytes 3538952 | tf_op jit(solution)/shard_map/ppermute | solution.py:513
  68.4 24.9 %collective-permute-start.6 = (f32[2,2,4,144,128]{4,3,2,1,0:T(8,128)S(1)}, f32[2,2,4,144,128]{4,3,2,1,0:T(8,128)S(1)}, u32[]{:S(2)}, u32[]{:S(2)}) collective-permute-start(f32[2,2,4,144,128]{4,3,2,1,0:T(8,128)S(1)} %shard_map.69), channel_id=1, source_target_pairs={{1,8},{8,1},{3,10},{10,3},{5,12},{12,5},{7,14},{14,7},{9,16},{16,9... | collective-permute-start | bytes 3538952 | tf_op jit(solution)/shard_map/ppermute | solution.py:511
  71.7 28.1 %collective-permute-start = (f32[2,2,4,136,128]{4,3,2,1,0:T(8,128)S(1)}, f32[2,2,4,136,128]{4,3,2,1,0:T(8,128)S(1)}, u32[]{:S(2)}, u32[]{:S(2)}) collective-permute-start(f32[2,2,4,136,128]{4,3,2,1,0:T(8,128)S(1)} %get-tuple-element.43), channel_id=1, source_target_pairs={{0,2},{1,6},{2,0},{3,4},{4,3},{5,7},{6,1},{7,5},{8,10},{9,14},{10,... | collective-permute-start | bytes 3342344 | tf_op jit(solution)/shard_map/ppermute | solution.py:499
  72.8 27.1 %collective-permute-start.1 = (f32[2,2,4,136,128]{4,3,2,1,0:T(8,128)S(1)}, f32[2,2,4,136,128]{4,3,2,1,0:T(8,128)}, u32[]{:S(2)}, u32[]{:S(2)}) collective-permute-start(f32[2,2,4,136,128]{4,3,2,1,0:T(8,128)S(1)} %get-tuple-element.44), channel_id=1, source_target_pairs={{0,0},{1,4},{2,2},{3,6},{4,1},{5,5},{6,3},{7,7},{8,8},{9,12},{10,1... | collective-permute-start | bytes 3342344 | tf_op jit(solution)/shard_map/ppermute | solution.py:499
  74.4 48.8 %collective-permute-start.2 = (f32[2,2,4,136,128]{4,3,2,1,0:T(8,128)S(1)}, f32[2,2,4,136,128]{4,3,2,1,0:T(8,128)}, u32[]{:S(2)}, u32[]{:S(2)}) collective-permute-start(f32[2,2,4,136,128]{4,3,2,1,0:T(8,128)S(1)} %get-tuple-element.45), channel_id=1, source_target_pairs={{0,6},{1,2},{2,4},{3,0},{4,7},{5,3},{6,5},{7,1},{8,14},{9,10},{10,... | collective-permute-start | bytes 3342344 | tf_op jit(solution)/shard_map/ppermute | solution.py:499
  80.5 45.8 %collective-permute-start.3 = (f32[2,2,4,136,128]{4,3,2,1,0:T(8,128)S(1)}, f32[2,2,4,136,128]{4,3,2,1,0:T(8,128)}, u32[]{:S(2)}, u32[]{:S(2)}) collective-permute-start(f32[2,2,4,136,128]{4,3,2,1,0:T(8,128)S(1)} %get-tuple-element.46), channel_id=1, source_target_pairs={{0,4},{1,0},{2,6},{3,2},{4,5},{5,1},{6,7},{7,3},{8,12},{9,8},{10,1... | collective-permute-start | bytes 3342344 | tf_op jit(solution)/shard_map/ppermute | solution.py:499
  129.3 4.6 %collective-permute-start.17 = (f32[4,4,144,128]{3,2,1,0:T(8,128)S(1)}, f32[4,4,144,128]{3,2,1,0:T(8,128)S(1)}, u32[]{:S(2)}, u32[]{:S(2)}) collective-permute-start(f32[4,4,144,128]{3,2,1,0:T(8,128)S(1)} %get-tuple-element.63.a_ref), channel_id=1, source_target_pairs={{0,1},{1,0},{2,3},{3,2},{4,5},{5,4},{6,7},{7,6},{8,9},{9,8},{10,11... | collective-permute-start | bytes 3538952 | tf_op jit(solution)/shard_map/ppermute | solution.py:549
  131.5 12.7 %collective-permute-start.16 = (f32[4,4,144,128]{3,2,1,0:T(8,128)S(1)}, f32[4,4,144,128]{3,2,1,0:T(8,128)S(1)}, u32[]{:S(2)}, u32[]{:S(2)}) collective-permute-start(f32[4,4,144,128]{3,2,1,0:T(8,128)S(1)} %get-tuple-element.60.b_ref), channel_id=1, source_target_pairs={{1,8},{8,1},{3,10},{10,3},{5,12},{12,5},{7,14},{14,7},{9,16},{16,9... | collective-permute-start | bytes 3538952 | tf_op jit(solution)/shard_map/ppermute | solution.py:548
  148.7 47.2 %collective-permute-start.24 = (f32[2,2,4,48,128]{4,3,2,1,0:T(8,128)S(1)}, f32[2,2,4,48,128]{4,3,2,1,0:T(8,128)S(1)}, u32[]{:S(2)}, u32[]{:S(2)}) collective-permute-start(f32[2,2,4,48,128]{4,3,2,1,0:T(8,128)S(1)} %get-tuple-element.73), channel_id=1, source_target_pairs={{2,0},{6,1},{0,2},{4,3},{3,4},{7,5},{1,6},{5,7},{10,8},{14,9},{8,1... | collective-permute-start | bytes 1179656 | tf_op jit(solution)/shard_map/ppermute | solution.py:577
  149.8 47.5 %collective-permute-start.25 = (f32[2,2,4,48,128]{4,3,2,1,0:T(8,128)S(1)}, f32[2,2,4,48,128]{4,3,2,1,0:T(8,128)S(1)}, u32[]{:S(2)}, u32[]{:S(2)}) collective-permute-start(f32[2,2,4,48,128]{4,3,2,1,0:T(8,128)S(1)} %get-tuple-element.74), channel_id=1, source_target_pairs={{0,0},{4,1},{2,2},{6,3},{1,4},{5,5},{3,6},{7,7},{8,8},{12,9},{10,1... | collective-permute-start | bytes 1179656 | tf_op jit(solution)/shard_map/ppermute | solution.py:577
  150.4 46.8 %collective-permute-start.22 = (f32[2,2,4,48,128]{4,3,2,1,0:T(8,128)S(1)}, f32[2,2,4,48,128]{4,3,2,1,0:T(8,128)S(1)}, u32[]{:S(2)}, u32[]{:S(2)}) collective-permute-start(f32[2,2,4,48,128]{4,3,2,1,0:T(8,128)S(1)} %get-tuple-element.71), channel_id=1, source_target_pairs={{6,0},{2,1},{4,2},{0,3},{7,4},{3,5},{5,6},{1,7},{14,8},{10,9},{12,... | collective-permute-start | bytes 1179656 | tf_op jit(solution)/shard_map/ppermute | solution.py:577
  158.4 11.0 %collective-permute-start.11 = (f32[1,1]{1,0:T(1,128)}, f32[1,1]{1,0:T(1,128)}, u32[]{:S(2)}, u32[]{:S(2)}) collective-permute-start(f32[1,1]{1,0:T(1,128)} %get-tuple-element.59), channel_id=1, source_target_pairs={{0,2},{1,3},{2,0},{3,1},{4,6},{5,7},{6,4},{7,5},{8,10},{9,11},{10,... | collective-permute-start | bytes 20 | tf_op jit(solution)/shard_map/ppermute | solution.py:471
  170.6 6.5 %collective-permute-start.12 = (f32[1,1]{1,0:T(1,128)}, f32[1,1]{1,0:T(1,128)}, u32[]{:S(2)}, u32[]{:S(2)}) collective-permute-start(f32[1,1]{1,0:T(1,128)} %add.19), channel_id=1, source_target_pairs={{0,4},{1,5},{2,6},{3,7},{4,0},{5,1},{6,2},{7,3},{8,12},{9,13},{10,... | collective-permute-start | bytes 20 | tf_op jit(solution)/shard_map/ppermute | solution.py:471
  184.6 9.8 %collective-permute-start.15 = (f32[1,1]{1,0:T(1,128)}, f32[1,1]{1,0:T(1,128)}, u32[]{:S(2)}, u32[]{:S(2)}) collective-permute-start(f32[1,1]{1,0:T(1,128)} %add.22), channel_id=1, source_target_pairs={{0,16},{1,17},{2,18},{3,19},{4,20},{5,21},{6,22},{7,23},{8,24},{9,... | collective-permute-start | bytes 20 | tf_op jit(solution)/shard_map/ppermute | solution.py:471
  193.3 39.4 %collective-permute-start.20 = (f32[2,2,4,80,128]{4,3,2,1,0:T(8,128)S(1)}, f32[2,2,4,80,128]{4,3,2,1,0:T(8,128)}, u32[]{:S(2)}, u32[]{:S(2)}) collective-permute-start(f32[2,2,4,80,128]{4,3,2,1,0:T(8,128)S(1)} %get-tuple-element.69), channel_id=1, source_target_pairs={{2,0},{6,1},{0,2},{4,3},{3,4},{7,5},{1,6},{5,7},{10,8},{14,9},{8,1... | collective-permute-start | bytes 1966088 | tf_op jit(solution)/shard_map/ppermute | solution.py:577
  194.4 38.3 %collective-permute-start.21 = (f32[2,2,4,80,128]{4,3,2,1,0:T(8,128)S(1)}, f32[2,2,4,80,128]{4,3,2,1,0:T(8,128)}, u32[]{:S(2)}, u32[]{:S(2)}) collective-permute-start(f32[2,2,4,80,128]{4,3,2,1,0:T(8,128)S(1)} %get-tuple-element.70), channel_id=1, source_target_pairs={{0,0},{4,1},{2,2},{6,3},{1,4},{5,5},{3,6},{7,7},{8,8},{12,9},{10,1... | collective-permute-start | bytes 1966088 | tf_op jit(solution)/shard_map/ppermute | solution.py:577
  195.9 39.6 %collective-permute-start.18 = (f32[2,2,4,80,128]{4,3,2,1,0:T(8,128)S(1)}, f32[2,2,4,80,128]{4,3,2,1,0:T(8,128)}, u32[]{:S(2)}, u32[]{:S(2)}) collective-permute-start(f32[2,2,4,80,128]{4,3,2,1,0:T(8,128)S(1)} %get-tuple-element.67), channel_id=1, source_target_pairs={{6,0},{2,1},{4,2},{0,3},{7,4},{3,5},{5,6},{1,7},{14,8},{10,9},{12,... | collective-permute-start | bytes 1966088 | tf_op jit(solution)/shard_map/ppermute | solution.py:577
  197.3 38.3 %collective-permute-start.19 = (f32[2,2,4,80,128]{4,3,2,1,0:T(8,128)S(1)}, f32[2,2,4,80,128]{4,3,2,1,0:T(8,128)}, u32[]{:S(2)}, u32[]{:S(2)}) collective-permute-start(f32[2,2,4,80,128]{4,3,2,1,0:T(8,128)S(1)} %get-tuple-element.68), channel_id=1, source_target_pairs={{4,0},{0,1},{6,2},{2,3},{5,4},{1,5},{7,6},{3,7},{12,8},{8,9},{14,1... | collective-permute-start | bytes 1966088 | tf_op jit(solution)/shard_map/ppermute | solution.py:577
  197.3 33.0 %collective-permute-start.23 = (f32[2,2,4,48,128]{4,3,2,1,0:T(8,128)S(1)}, f32[2,2,4,48,128]{4,3,2,1,0:T(8,128)}, u32[]{:S(2)}, u32[]{:S(2)}) collective-permute-start(f32[2,2,4,48,128]{4,3,2,1,0:T(8,128)S(1)} %get-tuple-element.72), channel_id=1, source_target_pairs={{4,0},{0,1},{6,2},{2,3},{5,4},{1,5},{7,6},{3,7},{12,8},{8,9},{14,1... | collective-permute-start | bytes 1179656 | tf_op jit(solution)/shard_map/ppermute | solution.py:577
  (15 other events, 122.7 us)
